TPU v7x, 32 devices: a whole 2x2x4 slice. The times are simulated.
32 devices in a mesh: pb: 4 (over y, x), wa: 8 (over z, core).
Axes of the slice: x: 2, y: 2, z: 4, core: 2. Of those that a mesh axis runs over, the one named last changes fastest.
Arguments:
- quartets: int32 [1024, 4, 128], P(('pb', 'wa')), may hold values from -1 to 49151, as said below
- counts: int32 [32], P(('pb', 'wa')), may hold values from 1 to 32, as said below
- eig: bfloat16 [24, 49152], P(None, 'pb'), may hold values from -1.1953125 to 1.1953125
- freq: bfloat16 [49152], P('pb'), may hold values from 0.5 to 2
- phi: bfloat16 [144, 1152], replicated, may hold values from -0.5390625 to 0.5390625
- cells: int32 [8, 9], replicated, may hold values from -2 to 2
Outputs:
- rates: float32 [49152], P(('pb', 'wa'))
Inputs may be any that keep to these rules, and one draw needn't show every extreme that they name: quartets[b, 0, n] is a mode of one of the 1024 q-points of the owner group of slot b (from 0 to 12287); the other three entries are all -1 or all modes of the mesh, and then their q-points and that of the first add up as q1 + q2 = q3 + q4 on the mesh. The used slots of a device are its first counts slots; some device has exactly 32.
All inputs are finite; a program needn't handle non-finite values.
Results may differ from a plain program's by a relative error of at most 0.0023.
Values may be sent and summed in bfloat16 or wider, within the bound.
No kernel may reach another device: no remote copies, remote signals or barrier semaphores. Data moves between devices by JAX's collectives and lax.ppermute only.
A program may use at most 64 MiB of HBM per device.

v0:
```python
import functools
import math

import jax
import jax.numpy as jnp
from jax import lax
from jax.experimental import pallas as pl
from jax.experimental.pallas import tpu as pltpu
from jax.sharding import PartitionSpec as P


QMESH = 16
LANES = 128
SUB = 8
GROUPS = 4
SLOT = LANES // GROUPS
PARTS = 4

smearing = 0.5


def occupation(value):
    return 1.0 / (jnp.exp(value) - 1.0)


def row_iota(rows):
    return lax.broadcasted_iota(jnp.int32, (rows, LANES), 0)


def window(kept):
    return -(-(kept + LANES - math.gcd(kept, LANES)) // LANES)


def prepare(branches, local, kept, offset, *refs):
    pool, (rows_out, meta_out, flags_out) = refs[:-3], refs[-3:]
    mine = lax.axis_index("pb")
    side = lax.rem(lax.axis_index("wa"), 2)
    start = lax.axis_index("wa") * kept
    lead = lax.rem(start, LANES)
    shards = lax.axis_size("pb")
    modes = jnp.concatenate([r[...].astype(jnp.int32) for r in pool], axis=0) + offset
    count = modes.shape[0]
    heading = (row_iota(count) & (PARTS - 1)) == 0
    safe = jnp.maximum(modes, 0)
    middle = safe.astype(jnp.float32) + 0.5
    owner = (middle * (1.0 / local)).astype(jnp.int32)
    point = (middle * (1.0 / branches)).astype(jnp.int32)
    near = owner ^ mine
    slot = near
    if shards == GROUPS:
        slot = jnp.where(near == 1, 1 + side, jnp.where(near == 2, 2 - side, near))
    inner = safe - owner * local
    depth = local // GROUPS
    group = ((inner.astype(jnp.float32) + 0.5) * (1.0 / depth)).astype(jnp.int32)
    rows_out[...] = (slot - group) * depth + inner
    following = pltpu.roll(modes, count - 1, 0)
    first = modes - start
    valid = heading & (following >= 0) & (first >= 0) & (first < kept)
    meta_out[...] = jnp.where(
        heading, jnp.where(valid, first + lead, -1), point + group * 65536
    )
    flags_out[...] = lax.dot_general(
        jnp.ones((SUB, LANES), jnp.bfloat16),
        jnp.where(valid, 1.0, 0.0).astype(jnp.bfloat16),
        (((1,), (1,)), ((), ())),
        preferred_element_type=jnp.float32,
    )


def fill_table(vectors, lines, table, base):
    comps, local = vectors.shape
    depth = local // GROUPS
    for t in range(depth // LANES):
        stack = []
        for g in range(GROUPS):
            at = g * depth + t * LANES
            stack.append(vectors[:, at : at + LANES].astype(jnp.float32))
            line = lines[at // LANES : at // LANES + 1, :].astype(jnp.float32)
            stack.append(jnp.broadcast_to(line, (SLOT - comps, LANES)))
        row = base + t * LANES
        table[row : row + LANES, :] = jnp.concatenate(stack, axis=0).T


def early(kept, heads, near, *refs):
    vectors, lines = refs[:near], refs[near : 2 * near]
    table, own = refs[2 * near :]
    comps, local = vectors[0].shape
    for at in range(near):
        fill_table(vectors[at], lines[at], table, at * (local // GROUPS))
    start = lax.axis_index("wa") * kept // LANES
    own_lines = lines[0][...].astype(jnp.float32)
    line_rows = row_iota(own_lines.shape[0])
    parts = []
    for h in range(heads):
        at = pl.multiple_of((start + h) * LANES, LANES)
        parts.append(vectors[0][:, pl.ds(at, LANES)].astype(jnp.float32))
    for h in range(heads):
        parts.append(
            jnp.sum(jnp.where(line_rows == start + h, own_lines, 0.0), axis=0, keepdims=True)
        )
    filler = own.shape[0] - heads * comps - heads
    parts.append(jnp.zeros((filler, LANES), jnp.float32))
    own[...] = jnp.concatenate(parts, axis=0).astype(jnp.bfloat16)


def held_rows(e, branches):
    out = []
    for v in range(branches * branches // SUB):
        low, high = v * SUB // branches, (v * SUB + SUB - 1) // branches
        if low == high:
            out.append(jnp.broadcast_to(e[low : low + 1], (SUB, LANES)))
        else:
            cut = high * branches - v * SUB
            out.append(jnp.where(row_iota(SUB) < cut, e[low : low + 1], e[high : high + 1]))
    return out


def cycled_rows(e, branches):
    period = math.lcm(SUB, branches)
    twice = jnp.concatenate([e[:branches]] * (period // branches), axis=0)
    return [twice[v * SUB : (v + 1) * SUB] for v in range(period // SUB)]


def kernel(
    branches,
    base,
    order,
    total,
    rows_any,
    meta,
    table_in,
    own,
    phi_hbm,
    cells,
    vectors,
    lines,
    out,
    table,
    near_a,
    near_b,
    spots_a,
    spots_b,
    phi,
    wide,
    acc,
    sems,
):
    comps = 2 * branches
    pairs = branches * branches
    clusters = SUB
    heads = out.shape[0]
    log = QMESH.bit_length() - 1
    count = total[0]
    last = rows_any.shape[0] - 1

    def block_at(i):
        return order[jnp.minimum(i, last)]

    def load(i, spots, which):
        return pltpu.make_async_copy(rows_any.at[block_at(i)], spots, sems.at[which])

    fetch_phi = pltpu.make_async_copy(phi_hbm, phi, sems.at[2])
    fetch_phi.start()
    load(0, spots_a, 0).start()
    load(1, spots_b, 1).start()
    fill_table(vectors, lines, table, base)
    acc[...] = jnp.zeros_like(acc)

    def gather(spots, near):
        for which in range(3):
            for n in range(LANES):
                at = which * LANES + n
                near[at : at + 1, :] = table[pl.ds(spots[which + 1, n], 1), :]

    def contract(info, near):
        others = []
        points = []
        for which in range(3):
            word = info[which + 1 : which + 2, :]
            group = lax.shift_right_logical(word, 16)
            points.append(word & 0xFFFF)
            flat = near[which * LANES : (which + 1) * LANES, :].T
            pick = flat[:SLOT]
            for g in range(1, GROUPS):
                pick = jnp.where(group == g, flat[g * SLOT : (g + 1) * SLOT], pick)
            others.append(pick)
        second, third, fourth = others
        local = info[0:1, :]
        head = lax.shift_right_arithmetic(local, 7)
        hot = jnp.where(row_iota(LANES) == (local & (LANES - 1)), 1.0, 0.0).astype(jnp.bfloat16)
        spread = jnp.dot(own[...], hot, preferred_element_type=jnp.float32)
        first = jnp.zeros((comps, LANES), jnp.float32)
        for h in range(heads):
            first = jnp.where(head == h, spread[h * comps : (h + 1) * comps], first)
        tail = spread[heads * comps :]
        first_freq = jnp.sum(
            jnp.where(row_iota(tail.shape[0]) == head, tail, 0.0), axis=0, keepdims=True
        )
        shift = jnp.zeros((clusters, LANES), jnp.int32)
        for which in range(3):
            p = points[which]
            coords = (
                lax.shift_right_logical(p, 2 * log),
                lax.shift_right_logical(p, log) & (QMESH - 1),
                p & (QMESH - 1),
            )
            for axis in range(3):
                shift = shift + cells[3 * which + axis] * coords[axis]
        angle = (shift & (QMESH - 1)).astype(jnp.float32) * (2.0 * math.pi / QMESH)
        cosine, sine = jnp.cos(angle), jnp.sin(angle)
        third_re, third_im = held_rows(third, branches), held_rows(third[branches:], branches)
        fourth_re, fourth_im = cycled_rows(fourth, branches), cycled_rows(fourth[branches:], branches)
        period = len(fourth_re)
        far = []
        for v in range(pairs // SUB):
            are, aim, bre, bim = third_re[v], third_im[v], fourth_re[v % period], fourth_im[v % period]
            far.append((are * bre - aim * bim, -(are * bim + aim * bre)))
        for k in range(clusters):
            cos_k, sin_k = cosine[k : k + 1], sine[k : k + 1]
            for v in range(0, pairs // SUB, 2):
                both = [(cos_k * re - sin_k * im, cos_k * im + sin_k * re) for re, im in far[v : v + 2]]
                at = k * pairs + v * SUB
                for part in range(2):
                    wide[at : at + 2 * SUB, part * LANES : (part + 1) * LANES] = jnp.concatenate(
                        [both[0][part], both[1][part]], axis=0
                    ).astype(jnp.bfloat16)
        weighted = jnp.dot(phi[...], wide[...], preferred_element_type=jnp.float32)
        first_re, first_im = held_rows(first, branches), held_rows(first[branches:], branches)
        second_re, second_im = cycled_rows(second, branches), cycled_rows(second[branches:], branches)
        sum_re = jnp.zeros((SUB, LANES), jnp.float32)
        sum_im = sum_re
        for v in range(pairs // SUB):
            are, aim, bre, bim = first_re[v], first_im[v], second_re[v % period], second_im[v % period]
            near_re, near_im = are * bre - aim * bim, are * bim + aim * bre
            wre = weighted[v * SUB : (v + 1) * SUB, :LANES]
            wim = weighted[v * SUB : (v + 1) * SUB, LANES:]
            sum_re = sum_re + (near_re * wre - near_im * wim)
            sum_im = sum_im + (near_re * wim + near_im * wre)
        value_re = jnp.sum(sum_re, axis=0, keepdims=True)
        value_im = jnp.sum(sum_im, axis=0, keepdims=True)
        f2, f3, f4 = (e[comps : comps + 1] for e in others)
        mismatch = first_freq + f2 - f3 - f4
        delta = jnp.exp(-((mismatch / smearing) ** 2)) / (smearing * math.sqrt(math.pi))
        weight = (
            (1.0 + occupation(f2)) * occupation(f3) * occupation(f4) / occupation(first_freq)
        )
        product = first_freq * f2 * f3 * f4
        term = (value_re * value_re + value_im * value_im) * delta * weight / product
        term = jnp.where(local >= 0, term, 0.0)
        size = acc.shape[0]
        placed = jnp.where(row_iota(size) == head, term, 0.0)
        parts = []
        for _ in range(3):
            part = placed.astype(jnp.bfloat16)
            parts.append(part)
            placed = placed - part.astype(jnp.float32)
        sums = lax.dot_general(
            jnp.concatenate(parts, axis=0),
            hot,
            (((1,), (1,)), ((), ())),
            preferred_element_type=jnp.float32,
        )
        acc[...] += sums[:size] + sums[size : 2 * size] + sums[2 * size :]

    load(0, spots_a, 0).wait()
    gather(spots_a, near_a)
    fetch_phi.wait()
    side_a, side_b = (near_a, spots_a, 0), (near_b, spots_b, 1)

    def half_step(i, here, there):
        load(i + 2, *here[1:]).start()
        load(i + 1, *there[1:]).wait()
        gather(there[1], there[0])
        contract(meta[block_at(i)], here[0])

    def two_blocks(j, carry):
        half_step(2 * j, side_a, side_b)

        @pl.when(2 * j + 1 < count)
        def _():
            half_step(2 * j + 1, side_b, side_a)

        return carry

    lax.fori_loop(0, lax.div(count + 1, 2), two_blocks, 0)
    even = lax.rem(count, 2) == 0

    @pl.when(even)
    def _():
        load(0, *side_b[1:]).wait()

    @pl.when(jnp.logical_not(even))
    def _():
        load(0, *side_a[1:]).wait()

    out[...] = acc[:heads, :]


def body(quartets, counts, eig, freq, phi, cells):
    comps, local = eig.shape
    branches = comps // 2
    shards = lax.axis_size("pb")
    workers = lax.axis_size("wa")
    held, parts, block = quartets.shape
    kept = local // workers
    heads = window(kept)
    clusters = cells.shape[0]
    offset = local * shards // 2
    both = ("pb", "wa")
    lines = freq.reshape(local // LANES, LANES)

    def swap(x):
        return lax.ppermute(x, "wa", [(i, i ^ 1) for i in range(workers)])

    def across(x, even, odd):
        pairs = []
        for p in range(shards):
            for w in range(workers):
                pairs.append((p * workers + w, (p ^ (odd if w % 2 else even)) * workers + w))
        return lax.ppermute(x, both, pairs)

    if shards == GROUPS:
        vectors, rows_of = [eig], [lines]
        for owned, kind in ((eig, vectors), (lines, rows_of)):
            one = across(owned, 1, 2)
            far = across(one, 2, 1)
            kind += [one, swap(one), far]
    else:
        vectors, rows_of = [eig], [lines]
        for k in range(1, shards):
            vectors.append(across(eig, k, k))
            rows_of.append(across(lines, k, k))

    slots = jnp.arange(held, dtype=jnp.int32)[:, None, None]
    coded = (jnp.where(slots < counts[0], quartets, -1) - offset).astype(jnp.int16)
    coded = coded.reshape(held * parts, block)
    line_up = [coded]
    for k in range(2, workers, 2):
        line_up.append(lax.ppermute(coded, "wa", [(i, i ^ k) for i in range(workers)]))
    column = jnp.concatenate(line_up, axis=0)
    other_column = swap(column)
    vmem = pl.BlockSpec(memory_space=pltpu.VMEM)
    smem = pl.BlockSpec(memory_space=pltpu.SMEM)
    hbm = pl.BlockSpec(memory_space=pl.ANY)
    far_space = pl.BlockSpec(memory_space=pltpu.HBM)
    total_rows = workers * held * parts
    rows, meta, flags = pl.pallas_call(
        functools.partial(prepare, branches, local, kept, offset),
        out_shape=[
            jax.ShapeDtypeStruct((total_rows, LANES), jnp.int32),
            jax.ShapeDtypeStruct((total_rows, LANES), jnp.int32),
            jax.ShapeDtypeStruct((SUB, total_rows), jnp.float32),
        ],
        in_specs=[vmem, vmem],
        compiler_params=pltpu.CompilerParams(vmem_limit_bytes=16 * 1024 * 1024),
    )(column, other_column)
    blocks = total_rows // parts
    index = jnp.arange(blocks, dtype=jnp.int32)
    owned = flags[0].reshape(blocks, parts)[:, 0] > 0.5
    place = jnp.cumsum(owned.astype(jnp.int32)) - 1
    order = jnp.sum(
        jnp.where((place[None, :] == index[:, None]) & owned[None, :], index[None, :], 0), axis=1
    )
    total = jnp.sum(owned.astype(jnp.int32)).reshape(1)
    signed = jnp.concatenate([cells[:, :3], -cells[:, 3:]], axis=1)
    spread_cells = jnp.broadcast_to(signed.T[:, :, None], (9, clusters, LANES))

    padded = -(-heads // 16) * 16
    own_rows = -(-heads * (comps + 1) // 16) * 16
    depth = local // GROUPS
    near = shards - 1
    table, own = pl.pallas_call(
        functools.partial(early, kept, heads, near),
        out_shape=[
            jax.ShapeDtypeStruct((shards * depth, LANES), jnp.float32),
            jax.ShapeDtypeStruct((own_rows, LANES), jnp.bfloat16),
        ],
        in_specs=[vmem] * (2 * near),
        out_specs=[vmem, vmem],
        compiler_params=pltpu.CompilerParams(vmem_limit_bytes=16 * 1024 * 1024),
    )(*vectors[:near], *rows_of[:near])
    rates, _ = pl.pallas_call(
        functools.partial(kernel, branches, near * depth),
        out_shape=[
            jax.ShapeDtypeStruct((heads, LANES), jnp.float32),
            jax.ShapeDtypeStruct(table.shape, table.dtype),
        ],
        in_specs=[smem, smem, hbm, vmem, vmem, vmem, far_space] + [vmem] * 3,
        out_specs=[vmem, vmem],
        input_output_aliases={4: 1},
        scratch_shapes=[
            pltpu.VMEM((3 * LANES, LANES), jnp.float32),
            pltpu.VMEM((3 * LANES, LANES), jnp.float32),
            pltpu.SMEM((parts, LANES), jnp.int32),
            pltpu.SMEM((parts, LANES), jnp.int32),
            pltpu.VMEM(phi.shape, phi.dtype),
            pltpu.VMEM((phi.shape[1], 2 * LANES), jnp.bfloat16),
            pltpu.VMEM((padded, LANES), jnp.float32),
            pltpu.SemaphoreType.DMA((3,)),
        ],
        compiler_params=pltpu.CompilerParams(vmem_limit_bytes=16 * 1024 * 1024),
    )(
        order,
        total,
        rows.reshape(blocks, parts, LANES),
        meta.reshape(blocks, parts, LANES),
        table,
        own,
        phi,
        spread_cells,
        vectors[near],
        rows_of[near],
    )
    rates = rates.reshape(heads * LANES)
    if heads * LANES == kept:
        return rates
    return lax.dynamic_slice_in_dim(rates, lax.axis_index("wa") * kept % LANES, kept, 0)


def solution(mesh):
    placed = (P(("pb", "wa"), None, None), P(("pb", "wa")), P(None, "pb"), P("pb"), P(), P())
    return jax.shard_map(
        body, mesh=mesh, in_specs=placed, out_specs=P(("pb", "wa")), check_vma=False
    )
```

profile of v0, /device:TPU:18, one launch (start us, length us, event | category | flops | bytes accessed | tf_op | source)
XLA Modules:
  0.0 49.5 jit_solution(10989432726278498763)
XLA Ops:
  0.7 0.9 %add_convert_fusion = s16[32,4,128]{2,1,0:T(4,128)(2,1)S(1)} fusion(s32[32,4,128]{2,1,0:T(4,128)} %param.6, pred[32]{0:T(512)(128)(4,1)S(1)} %iota_compare_fusion.1), kind=kLoop, calls=%fused_computation.6 | loop fusion | flops 49152 | bytes 98336 | tf_op jit(solution)/shard_map/convert_element_type | solution.py:335
  1.6 0.5 %collective-permute-start.2 = (s16[128,128]{1,0:T(8,128)(2,1)S(1)}, s16[128,128]{1,0:T(8,128)(2,1)S(1)}, u32[]{:S(2)}, u32[]{:S(2)}) collective-permute-start(s16[128,128]{1,0:T(8,128)(2,1)S(1)} %bitcast.18), channel_id=1, source_target_pairs={{0,6},{1,7},{2,4},{3,5},{4,2},{5,3},{6,0},{7,1},{8,14},{9,15},{10,... | collective-permute-start | bytes 98312 | tf_op jit(solution)/shard_map/ppermute | solution.py:339
  2.1 3.5 %collective-permute-start.1 = (s16[128,128]{1,0:T(8,128)(2,1)S(1)}, s16[128,128]{1,0:T(8,128)(2,1)S(1)}, u32[]{:S(2)}, u32[]{:S(2)}) collective-permute-start(s16[128,128]{1,0:T(8,128)(2,1)S(1)} %bitcast.19), channel_id=1, source_target_pairs={{0,4},{1,5},{2,6},{3,7},{4,0},{5,1},{6,2},{7,3},{8,12},{9,13},{10,... | collective-permute-start | bytes 98312 | tf_op jit(solution)/shard_map/ppermute | solution.py:339
  5.6 0.0 collective-permute-start
  5.6 0.5 %collective-permute-start.6 = (bf16[96,128]{1,0:T(8,128)(2,1)}, bf16[96,128]{1,0:T(8,128)(2,1)S(1)}, u32[]{:S(2)}, u32[]{:S(2)}) collective-permute-start(bf16[96,128]{1,0:T(8,128)(2,1)} %bitcast.16), channel_id=1, source_target_pairs={{0,8},{1,17},{2,10},{3,19},{4,12},{5,21},{6,14},{7,23},{8,0},{9,25... | collective-permute-start | bytes 73736 | tf_op jit(solution)/shard_map/ppermute | solution.py:320
  6.2 1.5 %collective-permute-start.4 = (bf16[24,12288]{1,0:T(8,128)(2,1)}, bf16[24,12288]{1,0:T(8,128)(2,1)S(1)}, u32[]{:S(2)}, u32[]{:S(2)}) collective-permute-start(bf16[24,12288]{1,0:T(8,128)(2,1)} %refs_0_.1), channel_id=1, source_target_pairs={{0,8},{1,17},{2,10},{3,19},{4,12},{5,21},{6,14},{7,23},{8,0},{9,25... | collective-permute-start | bytes 1769480 | tf_op jit(solution)/shard_map/ppermute | solution.py:320
  7.6 0.0 collective-permute-done.2
  7.7 0.2 collective-permute-done.1
  7.9 1.7 %collective-permute-done = s16[128,128]{1,0:T(8,128)(2,1)S(1)} collective-permute-done((s16[128,128]{1,0:T(8,128)(2,1)S(1)}, s16[128,128]{1,0:T(8,128)(2,1)S(1)}, u32[]{:S(2)}, u32[]{:S(2)}) %collective-permute-start) | collective-permute-done | bytes 32800 | tf_op jit(solution)/shard_map/ppermute | solution.py:339
  9.5 0.1 collective-permute-start.3
  9.6 0.8 %slice_negate_fusion = s32[8,6]{1,0:T(8,128)S(1)} fusion(s32[8,9]{1,0:T(8,128)} %param.11), kind=kLoop, calls=%fused_computation.8 | loop fusion | flops 48 | bytes 384 | tf_op jit(solution)/shard_map/neg | solution.py:365
  10.4 0.8 %add_bitcast_fusion = s32[9,8]{0,1:T(8,128)S(1)} fusion(s32[8,6]{1,0:T(8,128)S(1)} %slice_negate_fusion, s32[8,3]{1,0:T(8,128)} %bitcast.22), kind=kLoop, calls=%fused_computation.7 | loop fusion | flops 72 | bytes 576 | tf_op jit(solution)/shard_map/transpose | solution.py:366
  11.1 0.1 copy.10
  11.2 0.0 collective-permute-done.6.refs_4_
  11.2 1.5 %collective-permute-start.9 = (bf16[96,128]{1,0:T(8,128)(2,1)S(1)}, bf16[96,128]{1,0:T(8,128)(2,1)S(1)}, u32[]{:S(2)}, u32[]{:S(2)}) collective-permute-start(bf16[96,128]{1,0:T(8,128)(2,1)S(1)} %collective-permute-done.6.refs_4_), channel_id=1, source_target_pairs={{0,16},{1,9},{2,18},{3,11},{4,20},{5,13},{6,22},{7,15},{8,24},{9,1... | collective-permute-start | bytes 73736 | tf_op jit(solution)/shard_map/ppermute | solution.py:320
  12.8 0.0 collective-permute-start.7
  12.8 0.0 collective-permute-done.3.refs_1_
  12.8 1.3 %shard_map.64 = (s32[1024,128]{1,0:T(8,128)S(1)}, s32[1024,128]{1,0:T(8,128)S(1)}, f32[8,1024]{1,0:T(8,128)S(1)}) custom-call(s16[512,128]{1,0:T(8,128)(2,1)S(1)} %pad_add_fusion.refs_0_, s16[512,128]{1,0:T(8,128)(2,1)S(1)} %collective-permute-done.3.refs_1_), custom_call_target="tpu_custom_call" | custom-call | tf_op jit(solution)/shard_map/pallas_call | solution.py:347
  14.1 0.1 reshape_squeeze.3
  14.2 0.1 fusion.1
  14.3 2.2 %collective-permute-done.4.refs_1_ = bf16[24,12288]{1,0:T(8,128)(2,1)S(1)} collective-permute-done((bf16[24,12288]{1,0:T(8,128)(2,1)}, bf16[24,12288]{1,0:T(8,128)(2,1)S(1)}, u32[]{:S(2)}, u32[]{:S(2)}) %collective-permute-start.4) | collective-permute-done | bytes 589856 | tf_op jit(solution)/shard_map/ppermute | solution.py:320
  16.5 1.5 %collective-permute-start.8 = (bf16[24,12288]{1,0:T(8,128)(2,1)S(1)}, bf16[24,12288]{1,0:T(8,128)(2,1)S(1)}, u32[]{:S(2)}, u32[]{:S(2)}) collective-permute-start(bf16[24,12288]{1,0:T(8,128)(2,1)S(1)} %collective-permute-done.4.refs_1_), channel_id=1, source_target_pairs={{0,16},{1,9},{2,18},{3,11},{4,20},{5,13},{6,22},{7,15},{8,24},{9,1... | collective-permute-start | bytes 1769480 | tf_op jit(solution)/shard_map/ppermute | solution.py:320
  18.0 0.0 collective-permute-start.5
  18.0 0.1 convert_reduce_fusion
  18.1 0.3 reduce-window.9
  18.5 0.1 slice.21
  18.6 0.1 slice_reduce_fusion.1
  18.7 0.1 add_bitcast_fusion.1
  18.8 0.1 select_reduce_fusion.order
  18.9 0.7 %convert_reduce_fusion.1 = s32[]{:T(128)} fusion(pred[256]{0:T(512)(128)(4,1)S(1)} %get-tuple-element.17), kind=kLoop, calls=%fused_computation.10 | loop fusion | flops 511 | bytes 260 | tf_op jit(solution)/shard_map/reduce_sum | solution.py:364
  19.6 0.0 collective-permute-done.7.refs_5_
  19.6 0.4 collective-permute-done.5.refs_2_
  20.0 0.0 copy-start
  20.0 1.1 %copy-done = bf16[24,12288]{1,0:T(8,128)(2,1)S(1)} copy-done((bf16[24,12288]{1,0:T(8,128)(2,1)S(1)}, bf16[24,12288]{1,0:T(8,128)(2,1)}, u32[]{:S(2)}) %copy-start) | copy-done | bytes 589848
  21.1 0.0 copy-start.2
  21.1 0.7 %copy-done.2 = bf16[12288]{0:T(1024)(128)(2,1)S(1)} copy-done((bf16[12288]{0:T(1024)(128)(2,1)S(1)}, bf16[12288]{0:T(1024)(128)(2,1)}, u32[]{:S(2)}) %copy-start.2) | copy-done | bytes 24600
  21.8 1.3 %shard_map.65 = (f32[12288,128]{1,0:T(8,128)S(1)}, bf16[304,128]{1,0:T(8,128)(2,1)S(1)}) custom-call(bf16[24,12288]{1,0:T(8,128)(2,1)S(1)} %copy-done, bf16[24,12288]{1,0:T(8,128)(2,1)S(1)} %collective-permute-done.4.refs_1_, bf16[24,12288]{1,0:T(8,128)(2,1)S(1)} %collective-permute-done.5.refs_2_, bf16[96,128]{1,0:T(8,128)(2,1)S(1)} %bitcast.17, ...), custom_call_target="tpu_custom_call" | custom-call | tf_op jit(solution)/shard_map/pallas_call | solution.py:372
  23.1 0.0 collective-permute-done.9.lines
  23.1 3.3 %collective-permute-done.8.vectors = bf16[24,12288]{1,0:T(8,128)(2,1)S(1)} collective-permute-done((bf16[24,12288]{1,0:T(8,128)(2,1)S(1)}, bf16[24,12288]{1,0:T(8,128)(2,1)S(1)}, u32[]{:S(2)}, u32[]{:S(2)}) %collective-permute-start.8) | collective-permute-done | bytes 589856 | tf_op jit(solution)/shard_map/ppermute | solution.py:320
  26.4 0.1 broadcast_in_dim.39.cells
  26.5 0.0 copy-start.1
  26.5 1.0 %copy-done.1 = bf16[144,1152]{1,0:T(8,128)(2,1)S(1)} copy-done((bf16[144,1152]{1,0:T(8,128)(2,1)S(1)}, bf16[144,1152]{1,0:T(8,128)(2,1)}, u32[]{:S(2)}) %copy-start.1) | copy-done | bytes 331800
  27.5 22.1 %shard_map.66 = (f32[12,128]{1,0:T(8,128)}, f32[12288,128]{1,0:T(8,128)S(1)}) custom-call(s32[256]{0:T(256)S(1)} %select_reduce_fusion.order, s32[1]{0:T(128)} %bitcast.3.total, s32[256,4,128]{2,1,0:T(4,128)S(1)} %bitcast.14, s32[256,4,128]{2,1,0:T(4,128)S(1)} %bitcast.15, ...), custom_call_target="tpu_custom_call", output_to_operand_aliasing={{1}: (4, {})} | custom-call | tf_op jit(solution)/shard_map/pallas_call | solution.py:382
  (4 shorter events, 0.1 us)
Async XLA Ops:
  1.6 6.0 %collective-permute-start.2 = (s16[128,128]{1,0:T(8,128)(2,1)S(1)}, s16[128,128]{1,0:T(8,128)(2,1)S(1)}, u32[]{:S(2)}, u32[]{:S(2)}) collective-permute-start(s16[128,128]{1,0:T(8,128)(2,1)S(1)} %bitcast.18), channel_id=1, source_target_pairs={{0,6},{1,7},{2,4},{3,5},{4,2},{5,3},{6,0},{7,1},{8,14},{9,15},{10,... | collective-permute-start | bytes 98312 | tf_op jit(solution)/shard_map/ppermute | solution.py:339
  2.1 5.7 %collective-permute-start.1 = (s16[128,128]{1,0:T(8,128)(2,1)S(1)}, s16[128,128]{1,0:T(8,128)(2,1)S(1)}, u32[]{:S(2)}, u32[]{:S(2)}) collective-permute-start(s16[128,128]{1,0:T(8,128)(2,1)S(1)} %bitcast.19), channel_id=1, source_target_pairs={{0,4},{1,5},{2,6},{3,7},{4,0},{5,1},{6,2},{7,3},{8,12},{9,13},{10,... | collective-permute-start | bytes 98312 | tf_op jit(solution)/shard_map/ppermute | solution.py:339
  5.6 3.9 %collective-permute-start = (s16[128,128]{1,0:T(8,128)(2,1)S(1)}, s16[128,128]{1,0:T(8,128)(2,1)S(1)}, u32[]{:S(2)}, u32[]{:S(2)}) collective-permute-start(s16[128,128]{1,0:T(8,128)(2,1)S(1)} %bitcast.20), channel_id=1, source_target_pairs={{0,2},{1,3},{2,0},{3,1},{4,6},{5,7},{6,4},{7,5},{8,10},{9,11},{10,... | collective-permute-start | bytes 98312 | tf_op jit(solution)/shard_map/ppermute | solution.py:339
  5.6 5.6 %collective-permute-start.6 = (bf16[96,128]{1,0:T(8,128)(2,1)}, bf16[96,128]{1,0:T(8,128)(2,1)S(1)}, u32[]{:S(2)}, u32[]{:S(2)}) collective-permute-start(bf16[96,128]{1,0:T(8,128)(2,1)} %bitcast.16), channel_id=1, source_target_pairs={{0,8},{1,17},{2,10},{3,19},{4,12},{5,21},{6,14},{7,23},{8,0},{9,25... | collective-permute-start | bytes 73736 | tf_op jit(solution)/shard_map/ppermute | solution.py:320
  6.2 10.4 %collective-permute-start.4 = (bf16[24,12288]{1,0:T(8,128)(2,1)}, bf16[24,12288]{1,0:T(8,128)(2,1)S(1)}, u32[]{:S(2)}, u32[]{:S(2)}) collective-permute-start(bf16[24,12288]{1,0:T(8,128)(2,1)} %refs_0_.1), channel_id=1, source_target_pairs={{0,8},{1,17},{2,10},{3,19},{4,12},{5,21},{6,14},{7,23},{8,0},{9,25... | collective-permute-start | bytes 1769480 | tf_op jit(solution)/shard_map/ppermute | solution.py:320
  9.5 3.2 %collective-permute-start.3 = (s16[512,128]{1,0:T(8,128)(2,1)S(1)}, s16[512,128]{1,0:T(8,128)(2,1)S(1)}, u32[]{:S(2)}, u32[]{:S(2)}) collective-permute-start(s16[512,128]{1,0:T(8,128)(2,1)S(1)} %pad_add_fusion.refs_0_), channel_id=1, source_target_pairs={{0,1},{1,0},{2,3},{3,2},{4,5},{5,4},{6,7},{7,6},{8,9},{9,8},{10,11... | collective-permute-start | bytes 393224 | tf_op jit(solution)/shard_map/ppermute | solution.py:313
  11.2 11.9 %collective-permute-start.9 = (bf16[96,128]{1,0:T(8,128)(2,1)S(1)}, bf16[96,128]{1,0:T(8,128)(2,1)S(1)}, u32[]{:S(2)}, u32[]{:S(2)}) collective-permute-start(bf16[96,128]{1,0:T(8,128)(2,1)S(1)} %collective-permute-done.6.refs_4_), channel_id=1, source_target_pairs={{0,16},{1,9},{2,18},{3,11},{4,20},{5,13},{6,22},{7,15},{8,24},{9,1... | collective-permute-start | bytes 73736 | tf_op jit(solution)/shard_map/ppermute | solution.py:320
  12.8 6.9 %collective-permute-start.7 = (bf16[96,128]{1,0:T(8,128)(2,1)S(1)}, bf16[96,128]{1,0:T(8,128)(2,1)S(1)}, u32[]{:S(2)}, u32[]{:S(2)}) collective-permute-start(bf16[96,128]{1,0:T(8,128)(2,1)S(1)} %collective-permute-done.6.refs_4_), channel_id=1, source_target_pairs={{0,1},{1,0},{2,3},{3,2},{4,5},{5,4},{6,7},{7,6},{8,9},{9,8},{10,11... | collective-permute-start | bytes 73736 | tf_op jit(solution)/shard_map/ppermute | solution.py:313
  16.5 9.9 %collective-permute-start.8 = (bf16[24,12288]{1,0:T(8,128)(2,1)S(1)}, bf16[24,12288]{1,0:T(8,128)(2,1)S(1)}, u32[]{:S(2)}, u32[]{:S(2)}) collective-permute-start(bf16[24,12288]{1,0:T(8,128)(2,1)S(1)} %collective-permute-done.4.refs_1_), channel_id=1, source_target_pairs={{0,16},{1,9},{2,18},{3,11},{4,20},{5,13},{6,22},{7,15},{8,24},{9,1... | collective-permute-start | bytes 1769480 | tf_op jit(solution)/shard_map/ppermute | solution.py:320
  18.0 2.0 %collective-permute-start.5 = (bf16[24,12288]{1,0:T(8,128)(2,1)S(1)}, bf16[24,12288]{1,0:T(8,128)(2,1)S(1)}, u32[]{:S(2)}, u32[]{:S(2)}) collective-permute-start(bf16[24,12288]{1,0:T(8,128)(2,1)S(1)} %collective-permute-done.4.refs_1_), channel_id=1, source_target_pairs={{0,1},{1,0},{2,3},{3,2},{4,5},{5,4},{6,7},{7,6},{8,9},{9,8},{10,11... | collective-permute-start | bytes 1769480 | tf_op jit(solution)/shard_map/ppermute | solution.py:313
  20.0 1.1 %copy-start = (bf16[24,12288]{1,0:T(8,128)(2,1)S(1)}, bf16[24,12288]{1,0:T(8,128)(2,1)}, u32[]{:S(2)}) copy-start(bf16[24,12288]{1,0:T(8,128)(2,1)} %refs_0_.1) | copy-start | bytes 1769476
  21.1 0.7 %copy-start.2 = (bf16[12288]{0:T(1024)(128)(2,1)S(1)}, bf16[12288]{0:T(1024)(128)(2,1)}, u32[]{:S(2)}) copy-start(bf16[12288]{0:T(1024)(128)(2,1)} %param.9) | copy-start | bytes 73732
  26.5 1.0 %copy-start.1 = (bf16[144,1152]{1,0:T(8,128)(2,1)S(1)}, bf16[144,1152]{1,0:T(8,128)(2,1)}, u32[]{:S(2)}) copy-start(bf16[144,1152]{1,0:T(8,128)(2,1)} %phi_hbm.1) | copy-start | bytes 995332
where the time goes:
time: 49.9 us; the launch traced here: 49.5 us
  Pallas kernels  24.6 us (49%)
  starting transfers between devices  9.15 us (18%)
  waiting for transfers between devices  7.76 us (16%)
  other arithmetic  3.98 us (8%)
  local copies, waits for them, and re-layouts  3.29 us (7%)
  between operations  0.73 us (1%)
    pallas_call x1, Pallas kernels, body(): pl.pallas_call(functools.partial(kernel, branches, near * depth), out_sha...  22.1 us
    ppermute x4, waiting for transfers between devices, across(): return lax.ppermute(x, both, pairs)  5.46 us
    ppermute x4, starting transfers between devices, across(): return lax.ppermute(x, both, pairs)  5.07 us
    ppermute x3, starting transfers between devices, body(): lax.ppermute(coded, 'wa', [(i, i ^ k) for i in range(workers)])  4.01 us
    unnamed x6, local copies, waits for them, and re-layouts  2.78 us
    ppermute x3, waiting for transfers between devices, body(): lax.ppermute(coded, 'wa', [(i, i ^ k) for i in range(workers)])  1.88 us
    pallas_call x1, Pallas kernels, body(): pl.pallas_call(functools.partial(prepare, branches, local, kept, offset),...  1.28 us
    pallas_call x1, Pallas kernels, body(): pl.pallas_call(functools.partial(early, kept, heads, near), out_shape=[ja...  1.28 us
  transfers between devices with their start and end apart: 10, of which 5 were waited for; matrix products, arithmetic and copies ran while one was open for 7% of the time, Pallas kernels for 5%

commit v1 on v0

--- a/solution.py
+++ b/solution.py
@@ -15,6 +15,8 @@
 GROUPS = 4
 SLOT = LANES // GROUPS
 PARTS = 4
+AHEAD = 2
+DEPTH = 256
 
 smearing = 0.5
 
@@ -83,7 +85,8 @@
 
 def early(kept, heads, near, *refs):
     vectors, lines = refs[:near], refs[near : 2 * near]
-    table, own = refs[2 * near :]
+    phi_in, table, own, phi = refs[2 * near :]
+    phi[...] = phi_in[...]
     comps, local = vectors[0].shape
     for at in range(near):
         fill_table(vectors[at], lines[at], table, at * (local // GROUPS))
@@ -130,75 +133,67 @@
     meta,
     table_in,
     own,
-    phi_hbm,
+    phi,
     cells,
     vectors,
     lines,
     out,
     table,
-    near_a,
-    near_b,
-    spots_a,
-    spots_b,
-    phi,
-    wide,
+    gathered_a,
+    gathered_b,
+    pair_a,
+    pair_b,
+    single_a,
+    single_b,
+    wide_a,
+    wide_b,
+    product_a,
+    product_b,
+    placed,
+    place,
     acc,
+    spots,
     sems,
 ):
     comps = 2 * branches
     pairs = branches * branches
+    groups = pairs // SUB
     clusters = SUB
     heads = out.shape[0]
     log = QMESH.bit_length() - 1
     count = total[0]
     last = rows_any.shape[0] - 1
+    gathered, pair, single = (gathered_a, gathered_b), (pair_a, pair_b), (single_a, single_b)
+    wide, product = (wide_a, wide_b), (product_a, product_b)
 
     def block_at(i):
-        return order[jnp.minimum(i, last)]
-
-    def load(i, spots, which):
-        return pltpu.make_async_copy(rows_any.at[block_at(i)], spots, sems.at[which])
-
-    fetch_phi = pltpu.make_async_copy(phi_hbm, phi, sems.at[2])
-    fetch_phi.start()
-    load(0, spots_a, 0).start()
-    load(1, spots_b, 1).start()
-    fill_table(vectors, lines, table, base)
-    acc[...] = jnp.zeros_like(acc)
-
-    def gather(spots, near):
+        return order[jnp.clip(i, 0, last)]
+
+    def load(i, p):
+        return pltpu.make_async_copy(rows_any.at[block_at(i)], spots.at[p], sems.at[p])
+
+    def gather(p):
+        into = gathered[p]
         for which in range(3):
             for n in range(LANES):
                 at = which * LANES + n
-                near[at : at + 1, :] = table[pl.ds(spots[which + 1, n], 1), :]
-
-    def contract(info, near):
-        others = []
-        points = []
-        for which in range(3):
-            word = info[which + 1 : which + 2, :]
-            group = lax.shift_right_logical(word, 16)
-            points.append(word & 0xFFFF)
-            flat = near[which * LANES : (which + 1) * LANES, :].T
-            pick = flat[:SLOT]
-            for g in range(1, GROUPS):
-                pick = jnp.where(group == g, flat[g * SLOT : (g + 1) * SLOT], pick)
-            others.append(pick)
-        second, third, fourth = others
-        local = info[0:1, :]
+                into[at : at + 1, :] = table[pl.ds(spots[p, which + 1, n], 1), :]
+                yield
+
+    def one_hot(local):
+        inside = local & (LANES - 1)
+        return jnp.where(row_iota(LANES) == inside, 1.0, 0.0).astype(jnp.bfloat16)
+
+    def choose(i, rows, pair_out, single_out):
+        info = meta[block_at(i)]
+        local = jnp.where(i < count, info[0:1, :], -1)
         head = lax.shift_right_arithmetic(local, 7)
-        hot = jnp.where(row_iota(LANES) == (local & (LANES - 1)), 1.0, 0.0).astype(jnp.bfloat16)
-        spread = jnp.dot(own[...], hot, preferred_element_type=jnp.float32)
-        first = jnp.zeros((comps, LANES), jnp.float32)
-        for h in range(heads):
-            first = jnp.where(head == h, spread[h * comps : (h + 1) * comps], first)
-        tail = spread[heads * comps :]
-        first_freq = jnp.sum(
-            jnp.where(row_iota(tail.shape[0]) == head, tail, 0.0), axis=0, keepdims=True
-        )
+        spread = jnp.dot(own[...], one_hot(local), preferred_element_type=jnp.float32)
+        flats = [rows[w * LANES : (w + 1) * LANES, :].T for w in range(3)]
+        yield
         shift = jnp.zeros((clusters, LANES), jnp.int32)
         for which in range(3):
-            p = points[which]
+            p = info[which + 1 : which + 2, :] & 0xFFFF
             coords = (
                 lax.shift_right_logical(p, 2 * log),
                 lax.shift_right_logical(p, log) & (QMESH - 1),
@@ -206,94 +201,239 @@
             )
             for axis in range(3):
                 shift = shift + cells[3 * which + axis] * coords[axis]
+            yield
         angle = (shift & (QMESH - 1)).astype(jnp.float32) * (2.0 * math.pi / QMESH)
-        cosine, sine = jnp.cos(angle), jnp.sin(angle)
+        single_out[0:SUB, :] = jnp.cos(angle)
+        yield
+        single_out[SUB : 2 * SUB, :] = jnp.sin(angle)
+        yield
+        others = []
+        for which in range(3):
+            group = lax.shift_right_logical(info[which + 1 : which + 2, :], 16)
+            masks = [group == g for g in range(1, GROUPS)]
+            pick = []
+            for r in range(0, SLOT, SUB):
+                value = flats[which][r : r + SUB]
+                for g in range(1, GROUPS):
+                    at = g * SLOT + r
+                    value = jnp.where(masks[g - 1], flats[which][at : at + SUB], value)
+                pick.append(value)
+                yield
+            others.append(jnp.concatenate(pick, axis=0))
+        second, third, fourth = others
         third_re, third_im = held_rows(third, branches), held_rows(third[branches:], branches)
         fourth_re, fourth_im = cycled_rows(fourth, branches), cycled_rows(fourth[branches:], branches)
         period = len(fourth_re)
-        far = []
-        for v in range(pairs // SUB):
+        for v in range(groups):
             are, aim, bre, bim = third_re[v], third_im[v], fourth_re[v % period], fourth_im[v % period]
-            far.append((are * bre - aim * bim, -(are * bim + aim * bre)))
+            pair_out[v * SUB : (v + 1) * SUB, :] = are * bre - aim * bim
+            at = pairs + v * SUB
+            pair_out[at : at + SUB, :] = -(are * bim + aim * bre)
+            yield
+        at = 2 * SUB
+        single_out[at : at + SLOT, :] = second
+        first = jnp.zeros((comps, LANES), jnp.float32)
+        for h in range(heads):
+            first = jnp.where(head == h, spread[h * comps : (h + 1) * comps], first)
+            yield
+        tail = spread[heads * comps :]
+        first_freq = jnp.sum(
+            jnp.where(row_iota(tail.shape[0]) == head, tail, 0.0), axis=0, keepdims=True
+        )
+        at += SLOT
+        single_out[at : at + comps, :] = first
+        at += comps
+        wanted = [first_freq] + [e[comps : comps + 1] for e in others]
+        wanted.append(local.astype(jnp.float32))
+        for n, line in enumerate(wanted):
+            single_out[at + n : at + n + 1, :] = line
+        yield
+
+    def join(single_in, product_out):
+        at = 2 * SUB
+        second = single_in[at : at + comps, :]
+        at += SLOT
+        first = single_in[at : at + comps, :]
+        at += comps
+        f1, f2, f3, f4, local = (single_in[at + n : at + n + 1, :] for n in range(5))
+        yield
+        mismatch = f1 + f2 - f3 - f4
+        delta = jnp.exp(-((mismatch / smearing) ** 2)) / (smearing * math.sqrt(math.pi))
+        yield
+        weight = (1.0 + occupation(f2)) * occupation(f3) * occupation(f4) / occupation(f1)
+        yield
+        at = 2 * pairs
+        product_out[at : at + 1, :] = delta * weight / (f1 * f2 * f3 * f4)
+        product_out[at + 1 : at + 2, :] = local
+        yield
+        first_re, first_im = held_rows(first, branches), held_rows(first[branches:], branches)
+        second_re, second_im = cycled_rows(second, branches), cycled_rows(second[branches:], branches)
+        period = len(second_re)
+        for v in range(groups):
+            are, aim, bre, bim = first_re[v], first_im[v], second_re[v % period], second_im[v % period]
+            product_out[v * SUB : (v + 1) * SUB, :] = are * bre - aim * bim
+            at = pairs + v * SUB
+            product_out[at : at + SUB, :] = are * bim + aim * bre
+            yield
+
+    def turn(pair_in, single_in, wide_out):
         for k in range(clusters):
-            cos_k, sin_k = cosine[k : k + 1], sine[k : k + 1]
-            for v in range(0, pairs // SUB, 2):
-                both = [(cos_k * re - sin_k * im, cos_k * im + sin_k * re) for re, im in far[v : v + 2]]
+            cos_k, sin_k = single_in[k : k + 1, :], single_in[SUB + k : SUB + k + 1, :]
+            for v in range(0, groups, 2):
+                both = []
+                for u in (v, v + 1):
+                    re = pair_in[u * SUB : (u + 1) * SUB, :]
+                    im = pair_in[pairs + u * SUB : pairs + (u + 1) * SUB, :]
+                    both.append((cos_k * re - sin_k * im, cos_k * im + sin_k * re))
                 at = k * pairs + v * SUB
                 for part in range(2):
-                    wide[at : at + 2 * SUB, part * LANES : (part + 1) * LANES] = jnp.concatenate(
+                    wide_out[at : at + 2 * SUB, part * LANES : (part + 1) * LANES] = jnp.concatenate(
                         [both[0][part], both[1][part]], axis=0
                     ).astype(jnp.bfloat16)
-        weighted = jnp.dot(phi[...], wide[...], preferred_element_type=jnp.float32)
-        first_re, first_im = held_rows(first, branches), held_rows(first[branches:], branches)
-        second_re, second_im = cycled_rows(second, branches), cycled_rows(second[branches:], branches)
+                yield
+
+    def finish(i, weighted, product_in):
         sum_re = jnp.zeros((SUB, LANES), jnp.float32)
         sum_im = sum_re
-        for v in range(pairs // SUB):
-            are, aim, bre, bim = first_re[v], first_im[v], second_re[v % period], second_im[v % period]
-            near_re, near_im = are * bre - aim * bim, are * bim + aim * bre
-            wre = weighted[v * SUB : (v + 1) * SUB, :LANES]
-            wim = weighted[v * SUB : (v + 1) * SUB, LANES:]
-            sum_re = sum_re + (near_re * wre - near_im * wim)
-            sum_im = sum_im + (near_re * wim + near_im * wre)
+        for v in range(groups):
+            rows = slice(v * SUB, (v + 1) * SUB)
+            nre = product_in[rows, :]
+            nim = product_in[pairs + v * SUB : pairs + (v + 1) * SUB, :]
+            wre, wim = weighted[rows, :LANES], weighted[rows, LANES:]
+            sum_re = sum_re + (nre * wre - nim * wim)
+            sum_im = sum_im + (nre * wim + nim * wre)
+            yield
         value_re = jnp.sum(sum_re, axis=0, keepdims=True)
         value_im = jnp.sum(sum_im, axis=0, keepdims=True)
-        f2, f3, f4 = (e[comps : comps + 1] for e in others)
-        mismatch = first_freq + f2 - f3 - f4
-        delta = jnp.exp(-((mismatch / smearing) ** 2)) / (smearing * math.sqrt(math.pi))
-        weight = (
-            (1.0 + occupation(f2)) * occupation(f3) * occupation(f4) / occupation(first_freq)
-        )
-        product = first_freq * f2 * f3 * f4
-        term = (value_re * value_re + value_im * value_im) * delta * weight / product
-        term = jnp.where(local >= 0, term, 0.0)
+        yield
+        at = 2 * pairs
+        factor = product_in[at : at + 1, :]
+        local = product_in[at + 1 : at + 2, :].astype(jnp.int32)
+        local = jnp.where(i >= 0, local, -1)
+        term = (value_re * value_re + value_im * value_im) * factor
         size = acc.shape[0]
-        placed = jnp.where(row_iota(size) == head, term, 0.0)
-        parts = []
-        for _ in range(3):
-            part = placed.astype(jnp.bfloat16)
-            parts.append(part)
-            placed = placed - part.astype(jnp.float32)
+        rest = jnp.where(row_iota(size) == lax.shift_right_arithmetic(local, 7), term, 0.0)
+        place[0:1, :] = local
+        yield
+        for n in range(3):
+            part = rest.astype(jnp.bfloat16)
+            placed[n * size : (n + 1) * size, :] = part
+            rest = rest - part.astype(jnp.float32)
+        yield
+
+    def run(*tracks):
+        total_steps = max(n for _, n in tracks)
+        done = [0] * len(tracks)
+        for step in range(1, total_steps + 1):
+            for t, (track, n) in enumerate(tracks):
+                while done[t] * total_steps < step * n:
+                    next(track, None)
+                    done[t] += 1
+        for track, _ in tracks:
+            for _ in track:
+                pass
+
+    gather_steps = 3 * LANES
+    choose_steps = 20 + groups + heads
+    join_steps = 4 + groups
+    turn_steps = clusters * groups // 2
+    finish_steps = groups + 3
+
+    pieces = [(at, min(at + DEPTH, clusters * pairs)) for at in range(0, clusters * pairs, DEPTH)]
+
+    def multiply(wide_in, held):
+        for low, high in pieces:
+            part = jnp.dot(phi[:, low:high], wide_in[low:high, :], preferred_element_type=jnp.float32)
+            held[:] = [part if not held else held[0] + part]
+            yield
+
+    def step(i, p):
+        load(i + 3, 1 - p).start()
+        load(i + 2, p).wait()
         sums = lax.dot_general(
-            jnp.concatenate(parts, axis=0),
-            hot,
+            placed[...],
+            one_hot(place[0:1, :]),
             (((1,), (1,)), ((), ())),
             preferred_element_type=jnp.float32,
         )
+        weighted = []
+        run(
+            (choose(i + 1, gathered[1 - p], pair[1 - p], single[1 - p]), choose_steps),
+            (multiply(wide[1 - p], weighted), len(pieces)),
+            (turn(pair[p], single[p], wide[p]), turn_steps),
+            (join(single[p], product[p]), join_steps),
+            (gather(p), gather_steps),
+        )
+        run((finish(i - 1, weighted[0], product[1 - p]), finish_steps))
+        size = acc.shape[0]
         acc[...] += sums[:size] + sums[size : 2 * size] + sums[2 * size :]
 
-    load(0, spots_a, 0).wait()
-    gather(spots_a, near_a)
-    fetch_phi.wait()
-    side_a, side_b = (near_a, spots_a, 0), (near_b, spots_b, 1)
-
-    def half_step(i, here, there):
-        load(i + 2, *here[1:]).start()
-        load(i + 1, *there[1:]).wait()
-        gather(there[1], there[0])
-        contract(meta[block_at(i)], here[0])
-
-    def two_blocks(j, carry):
-        half_step(2 * j, side_a, side_b)
-
-        @pl.when(2 * j + 1 < count)
+    load(0, 0).start()
+    load(1, 1).start()
+    acc[...] = jnp.zeros_like(acc)
+    placed[...] = jnp.zeros_like(placed)
+    place[...] = jnp.zeros_like(place)
+    fill_table(vectors, lines, table, base)
+    load(0, 0).wait()
+    run((gather(0), gather_steps))
+    load(2, 0).start()
+    load(1, 1).wait()
+    run((choose(0, gathered_a, pair_a, single_a), choose_steps), (gather(1), gather_steps))
+
+    def two_steps(j, carry):
+        step(2 * j, 0)
+
+        @pl.when(2 * j + 1 < count + 2)
         def _():
-            half_step(2 * j + 1, side_b, side_a)
+            step(2 * j + 1, 1)
 
         return carry
 
-    lax.fori_loop(0, lax.div(count + 1, 2), two_blocks, 0)
+    lax.fori_loop(0, lax.div(count + 3, 2), two_steps, 0)
     even = lax.rem(count, 2) == 0
 
     @pl.when(even)
     def _():
-        load(0, *side_b[1:]).wait()
+        load(0, 0).wait()
 
     @pl.when(jnp.logical_not(even))
     def _():
-        load(0, *side_a[1:]).wait()
+        load(0, 1).wait()
 
     out[...] = acc[:heads, :]
+
+
+def rates_call(branches, base, heads, padded, *args):
+    rows, table, phi = args[2], args[4], args[6]
+    pairs = branches * branches
+    singles = 2 * SUB + SLOT + 2 * branches + SUB
+    vmem = pl.BlockSpec(memory_space=pltpu.VMEM)
+    smem = pl.BlockSpec(memory_space=pltpu.SMEM)
+    loose = pl.BlockSpec(memory_space=pl.ANY)
+    rates, _ = pl.pallas_call(
+        functools.partial(kernel, branches, base),
+        out_shape=[
+            jax.ShapeDtypeStruct((heads, LANES), jnp.float32),
+            jax.ShapeDtypeStruct(table.shape, table.dtype),
+        ],
+        in_specs=[smem, smem, loose] + [vmem] * 7,
+        out_specs=[vmem, vmem],
+        input_output_aliases={4: 1},
+        scratch_shapes=[
+            *[pltpu.VMEM((3 * LANES, LANES), jnp.float32)] * 2,
+            *[pltpu.VMEM((2 * pairs, LANES), jnp.float32)] * 2,
+            *[pltpu.VMEM((singles, LANES), jnp.float32)] * 2,
+            *[pltpu.VMEM((phi.shape[1], 2 * LANES), jnp.bfloat16)] * 2,
+            *[pltpu.VMEM((2 * pairs + SUB, LANES), jnp.float32)] * 2,
+            pltpu.VMEM((3 * padded, LANES), jnp.bfloat16),
+            pltpu.VMEM((SUB, LANES), jnp.int32),
+            pltpu.VMEM((padded, LANES), jnp.float32),
+            pltpu.SMEM((AHEAD, *rows.shape[1:]), jnp.int32),
+            pltpu.SemaphoreType.DMA((AHEAD,)),
+        ],
+        compiler_params=pltpu.CompilerParams(vmem_limit_bytes=16 * 1024 * 1024),
+    )(*args)
+    return rates
 
 
 def body(quartets, counts, eig, freq, phi, cells):
@@ -369,37 +509,22 @@
     own_rows = -(-heads * (comps + 1) // 16) * 16
     depth = local // GROUPS
     near = shards - 1
-    table, own = pl.pallas_call(
+    table, own, phi = pl.pallas_call(
         functools.partial(early, kept, heads, near),
         out_shape=[
             jax.ShapeDtypeStruct((shards * depth, LANES), jnp.float32),
             jax.ShapeDtypeStruct((own_rows, LANES), jnp.bfloat16),
+            jax.ShapeDtypeStruct(phi.shape, phi.dtype),
         ],
-        in_specs=[vmem] * (2 * near),
-        out_specs=[vmem, vmem],
+        in_specs=[vmem] * (2 * near + 1),
+        out_specs=[vmem] * 3,
         compiler_params=pltpu.CompilerParams(vmem_limit_bytes=16 * 1024 * 1024),
-    )(*vectors[:near], *rows_of[:near])
-    rates, _ = pl.pallas_call(
-        functools.partial(kernel, branches, near * depth),
-        out_shape=[
-            jax.ShapeDtypeStruct((heads, LANES), jnp.float32),
-            jax.ShapeDtypeStruct(table.shape, table.dtype),
-        ],
-        in_specs=[smem, smem, hbm, vmem, vmem, vmem, far_space] + [vmem] * 3,
-        out_specs=[vmem, vmem],
-        input_output_aliases={4: 1},
-        scratch_shapes=[
-            pltpu.VMEM((3 * LANES, LANES), jnp.float32),
-            pltpu.VMEM((3 * LANES, LANES), jnp.float32),
-            pltpu.SMEM((parts, LANES), jnp.int32),
-            pltpu.SMEM((parts, LANES), jnp.int32),
-            pltpu.VMEM(phi.shape, phi.dtype),
-            pltpu.VMEM((phi.shape[1], 2 * LANES), jnp.bfloat16),
-            pltpu.VMEM((padded, LANES), jnp.float32),
-            pltpu.SemaphoreType.DMA((3,)),
-        ],
-        compiler_params=pltpu.CompilerParams(vmem_limit_bytes=16 * 1024 * 1024),
-    )(
+    )(*vectors[:near], *rows_of[:near], phi)
+    rates = rates_call(
+        branches,
+        near * depth,
+        heads,
+        padded,
         order,
         total,
         rows.reshape(blocks, parts, LANES),

time: 49.9 us -> 44.4 us (0.89)
  Pallas kernels: 24.6 us -> 20.1 us
  waiting for transfers between devices: 7.76 us -> 6.77 us
    pallas_call x1, Pallas kernels: 22.1 us -> 17.6 us  [rates_call(): pl.pallas_call(functools.partial(kernel, branches, base), out_shape=[jax....]
    ppermute x4, waiting for transfers between devices: 5.46 us -> 4.47 us  [across(): return lax.ppermute(x, both, pairs)]
  transfers between devices with their start and end apart: 10 -> 10, of which waited for: 5 -> 5; matrix products, arithmetic and copies ran while one was open for 7% -> 8% of each run, Pallas kernels for 5% -> 6%
where the time goes in v1:
time: 44.4 us; the launch traced here: 44 us
  Pallas kernels  20.1 us (45%)
  starting transfers between devices  9.15 us (21%)
  waiting for transfers between devices  6.77 us (15%)
  other arithmetic  3.98 us (9%)
  local copies, waits for them, and re-layouts  3.28 us (7%)
  between operations  0.73 us (2%)
    pallas_call x1, Pallas kernels, rates_call(): pl.pallas_call(functools.partial(kernel, branches, base), out_shape=[jax....  17.6 us
    ppermute x4, starting transfers between devices, across(): return lax.ppermute(x, both, pairs)  5.07 us
    ppermute x4, waiting for transfers between devices, across(): return lax.ppermute(x, both, pairs)  4.47 us
    ppermute x3, starting transfers between devices, body(): lax.ppermute(coded, 'wa', [(i, i ^ k) for i in range(workers)])  4.01 us
    unnamed x6, local copies, waits for them, and re-layouts  2.77 us
    ppermute x3, waiting for transfers between devices, body(): lax.ppermute(coded, 'wa', [(i, i ^ k) for i in range(workers)])  1.88 us
    pallas_call x1, Pallas kernels, body(): pl.pallas_call(functools.partial(early, kept, heads, near), out_shape=[ja...  1.28 us
    pallas_call x1, Pallas kernels, body(): pl.pallas_call(functools.partial(prepare, branches, local, kept, offset),...  1.28 us
  transfers between devices with their start and end apart: 10, of which 5 were waited for; matrix products, arithmetic and copies ran while one was open for 8% of the time, Pallas kernels for 6%

profile of v1, /device:TPU:18, one launch (start us, length us, event | category | flops | bytes accessed | tf_op | source)
XLA Modules:
  0.0 44.0 jit_solution(11422124317111935750)
XLA Ops:
  0.7 0.9 %add_convert_fusion = s16[32,4,128]{2,1,0:T(4,128)(2,1)S(1)} fusion(s32[32,4,128]{2,1,0:T(4,128)} %param.6, pred[32]{0:T(512)(128)(4,1)S(1)} %iota_compare_fusion.1), kind=kLoop, calls=%fused_computation.6 | loop fusion | flops 49152 | bytes 98336 | tf_op jit(solution)/shard_map/convert_element_type | solution.py:475
  1.6 0.5 %collective-permute-start.2 = (s16[128,128]{1,0:T(8,128)(2,1)S(1)}, s16[128,128]{1,0:T(8,128)(2,1)S(1)}, u32[]{:S(2)}, u32[]{:S(2)}) collective-permute-start(s16[128,128]{1,0:T(8,128)(2,1)S(1)} %bitcast.18), channel_id=1, source_target_pairs={{0,6},{1,7},{2,4},{3,5},{4,2},{5,3},{6,0},{7,1},{8,14},{9,15},{10,... | collective-permute-start | bytes 98312 | tf_op jit(solution)/shard_map/ppermute | solution.py:479
  2.1 3.5 %collective-permute-start.1 = (s16[128,128]{1,0:T(8,128)(2,1)S(1)}, s16[128,128]{1,0:T(8,128)(2,1)S(1)}, u32[]{:S(2)}, u32[]{:S(2)}) collective-permute-start(s16[128,128]{1,0:T(8,128)(2,1)S(1)} %bitcast.19), channel_id=1, source_target_pairs={{0,4},{1,5},{2,6},{3,7},{4,0},{5,1},{6,2},{7,3},{8,12},{9,13},{10,... | collective-permute-start | bytes 98312 | tf_op jit(solution)/shard_map/ppermute | solution.py:479
  5.6 0.0 collective-permute-start
  5.6 0.5 %collective-permute-start.6 = (bf16[96,128]{1,0:T(8,128)(2,1)}, bf16[96,128]{1,0:T(8,128)(2,1)S(1)}, u32[]{:S(2)}, u32[]{:S(2)}) collective-permute-start(bf16[96,128]{1,0:T(8,128)(2,1)} %bitcast.16), channel_id=1, source_target_pairs={{0,8},{1,17},{2,10},{3,19},{4,12},{5,21},{6,14},{7,23},{8,0},{9,25... | collective-permute-start | bytes 73736 | tf_op jit(solution)/shard_map/ppermute | solution.py:460
  6.2 1.5 %collective-permute-start.4 = (bf16[24,12288]{1,0:T(8,128)(2,1)}, bf16[24,12288]{1,0:T(8,128)(2,1)S(1)}, u32[]{:S(2)}, u32[]{:S(2)}) collective-permute-start(bf16[24,12288]{1,0:T(8,128)(2,1)} %refs_0_.1), channel_id=1, source_target_pairs={{0,8},{1,17},{2,10},{3,19},{4,12},{5,21},{6,14},{7,23},{8,0},{9,25... | collective-permute-start | bytes 1769480 | tf_op jit(solution)/shard_map/ppermute | solution.py:460
  7.6 0.0 collective-permute-done.2
  7.7 0.2 collective-permute-done.1
  7.9 1.7 %collective-permute-done = s16[128,128]{1,0:T(8,128)(2,1)S(1)} collective-permute-done((s16[128,128]{1,0:T(8,128)(2,1)S(1)}, s16[128,128]{1,0:T(8,128)(2,1)S(1)}, u32[]{:S(2)}, u32[]{:S(2)}) %collective-permute-start) | collective-permute-done | bytes 32800 | tf_op jit(solution)/shard_map/ppermute | solution.py:479
  9.5 0.1 collective-permute-start.3
  9.6 0.8 %slice_negate_fusion = s32[8,6]{1,0:T(8,128)S(1)} fusion(s32[8,9]{1,0:T(8,128)} %param.11), kind=kLoop, calls=%fused_computation.8 | loop fusion | flops 48 | bytes 384 | tf_op jit(solution)/shard_map/neg | solution.py:505
  10.4 0.8 %add_bitcast_fusion = s32[9,8]{0,1:T(8,128)S(1)} fusion(s32[8,6]{1,0:T(8,128)S(1)} %slice_negate_fusion, s32[8,3]{1,0:T(8,128)} %bitcast.22), kind=kLoop, calls=%fused_computation.7 | loop fusion | flops 72 | bytes 576 | tf_op jit(solution)/shard_map/transpose | solution.py:506
  11.1 0.1 copy.10
  11.2 0.0 collective-permute-done.6.refs_4_
  11.2 1.5 %collective-permute-start.9 = (bf16[96,128]{1,0:T(8,128)(2,1)S(1)}, bf16[96,128]{1,0:T(8,128)(2,1)S(1)}, u32[]{:S(2)}, u32[]{:S(2)}) collective-permute-start(bf16[96,128]{1,0:T(8,128)(2,1)S(1)} %collective-permute-done.6.refs_4_), channel_id=1, source_target_pairs={{0,16},{1,9},{2,18},{3,11},{4,20},{5,13},{6,22},{7,15},{8,24},{9,1... | collective-permute-start | bytes 73736 | tf_op jit(solution)/shard_map/ppermute | solution.py:460
  12.8 0.0 collective-permute-start.7
  12.8 0.0 collective-permute-done.3.refs_1_
  12.8 1.3 %shard_map.64 = (s32[1024,128]{1,0:T(8,128)S(1)}, s32[1024,128]{1,0:T(8,128)S(1)}, f32[8,1024]{1,0:T(8,128)S(1)}) custom-call(s16[512,128]{1,0:T(8,128)(2,1)S(1)} %pad_add_fusion.refs_0_, s16[512,128]{1,0:T(8,128)(2,1)S(1)} %collective-permute-done.3.refs_1_), custom_call_target="tpu_custom_call" | custom-call | tf_op jit(solution)/shard_map/pallas_call | solution.py:487
  14.1 0.1 reshape_squeeze.3
  14.2 0.1 fusion.1
  14.3 2.2 %collective-permute-done.4.refs_1_ = bf16[24,12288]{1,0:T(8,128)(2,1)S(1)} collective-permute-done((bf16[24,12288]{1,0:T(8,128)(2,1)}, bf16[24,12288]{1,0:T(8,128)(2,1)S(1)}, u32[]{:S(2)}, u32[]{:S(2)}) %collective-permute-start.4) | collective-permute-done | bytes 589856 | tf_op jit(solution)/shard_map/ppermute | solution.py:460
  16.5 1.5 %collective-permute-start.8 = (bf16[24,12288]{1,0:T(8,128)(2,1)S(1)}, bf16[24,12288]{1,0:T(8,128)(2,1)S(1)}, u32[]{:S(2)}, u32[]{:S(2)}) collective-permute-start(bf16[24,12288]{1,0:T(8,128)(2,1)S(1)} %collective-permute-done.4.refs_1_), channel_id=1, source_target_pairs={{0,16},{1,9},{2,18},{3,11},{4,20},{5,13},{6,22},{7,15},{8,24},{9,1... | collective-permute-start | bytes 1769480 | tf_op jit(solution)/shard_map/ppermute | solution.py:460
  18.0 0.0 collective-permute-start.5
  18.0 0.1 convert_reduce_fusion
  18.1 0.3 reduce-window.9
  18.5 0.1 slice.21
  18.6 0.1 slice_reduce_fusion.1
  18.7 0.1 add_bitcast_fusion.1
  18.8 0.1 select_reduce_fusion.order
  18.9 0.7 %convert_reduce_fusion.1 = s32[]{:T(128)} fusion(pred[256]{0:T(512)(128)(4,1)S(1)} %get-tuple-element.19), kind=kLoop, calls=%fused_computation.10 | loop fusion | flops 511 | bytes 260 | tf_op jit(solution)/shard_map/reduce_sum | solution.py:504
  19.6 0.0 collective-permute-done.7.refs_5_
  19.6 0.4 collective-permute-done.5.refs_2_
  20.0 0.0 copy-start
  20.0 1.1 %copy-done = bf16[24,12288]{1,0:T(8,128)(2,1)S(1)} copy-done((bf16[24,12288]{1,0:T(8,128)(2,1)S(1)}, bf16[24,12288]{1,0:T(8,128)(2,1)}, u32[]{:S(2)}) %copy-start) | copy-done | bytes 589848
  21.1 0.0 copy-start.1
  21.1 1.0 %copy-done.1 = bf16[144,1152]{1,0:T(8,128)(2,1)S(1)} copy-done((bf16[144,1152]{1,0:T(8,128)(2,1)S(1)}, bf16[144,1152]{1,0:T(8,128)(2,1)}, u32[]{:S(2)}) %copy-start.1) | copy-done | bytes 331800
  22.1 0.0 copy-start.2
  22.1 0.7 %copy-done.2 = bf16[12288]{0:T(1024)(128)(2,1)S(1)} copy-done((bf16[12288]{0:T(1024)(128)(2,1)S(1)}, bf16[12288]{0:T(1024)(128)(2,1)}, u32[]{:S(2)}) %copy-start.2) | copy-done | bytes 24600
  22.8 1.3 %shard_map.65 = (f32[12288,128]{1,0:T(8,128)S(1)}, bf16[304,128]{1,0:T(8,128)(2,1)S(1)}, bf16[144,1152]{1,0:T(8,128)(2,1)S(1)}) custom-call(bf16[24,12288]{1,0:T(8,128)(2,1)S(1)} %copy-done, bf16[24,12288]{1,0:T(8,128)(2,1)S(1)} %collective-permute-done.4.refs_1_, bf16[24,12288]{1,0:T(8,128)(2,1)S(1)} %collective-permute-done.5.refs_2_, ...), custom_call_target="tpu_custom_call" | custom-call | tf_op jit(solution)/shard_map/pallas_call | solution.py:512
  24.1 0.0 collective-permute-done.9.lines
  24.1 2.3 %collective-permute-done.8.vectors = bf16[24,12288]{1,0:T(8,128)(2,1)S(1)} collective-permute-done((bf16[24,12288]{1,0:T(8,128)(2,1)S(1)}, bf16[24,12288]{1,0:T(8,128)(2,1)S(1)}, u32[]{:S(2)}, u32[]{:S(2)}) %collective-permute-start.8) | collective-permute-done | bytes 589856 | tf_op jit(solution)/shard_map/ppermute | solution.py:460
  26.4 0.1 broadcast_in_dim.39.cells
  26.5 17.6 %shard_map.66 = (f32[12,128]{1,0:T(8,128)}, f32[12288,128]{1,0:T(8,128)S(1)}) custom-call(s32[256]{0:T(256)S(1)} %select_reduce_fusion.order, s32[1]{0:T(128)} %bitcast.3.total, s32[256,4,128]{2,1,0:T(4,128)S(1)} %bitcast.14, s32[256,4,128]{2,1,0:T(4,128)S(1)} %bitcast.15, ...), custom_call_target="tpu_custom_call", output_to_operand_aliasing={{1}: (4, {})} | custom-call | tf_op jit(solution)/shard_map/pallas_call | solution.py:413
  (4 shorter events, 0.1 us)
Async XLA Ops:
  1.6 6.0 %collective-permute-start.2 = (s16[128,128]{1,0:T(8,128)(2,1)S(1)}, s16[128,128]{1,0:T(8,128)(2,1)S(1)}, u32[]{:S(2)}, u32[]{:S(2)}) collective-permute-start(s16[128,128]{1,0:T(8,128)(2,1)S(1)} %bitcast.18), channel_id=1, source_target_pairs={{0,6},{1,7},{2,4},{3,5},{4,2},{5,3},{6,0},{7,1},{8,14},{9,15},{10,... | collective-permute-start | bytes 98312 | tf_op jit(solution)/shard_map/ppermute | solution.py:479
  2.1 5.7 %collective-permute-start.1 = (s16[128,128]{1,0:T(8,128)(2,1)S(1)}, s16[128,128]{1,0:T(8,128)(2,1)S(1)}, u32[]{:S(2)}, u32[]{:S(2)}) collective-permute-start(s16[128,128]{1,0:T(8,128)(2,1)S(1)} %bitcast.19), channel_id=1, source_target_pairs={{0,4},{1,5},{2,6},{3,7},{4,0},{5,1},{6,2},{7,3},{8,12},{9,13},{10,... | collective-permute-start | bytes 98312 | tf_op jit(solution)/shard_map/ppermute | solution.py:479
  5.6 3.9 %collective-permute-start = (s16[128,128]{1,0:T(8,128)(2,1)S(1)}, s16[128,128]{1,0:T(8,128)(2,1)S(1)}, u32[]{:S(2)}, u32[]{:S(2)}) collective-permute-start(s16[128,128]{1,0:T(8,128)(2,1)S(1)} %bitcast.20), channel_id=1, source_target_pairs={{0,2},{1,3},{2,0},{3,1},{4,6},{5,7},{6,4},{7,5},{8,10},{9,11},{10,... | collective-permute-start | bytes 98312 | tf_op jit(solution)/shard_map/ppermute | solution.py:479
  5.6 5.6 %collective-permute-start.6 = (bf16[96,128]{1,0:T(8,128)(2,1)}, bf16[96,128]{1,0:T(8,128)(2,1)S(1)}, u32[]{:S(2)}, u32[]{:S(2)}) collective-permute-start(bf16[96,128]{1,0:T(8,128)(2,1)} %bitcast.16), channel_id=1, source_target_pairs={{0,8},{1,17},{2,10},{3,19},{4,12},{5,21},{6,14},{7,23},{8,0},{9,25... | collective-permute-start | bytes 73736 | tf_op jit(solution)/shard_map/ppermute | solution.py:460
  6.2 10.4 %collective-permute-start.4 = (bf16[24,12288]{1,0:T(8,128)(2,1)}, bf16[24,12288]{1,0:T(8,128)(2,1)S(1)}, u32[]{:S(2)}, u32[]{:S(2)}) collective-permute-start(bf16[24,12288]{1,0:T(8,128)(2,1)} %refs_0_.1), channel_id=1, source_target_pairs={{0,8},{1,17},{2,10},{3,19},{4,12},{5,21},{6,14},{7,23},{8,0},{9,25... | collective-permute-start | bytes 1769480 | tf_op jit(solution)/shard_map/ppermute | solution.py:460
  9.5 3.2 %collective-permute-start.3 = (s16[512,128]{1,0:T(8,128)(2,1)S(1)}, s16[512,128]{1,0:T(8,128)(2,1)S(1)}, u32[]{:S(2)}, u32[]{:S(2)}) collective-permute-start(s16[512,128]{1,0:T(8,128)(2,1)S(1)} %pad_add_fusion.refs_0_), channel_id=1, source_target_pairs={{0,1},{1,0},{2,3},{3,2},{4,5},{5,4},{6,7},{7,6},{8,9},{9,8},{10,11... | collective-permute-start | bytes 393224 | tf_op jit(solution)/shard_map/ppermute | solution.py:453
  11.2 12.9 %collective-permute-start.9 = (bf16[96,128]{1,0:T(8,128)(2,1)S(1)}, bf16[96,128]{1,0:T(8,128)(2,1)S(1)}, u32[]{:S(2)}, u32[]{:S(2)}) collective-permute-start(bf16[96,128]{1,0:T(8,128)(2,1)S(1)} %collective-permute-done.6.refs_4_), channel_id=1, source_target_pairs={{0,16},{1,9},{2,18},{3,11},{4,20},{5,13},{6,22},{7,15},{8,24},{9,1... | collective-permute-start | bytes 73736 | tf_op jit(solution)/shard_map/ppermute | solution.py:460
  12.8 6.9 %collective-permute-start.7 = (bf16[96,128]{1,0:T(8,128)(2,1)S(1)}, bf16[96,128]{1,0:T(8,128)(2,1)S(1)}, u32[]{:S(2)}, u32[]{:S(2)}) collective-permute-start(bf16[96,128]{1,0:T(8,128)(2,1)S(1)} %collective-permute-done.6.refs_4_), channel_id=1, source_target_pairs={{0,1},{1,0},{2,3},{3,2},{4,5},{5,4},{6,7},{7,6},{8,9},{9,8},{10,11... | collective-permute-start | bytes 73736 | tf_op jit(solution)/shard_map/ppermute | solution.py:453
  16.5 9.9 %collective-permute-start.8 = (bf16[24,12288]{1,0:T(8,128)(2,1)S(1)}, bf16[24,12288]{1,0:T(8,128)(2,1)S(1)}, u32[]{:S(2)}, u32[]{:S(2)}) collective-permute-start(bf16[24,12288]{1,0:T(8,128)(2,1)S(1)} %collective-permute-done.4.refs_1_), channel_id=1, source_target_pairs={{0,16},{1,9},{2,18},{3,11},{4,20},{5,13},{6,22},{7,15},{8,24},{9,1... | collective-permute-start | bytes 1769480 | tf_op jit(solution)/shard_map/ppermute | solution.py:460
  18.0 2.0 %collective-permute-start.5 = (bf16[24,12288]{1,0:T(8,128)(2,1)S(1)}, bf16[24,12288]{1,0:T(8,128)(2,1)S(1)}, u32[]{:S(2)}, u32[]{:S(2)}) collective-permute-start(bf16[24,12288]{1,0:T(8,128)(2,1)S(1)} %collective-permute-done.4.refs_1_), channel_id=1, source_target_pairs={{0,1},{1,0},{2,3},{3,2},{4,5},{5,4},{6,7},{7,6},{8,9},{9,8},{10,11... | collective-permute-start | bytes 1769480 | tf_op jit(solution)/shard_map/ppermute | solution.py:453
  20.0 1.1 %copy-start = (bf16[24,12288]{1,0:T(8,128)(2,1)S(1)}, bf16[24,12288]{1,0:T(8,128)(2,1)}, u32[]{:S(2)}) copy-start(bf16[24,12288]{1,0:T(8,128)(2,1)} %refs_0_.1) | copy-start | bytes 1769476
  21.1 1.0 %copy-start.1 = (bf16[144,1152]{1,0:T(8,128)(2,1)S(1)}, bf16[144,1152]{1,0:T(8,128)(2,1)}, u32[]{:S(2)}) copy-start(bf16[144,1152]{1,0:T(8,128)(2,1)} %refs_6_.1) | copy-start | bytes 995332
  22.1 0.7 %copy-start.2 = (bf16[12288]{0:T(1024)(128)(2,1)S(1)}, bf16[12288]{0:T(1024)(128)(2,1)}, u32[]{:S(2)}) copy-start(bf16[12288]{0:T(1024)(128)(2,1)} %param.9) | copy-start | bytes 73732

commit v2 on v1

--- a/solution.py
+++ b/solution.py
@@ -34,7 +34,7 @@
 
 
 def prepare(branches, local, kept, offset, *refs):
-    pool, (rows_out, meta_out, flags_out) = refs[:-3], refs[-3:]
+    pool, (rows_out, meta_out, order_out) = refs[:-3], refs[-3:]
     mine = lax.axis_index("pb")
     side = lax.rem(lax.axis_index("wa"), 2)
     start = lax.axis_index("wa") * kept
@@ -55,48 +55,99 @@
     depth = local // GROUPS
     group = ((inner.astype(jnp.float32) + 0.5) * (1.0 / depth)).astype(jnp.int32)
     rows_out[...] = (slot - group) * depth + inner
+    if shards == GROUPS:
+        group = jnp.where(near == GROUPS - 1, group ^ (lax.axis_index("wa") & (GROUPS - 1)), group)
     following = pltpu.roll(modes, count - 1, 0)
     first = modes - start
     valid = heading & (following >= 0) & (first >= 0) & (first < kept)
     meta_out[...] = jnp.where(
         heading, jnp.where(valid, first + lead, -1), point + group * 65536
     )
-    flags_out[...] = lax.dot_general(
+    lanes = (((1,), (1,)), ((), ()))
+    marks = lax.dot_general(
         jnp.ones((SUB, LANES), jnp.bfloat16),
         jnp.where(valid, 1.0, 0.0).astype(jnp.bfloat16),
-        (((1,), (1,)), ((), ())),
+        lanes,
         preferred_element_type=jnp.float32,
     )
-
-
-def fill_table(vectors, lines, table, base):
-    comps, local = vectors.shape
-    depth = local // GROUPS
+    blocks = count // PARTS
+
+    def index(rows, dim):
+        return lax.broadcasted_iota(jnp.int32, (rows, blocks), dim)
+
+    fold = jnp.where(index(count, 0) // PARTS == index(count, 1), 1.0, 0.0).astype(jnp.bfloat16)
+    found = jnp.dot(marks.astype(jnp.bfloat16), fold, preferred_element_type=jnp.float32) > 0.5
+    before = jnp.where(index(blocks, 0) <= index(blocks, 1), 1.0, 0.0).astype(jnp.bfloat16)
+    rank = jnp.dot(
+        jnp.where(found, 1.0, 0.0).astype(jnp.bfloat16), before, preferred_element_type=jnp.float32
+    )
+    spot = jnp.where(found, rank, 0.0)[0:1, :].astype(jnp.int32)
+    chosen = jnp.where(index(blocks, 0) + 1 == spot, 1.0, 0.0).astype(jnp.bfloat16)
+    number = index(SUB, 1)
+    order = jnp.zeros((SUB, blocks), jnp.float32)
+    for digit, scale in ((number & 15, 1.0), (number >> 4, 16.0)):
+        order = order + scale * lax.dot_general(
+            digit.astype(jnp.float32).astype(jnp.bfloat16),
+            chosen,
+            lanes,
+            preferred_element_type=jnp.float32,
+        )
+    order_out[:, :blocks] = order[0:1, :].astype(jnp.int32)
+    order_out[:, blocks:] = jnp.broadcast_to(rank[0:1, blocks - 1 :], (1, LANES)).astype(jnp.int32)
+
+
+def shard_quarters(vectors, lines):
+    depth = vectors.shape[1] // GROUPS
+
+    def quarter(g):
+        def chunk(t):
+            at = g * depth + t * LANES
+            row = at // LANES
+            return vectors[:, at : at + LANES], lines[row : row + 1, :]
+
+        return chunk
+
+    return [quarter(g) for g in range(GROUPS)], depth
+
+
+def piece_quarters(pieces, depth):
+    def quarter(piece):
+        def chunk(t):
+            return piece[:, t * LANES : (t + 1) * LANES], piece[t : t + 1, depth : depth + LANES]
+
+        return chunk
+
+    return [quarter(piece) for piece in pieces], depth
+
+
+def fill_table(source, table, base):
+    quarters, depth = source
     for t in range(depth // LANES):
         stack = []
-        for g in range(GROUPS):
-            at = g * depth + t * LANES
-            stack.append(vectors[:, at : at + LANES].astype(jnp.float32))
-            line = lines[at // LANES : at // LANES + 1, :].astype(jnp.float32)
-            stack.append(jnp.broadcast_to(line, (SLOT - comps, LANES)))
+        for quarter in quarters:
+            vectors, line = quarter(t)
+            stack.append(vectors.astype(jnp.float32))
+            filler = SLOT - vectors.shape[0]
+            stack.append(jnp.broadcast_to(line.astype(jnp.float32), (filler, LANES)))
         row = base + t * LANES
         table[row : row + LANES, :] = jnp.concatenate(stack, axis=0).T
 
 
-def early(kept, heads, near, *refs):
-    vectors, lines = refs[:near], refs[near : 2 * near]
-    phi_in, table, own, phi = refs[2 * near :]
+def begin(kept, heads, vectors, lines, phi_in, cells_in, table, own, phi, cells):
+    comps = vectors.shape[0]
     phi[...] = phi_in[...]
-    comps, local = vectors[0].shape
-    for at in range(near):
-        fill_table(vectors[at], lines[at], table, at * (local // GROUPS))
+    cell = cells_in[...]
+    for j in range(cell.shape[1]):
+        column = cell[:, j : j + 1]
+        cells[j] = jnp.broadcast_to(column if j < 3 else -column, (cell.shape[0], LANES))
+    fill_table(shard_quarters(vectors, lines), table, 0)
     start = lax.axis_index("wa") * kept // LANES
-    own_lines = lines[0][...].astype(jnp.float32)
+    own_lines = lines[...].astype(jnp.float32)
     line_rows = row_iota(own_lines.shape[0])
     parts = []
     for h in range(heads):
         at = pl.multiple_of((start + h) * LANES, LANES)
-        parts.append(vectors[0][:, pl.ds(at, LANES)].astype(jnp.float32))
+        parts.append(vectors[:, pl.ds(at, LANES)].astype(jnp.float32))
     for h in range(heads):
         parts.append(
             jnp.sum(jnp.where(line_rows == start + h, own_lines, 0.0), axis=0, keepdims=True)
@@ -104,6 +155,18 @@
     filler = own.shape[0] - heads * comps - heads
     parts.append(jnp.zeros((filler, LANES), jnp.float32))
     own[...] = jnp.concatenate(parts, axis=0).astype(jnp.bfloat16)
+
+
+def extend(slots, pieces, table_in, *refs):
+    table = refs[-1]
+    whole = len(slots)
+    for n, slot in enumerate(slots):
+        vectors, lines = refs[n], refs[whole + n]
+        fill_table(shard_quarters(vectors, lines), table, slot * vectors.shape[1] // GROUPS)
+    if pieces:
+        parts = refs[2 * whole : -1]
+        depth = parts[0].shape[1] - LANES
+        fill_table(piece_quarters(parts, depth), table, (GROUPS - 1) * depth)
 
 
 def held_rows(e, branches):
@@ -128,7 +191,6 @@
     branches,
     base,
     order,
-    total,
     rows_any,
     meta,
     table_in,
@@ -161,13 +223,13 @@
     clusters = SUB
     heads = out.shape[0]
     log = QMESH.bit_length() - 1
-    count = total[0]
     last = rows_any.shape[0] - 1
+    count = order[0, last + 1]
     gathered, pair, single = (gathered_a, gathered_b), (pair_a, pair_b), (single_a, single_b)
     wide, product = (wide_a, wide_b), (product_a, product_b)
 
     def block_at(i):
-        return order[jnp.clip(i, 0, last)]
+        return order[0, jnp.clip(i, 0, last)]
 
     def load(i, p):
         return pltpu.make_async_copy(rows_any.at[block_at(i)], spots.at[p], sems.at[p])
@@ -373,7 +435,7 @@
     acc[...] = jnp.zeros_like(acc)
     placed[...] = jnp.zeros_like(placed)
     place[...] = jnp.zeros_like(place)
-    fill_table(vectors, lines, table, base)
+    fill_table(shard_quarters(vectors, lines), table, base)
     load(0, 0).wait()
     run((gather(0), gather_steps))
     load(2, 0).start()
@@ -404,7 +466,7 @@
 
 
 def rates_call(branches, base, heads, padded, *args):
-    rows, table, phi = args[2], args[4], args[6]
+    rows, table, phi = args[1], args[3], args[5]
     pairs = branches * branches
     singles = 2 * SUB + SLOT + 2 * branches + SUB
     vmem = pl.BlockSpec(memory_space=pltpu.VMEM)
@@ -416,9 +478,9 @@
             jax.ShapeDtypeStruct((heads, LANES), jnp.float32),
             jax.ShapeDtypeStruct(table.shape, table.dtype),
         ],
-        in_specs=[smem, smem, loose] + [vmem] * 7,
+        in_specs=[smem, loose] + [vmem] * 7,
         out_specs=[vmem, vmem],
-        input_output_aliases={4: 1},
+        input_output_aliases={3: 1},
         scratch_shapes=[
             *[pltpu.VMEM((3 * LANES, LANES), jnp.float32)] * 2,
             *[pltpu.VMEM((2 * pairs, LANES), jnp.float32)] * 2,
@@ -447,6 +509,7 @@
     clusters = cells.shape[0]
     offset = local * shards // 2
     both = ("pb", "wa")
+    worker = lax.axis_index("wa")
     lines = freq.reshape(local // LANES, LANES)
 
     def swap(x):
@@ -459,12 +522,26 @@
                 pairs.append((p * workers + w, (p ^ (odd if w % 2 else even)) * workers + w))
         return lax.ppermute(x, both, pairs)
 
+    depth = local // GROUPS
+    pieces = []
     if shards == GROUPS:
-        vectors, rows_of = [eig], [lines]
-        for owned, kind in ((eig, vectors), (lines, rows_of)):
-            one = across(owned, 1, 2)
-            far = across(one, 2, 1)
-            kind += [one, swap(one), far]
+        which = worker % GROUPS
+        rows = depth // LANES
+        payload = jnp.concatenate(
+            [
+                lax.dynamic_slice_in_dim(eig, which * depth, depth, 1),
+                lax.dynamic_slice_in_dim(lines, which * rows, rows, 0),
+            ],
+            axis=1,
+        )
+        straight = across(payload, shards - 1, shards - 1)
+        one = across(eig, 1, 2)
+        one_lines = across(lines, 1, 2)
+        along = lax.ppermute(straight, "wa", [(i, i ^ 2) for i in range(workers)])
+        pieces = [straight, swap(straight), along]
+        pieces.append(swap(along))
+        vectors = [eig, one, swap(one)]
+        rows_of = [lines, one_lines, swap(one_lines)]
     else:
         vectors, rows_of = [eig], [lines]
         for k in range(1, shards):
@@ -484,57 +561,56 @@
     hbm = pl.BlockSpec(memory_space=pl.ANY)
     far_space = pl.BlockSpec(memory_space=pltpu.HBM)
     total_rows = workers * held * parts
-    rows, meta, flags = pl.pallas_call(
+    rows, meta, order = pl.pallas_call(
         functools.partial(prepare, branches, local, kept, offset),
         out_shape=[
             jax.ShapeDtypeStruct((total_rows, LANES), jnp.int32),
             jax.ShapeDtypeStruct((total_rows, LANES), jnp.int32),
-            jax.ShapeDtypeStruct((SUB, total_rows), jnp.float32),
+            jax.ShapeDtypeStruct((1, total_rows // parts + LANES), jnp.int32),
         ],
         in_specs=[vmem, vmem],
+        out_specs=[vmem] * 3,
         compiler_params=pltpu.CompilerParams(vmem_limit_bytes=16 * 1024 * 1024),
     )(column, other_column)
     blocks = total_rows // parts
-    index = jnp.arange(blocks, dtype=jnp.int32)
-    owned = flags[0].reshape(blocks, parts)[:, 0] > 0.5
-    place = jnp.cumsum(owned.astype(jnp.int32)) - 1
-    order = jnp.sum(
-        jnp.where((place[None, :] == index[:, None]) & owned[None, :], index[None, :], 0), axis=1
-    )
-    total = jnp.sum(owned.astype(jnp.int32)).reshape(1)
-    signed = jnp.concatenate([cells[:, :3], -cells[:, 3:]], axis=1)
-    spread_cells = jnp.broadcast_to(signed.T[:, :, None], (9, clusters, LANES))
-
     padded = -(-heads // 16) * 16
     own_rows = -(-heads * (comps + 1) // 16) * 16
-    depth = local // GROUPS
-    near = shards - 1
-    table, own, phi = pl.pallas_call(
-        functools.partial(early, kept, heads, near),
+    table, own, phi, spread_cells = pl.pallas_call(
+        functools.partial(begin, kept, heads),
         out_shape=[
             jax.ShapeDtypeStruct((shards * depth, LANES), jnp.float32),
             jax.ShapeDtypeStruct((own_rows, LANES), jnp.bfloat16),
             jax.ShapeDtypeStruct(phi.shape, phi.dtype),
+            jax.ShapeDtypeStruct((cells.shape[1], clusters, LANES), jnp.int32),
         ],
-        in_specs=[vmem] * (2 * near + 1),
-        out_specs=[vmem] * 3,
+        in_specs=[vmem] * 4,
+        out_specs=[vmem] * 4,
         compiler_params=pltpu.CompilerParams(vmem_limit_bytes=16 * 1024 * 1024),
-    )(*vectors[:near], *rows_of[:near], phi)
+    )(eig, lines, phi, cells)
+    final = len(vectors) - 1
+    whole = tuple(range(1, final))
+    table = pl.pallas_call(
+        functools.partial(extend, whole, bool(pieces)),
+        out_shape=jax.ShapeDtypeStruct(table.shape, table.dtype),
+        in_specs=[vmem] * (1 + 2 * len(whole) + len(pieces)),
+        out_specs=vmem,
+        input_output_aliases={0: 0},
+        compiler_params=pltpu.CompilerParams(vmem_limit_bytes=16 * 1024 * 1024),
+    )(table, *vectors[1:final], *rows_of[1:final], *pieces)
     rates = rates_call(
         branches,
-        near * depth,
+        final * depth,
         heads,
         padded,
         order,
-        total,
         rows.reshape(blocks, parts, LANES),
         meta.reshape(blocks, parts, LANES),
         table,
         own,
         phi,
         spread_cells,
-        vectors[near],
-        rows_of[near],
+        vectors[final],
+        rows_of[final],
     )
     rates = rates.reshape(heads * LANES)
     if heads * LANES == kept:

time: 44.4 us -> 51 us (1.15)
  the two profiles are of different devices: /device:TPU:18 before, /device:TPU:1 now
where the time goes in v2:
time: 51 us; the launch traced here: 50.6 us
  starting transfers between devices  19.5 us (38%)
  Pallas kernels  15.7 us (31%)
  waiting for transfers between devices  8.57 us (17%)
  local copies, waits for them, and re-layouts  5.11 us (10%)
  other arithmetic  0.97 us (2%)
  between operations  0.75 us (1%)
    pallas_call x1, Pallas kernels, rates_call(): pl.pallas_call(functools.partial(kernel, branches, base), out_shape=[jax....  13.1 us
    ppermute x5, starting transfers between devices, swap(): return lax.ppermute(x, 'wa', [(i, i ^ 1) for i in range(workers)])  10.5 us
    ppermute x3, waiting for transfers between devices, across(): return lax.ppermute(x, both, pairs)  8.53 us
    ppermute x3, starting transfers between devices, body(): lax.ppermute(coded, 'wa', [(i, i ^ k) for i in range(workers)])  3.61 us
    ppermute x3, starting transfers between devices, across(): return lax.ppermute(x, both, pairs)  3.5 us
    unnamed x8, local copies, waits for them, and re-layouts  3.46 us
    ppermute x1, starting transfers between devices, body(): along = lax.ppermute(straight, 'wa', [(i, i ^ 2) for i in range(workers)])  1.89 us
    pallas_call x1, Pallas kernels, body(): pl.pallas_call(functools.partial(prepare, branches, local, kept, offset),...  1.27 us
  transfers between devices with their start and end apart: 12, of which 2 were waited for; matrix products, arithmetic and copies ran while one was open for 5% of the time, Pallas kernels for 5%

profile of v2, /device:TPU:1, one launch (start us, length us, event | category | flops | bytes accessed | tf_op | source)
XLA Modules:
  0.0 50.6 jit_solution(12414457195419120111)
XLA Ops:
  0.0 2.1 %collective-permute-start.4 = (bf16[24,12288]{1,0:T(8,128)(2,1)}, bf16[24,12288]{1,0:T(8,128)(2,1)S(1)}, u32[]{:S(2)}, u32[]{:S(2)}) collective-permute-start(bf16[24,12288]{1,0:T(8,128)(2,1)} %vectors.1), channel_id=1, source_target_pairs={{0,8},{1,17},{2,10},{3,19},{4,12},{5,21},{6,14},{7,23},{8,0},{9,25... | collective-permute-start | bytes 1769480 | tf_op jit(solution)/shard_map/ppermute | solution.py:523
  2.1 1.0 %constant_dynamic-slice_fusion.1 = bf16[24,3072]{1,0:T(8,128)(2,1)S(1)} fusion(bf16[24,12288]{1,0:T(8,128)(2,1)} %vectors.1, s32[]{:T(128)S(6)} %select_n.19), kind=kLoop, calls=%fused_computation.4 | loop fusion | bytes 294916 | tf_op jit(solution)/shard_map/dynamic_slice | solution.py:532
  3.0 0.7 %constant_dynamic-slice_fusion = bf16[24,128]{1,0:T(8,128)(2,1)S(1)} fusion(bf16[96,128]{1,0:T(8,128)(2,1)} %bitcast.9, s32[]{:T(128)S(6)} %select_n.20), kind=kLoop, calls=%fused_computation.3 | loop fusion | bytes 12292 | tf_op jit(solution)/shard_map/dynamic_slice | solution.py:533
  3.7 1.2 %collective-permute-start.6 = (bf16[24,3200]{1,0:T(8,128)(2,1)S(1)}, bf16[24,3200]{1,0:T(8,128)(2,1)S(1)}, u32[]{:S(2)}, u32[]{:S(2)}) collective-permute-start(bf16[24,3200]{1,0:T(8,128)(2,1)S(1)} %pad_maximum_fusion), channel_id=1, source_target_pairs={{0,24},{1,25},{2,26},{3,27},{4,28},{5,29},{6,30},{7,31},{8,16},{9,... | collective-permute-start | bytes 460808 | tf_op jit(solution)/shard_map/ppermute | solution.py:523
  5.6 5.9 %collective-permute-done.4.refs_0_ = bf16[24,12288]{1,0:T(8,128)(2,1)S(1)} collective-permute-done((bf16[24,12288]{1,0:T(8,128)(2,1)}, bf16[24,12288]{1,0:T(8,128)(2,1)S(1)}, u32[]{:S(2)}, u32[]{:S(2)}) %collective-permute-start.4) | collective-permute-done | bytes 589856 | tf_op jit(solution)/shard_map/ppermute | solution.py:523
  11.5 1.2 %collective-permute-start.10 = (bf16[24,12288]{1,0:T(8,128)(2,1)S(1)}, bf16[24,12288]{1,0:T(8,128)(2,1)S(1)}, u32[]{:S(2)}, u32[]{:S(2)}) collective-permute-start(bf16[24,12288]{1,0:T(8,128)(2,1)S(1)} %collective-permute-done.4.refs_0_), channel_id=1, source_target_pairs={{0,1},{1,0},{2,3},{3,2},{4,5},{5,4},{6,7},{7,6},{8,9},{9,8},{10,11... | collective-permute-start | bytes 1769480 | tf_op jit(solution)/shard_map/ppermute | solution.py:516
  12.7 0.0 collective-permute-done.6.refs_2_
  12.7 1.9 %collective-permute-start.8 = (bf16[24,3200]{1,0:T(8,128)(2,1)S(1)}, bf16[24,3200]{1,0:T(8,128)(2,1)S(1)}, u32[]{:S(2)}, u32[]{:S(2)}) collective-permute-start(bf16[24,3200]{1,0:T(8,128)(2,1)S(1)} %collective-permute-done.6.refs_2_), channel_id=1, source_target_pairs={{0,2},{1,3},{2,0},{3,1},{4,6},{5,7},{6,4},{7,5},{8,10},{9,11},{10,... | collective-permute-start | bytes 460808 | tf_op jit(solution)/shard_map/ppermute | solution.py:540
  14.6 0.9 %add_convert_fusion = s16[32,4,128]{2,1,0:T(4,128)(2,1)S(1)} fusion(s32[32,4,128]{2,1,0:T(4,128)} %param.6, pred[32]{0:T(512)(128)(4,1)S(1)} %iota_compare_fusion), kind=kLoop, calls=%fused_computation.2 | loop fusion | flops 49152 | bytes 98336 | tf_op jit(solution)/shard_map/convert_element_type | solution.py:552
  15.5 0.1 collective-permute-start
  15.6 2.5 %collective-permute-start.1 = (s16[128,128]{1,0:T(8,128)(2,1)S(1)}, s16[128,128]{1,0:T(8,128)(2,1)S(1)}, u32[]{:S(2)}, u32[]{:S(2)}) collective-permute-start(s16[128,128]{1,0:T(8,128)(2,1)S(1)} %bitcast.13), channel_id=1, source_target_pairs={{0,4},{1,5},{2,6},{3,7},{4,0},{5,1},{6,2},{7,3},{8,12},{9,13},{10,... | collective-permute-start | bytes 98312 | tf_op jit(solution)/shard_map/ppermute | solution.py:556
  18.1 1.1 %collective-permute-start.2 = (s16[128,128]{1,0:T(8,128)(2,1)S(1)}, s16[128,128]{1,0:T(8,128)(2,1)S(1)}, u32[]{:S(2)}, u32[]{:S(2)}) collective-permute-start(s16[128,128]{1,0:T(8,128)(2,1)S(1)} %bitcast.14), channel_id=1, source_target_pairs={{0,6},{1,7},{2,4},{3,5},{4,2},{5,3},{6,0},{7,1},{8,14},{9,15},{10,... | collective-permute-start | bytes 98312 | tf_op jit(solution)/shard_map/ppermute | solution.py:556
  19.2 0.0 collective-permute-done
  19.2 3.7 %collective-permute-start.7 = (bf16[24,3200]{1,0:T(8,128)(2,1)S(1)}, bf16[24,3200]{1,0:T(8,128)(2,1)S(1)}, u32[]{:S(2)}, u32[]{:S(2)}) collective-permute-start(bf16[24,3200]{1,0:T(8,128)(2,1)S(1)} %collective-permute-done.6.refs_2_), channel_id=1, source_target_pairs={{0,1},{1,0},{2,3},{3,2},{4,5},{5,4},{6,7},{7,6},{8,9},{9,8},{10,11... | collective-permute-start | bytes 460808 | tf_op jit(solution)/shard_map/ppermute | solution.py:516
  22.8 0.0 collective-permute-done.8.refs_4_
  22.8 0.1 collective-permute-start.9
  22.9 0.0 collective-permute-done.1
  22.9 0.0 collective-permute-done.2
  22.9 4.3 %collective-permute-start.3 = (s16[512,128]{1,0:T(8,128)(2,1)S(1)}, s16[512,128]{1,0:T(8,128)(2,1)S(1)}, u32[]{:S(2)}, u32[]{:S(2)}) collective-permute-start(s16[512,128]{1,0:T(8,128)(2,1)S(1)} %pad_add_fusion.refs_0_), channel_id=1, source_target_pairs={{0,1},{1,0},{2,3},{3,2},{4,5},{5,4},{6,7},{7,6},{8,9},{9,8},{10,11... | collective-permute-start | bytes 393224 | tf_op jit(solution)/shard_map/ppermute | solution.py:516
  27.3 0.2 collective-permute-start.5
  27.5 2.7 %collective-permute-done.5.refs_1_ = bf16[96,128]{1,0:T(8,128)(2,1)S(1)} collective-permute-done((bf16[96,128]{1,0:T(8,128)(2,1)}, bf16[96,128]{1,0:T(8,128)(2,1)S(1)}, u32[]{:S(2)}, u32[]{:S(2)}) %collective-permute-start.5) | collective-permute-done | bytes 24608 | tf_op jit(solution)/shard_map/ppermute | solution.py:523
  30.1 1.2 %collective-permute-start.11 = (bf16[96,128]{1,0:T(8,128)(2,1)S(1)}, bf16[96,128]{1,0:T(8,128)(2,1)S(1)}, u32[]{:S(2)}, u32[]{:S(2)}) collective-permute-start(bf16[96,128]{1,0:T(8,128)(2,1)S(1)} %collective-permute-done.5.refs_1_), channel_id=1, source_target_pairs={{0,1},{1,0},{2,3},{3,2},{4,5},{5,4},{6,7},{7,6},{8,9},{9,8},{10,11... | collective-permute-start | bytes 73736 | tf_op jit(solution)/shard_map/ppermute | solution.py:516
  31.4 0.0 copy-start
  31.4 1.1 %copy-done = bf16[24,12288]{1,0:T(8,128)(2,1)S(1)} copy-done((bf16[24,12288]{1,0:T(8,128)(2,1)S(1)}, bf16[24,12288]{1,0:T(8,128)(2,1)}, u32[]{:S(2)}) %copy-start) | copy-done | bytes 589848
  32.4 0.0 copy-start.1
  32.4 1.0 %copy-done.1 = bf16[144,1152]{1,0:T(8,128)(2,1)S(1)} copy-done((bf16[144,1152]{1,0:T(8,128)(2,1)S(1)}, bf16[144,1152]{1,0:T(8,128)(2,1)}, u32[]{:S(2)}) %copy-start.1) | copy-done | bytes 331800
  33.4 0.0 copy-start.2
  33.4 0.7 %copy-done.2 = bf16[12288]{0:T(1024)(128)(2,1)S(1)} copy-done((bf16[12288]{0:T(1024)(128)(2,1)S(1)}, bf16[12288]{0:T(1024)(128)(2,1)}, u32[]{:S(2)}) %copy-start.2) | copy-done | bytes 24600
  34.1 0.0 copy-start.3
  34.2 0.7 %copy-done.3 = s32[8,9]{1,0:T(8,128)S(1)} copy-done((s32[8,9]{1,0:T(8,128)S(1)}, s32[8,9]{1,0:T(8,128)}, u32[]{:S(2)}) %copy-start.3) | copy-done | bytes 312
  34.8 0.5 shard_map.65
  35.3 0.0 collective-permute-done.3.refs_1_
  35.4 1.3 %shard_map.64 = (s32[1024,128]{1,0:T(8,128)S(1)}, s32[1024,128]{1,0:T(8,128)S(1)}, s32[1,384]{1,0:T(1,128)S(1)}) custom-call(s16[512,128]{1,0:T(8,128)(2,1)S(1)} %pad_add_fusion.refs_0_, s16[512,128]{1,0:T(8,128)(2,1)S(1)} %collective-permute-done.3.refs_1_), custom_call_target="tpu_custom_call" | custom-call | tf_op jit(solution)/shard_map/pallas_call | solution.py:564
  36.6 0.0 collective-permute-done.7.refs_3_
  36.7 0.0 collective-permute-done.9.refs_5_
  36.7 0.9 %shard_map.66.table_in = f32[12288,128]{1,0:T(8,128)S(1)} custom-call(f32[12288,128]{1,0:T(8,128)S(1)} %get-tuple-element.16.table_in, bf16[24,12288]{1,0:T(8,128)(2,1)S(1)} %collective-permute-done.4.refs_0_, bf16[96,128]{1,0:T(8,128)(2,1)S(1)} %collective-permute-done.5.refs_1_, ...), custom_call_target="tpu_custom_call", output_to_operand_aliasing={{}: (0, {})} | custom-call | tf_op jit(solution)/shard_map/pallas_call | solution.py:592
  37.5 0.0 collective-permute-done.11.lines
  37.5 0.0 collective-permute-done.10.vectors
  37.6 13.1 %shard_map.67 = (f32[12,128]{1,0:T(8,128)}, f32[12288,128]{1,0:T(8,128)S(1)}) custom-call(s32[1,384]{1,0:T(1,128)S(1)} %get-tuple-element.13.order, s32[256,4,128]{2,1,0:T(4,128)S(1)} %bitcast.7, s32[256,4,128]{2,1,0:T(4,128)S(1)} %bitcast.8, f32[12288,128]{1,0:T(8,128)S(1)} %shard_map.66.table_in, ...), custom_call_target="tpu_custom_call", output_to_operand_aliasing={{1}: (3, {})} | custom-call | tf_op jit(solution)/shard_map/pallas_call | solution.py:475
  (3 shorter events, 0.0 us)
Async XLA Ops:
  0.0 11.5 %collective-permute-start.4 = (bf16[24,12288]{1,0:T(8,128)(2,1)}, bf16[24,12288]{1,0:T(8,128)(2,1)S(1)}, u32[]{:S(2)}, u32[]{:S(2)}) collective-permute-start(bf16[24,12288]{1,0:T(8,128)(2,1)} %vectors.1), channel_id=1, source_target_pairs={{0,8},{1,17},{2,10},{3,19},{4,12},{5,21},{6,14},{7,23},{8,0},{9,25... | collective-permute-start | bytes 1769480 | tf_op jit(solution)/shard_map/ppermute | solution.py:523
  3.7 9.0 %collective-permute-start.6 = (bf16[24,3200]{1,0:T(8,128)(2,1)S(1)}, bf16[24,3200]{1,0:T(8,128)(2,1)S(1)}, u32[]{:S(2)}, u32[]{:S(2)}) collective-permute-start(bf16[24,3200]{1,0:T(8,128)(2,1)S(1)} %pad_maximum_fusion), channel_id=1, source_target_pairs={{0,24},{1,25},{2,26},{3,27},{4,28},{5,29},{6,30},{7,31},{8,16},{9,... | collective-permute-start | bytes 460808 | tf_op jit(solution)/shard_map/ppermute | solution.py:523
  11.5 26.1 %collective-permute-start.10 = (bf16[24,12288]{1,0:T(8,128)(2,1)S(1)}, bf16[24,12288]{1,0:T(8,128)(2,1)S(1)}, u32[]{:S(2)}, u32[]{:S(2)}) collective-permute-start(bf16[24,12288]{1,0:T(8,128)(2,1)S(1)} %collective-permute-done.4.refs_0_), channel_id=1, source_target_pairs={{0,1},{1,0},{2,3},{3,2},{4,5},{5,4},{6,7},{7,6},{8,9},{9,8},{10,11... | collective-permute-start | bytes 1769480 | tf_op jit(solution)/shard_map/ppermute | solution.py:516
  12.7 10.1 %collective-permute-start.8 = (bf16[24,3200]{1,0:T(8,128)(2,1)S(1)}, bf16[24,3200]{1,0:T(8,128)(2,1)S(1)}, u32[]{:S(2)}, u32[]{:S(2)}) collective-permute-start(bf16[24,3200]{1,0:T(8,128)(2,1)S(1)} %collective-permute-done.6.refs_2_), channel_id=1, source_target_pairs={{0,2},{1,3},{2,0},{3,1},{4,6},{5,7},{6,4},{7,5},{8,10},{9,11},{10,... | collective-permute-start | bytes 460808 | tf_op jit(solution)/shard_map/ppermute | solution.py:540
  15.5 3.6 %collective-permute-start = (s16[128,128]{1,0:T(8,128)(2,1)S(1)}, s16[128,128]{1,0:T(8,128)(2,1)S(1)}, u32[]{:S(2)}, u32[]{:S(2)}) collective-permute-start(s16[128,128]{1,0:T(8,128)(2,1)S(1)} %bitcast.12), channel_id=1, source_target_pairs={{0,2},{1,3},{2,0},{3,1},{4,6},{5,7},{6,4},{7,5},{8,10},{9,11},{10,... | collective-permute-start | bytes 98312 | tf_op jit(solution)/shard_map/ppermute | solution.py:556
  15.6 7.3 %collective-permute-start.1 = (s16[128,128]{1,0:T(8,128)(2,1)S(1)}, s16[128,128]{1,0:T(8,128)(2,1)S(1)}, u32[]{:S(2)}, u32[]{:S(2)}) collective-permute-start(s16[128,128]{1,0:T(8,128)(2,1)S(1)} %bitcast.13), channel_id=1, source_target_pairs={{0,4},{1,5},{2,6},{3,7},{4,0},{5,1},{6,2},{7,3},{8,12},{9,13},{10,... | collective-permute-start | bytes 98312 | tf_op jit(solution)/shard_map/ppermute | solution.py:556
  18.1 4.8 %collective-permute-start.2 = (s16[128,128]{1,0:T(8,128)(2,1)S(1)}, s16[128,128]{1,0:T(8,128)(2,1)S(1)}, u32[]{:S(2)}, u32[]{:S(2)}) collective-permute-start(s16[128,128]{1,0:T(8,128)(2,1)S(1)} %bitcast.14), channel_id=1, source_target_pairs={{0,6},{1,7},{2,4},{3,5},{4,2},{5,3},{6,0},{7,1},{8,14},{9,15},{10,... | collective-permute-start | bytes 98312 | tf_op jit(solution)/shard_map/ppermute | solution.py:556
  19.2 17.5 %collective-permute-start.7 = (bf16[24,3200]{1,0:T(8,128)(2,1)S(1)}, bf16[24,3200]{1,0:T(8,128)(2,1)S(1)}, u32[]{:S(2)}, u32[]{:S(2)}) collective-permute-start(bf16[24,3200]{1,0:T(8,128)(2,1)S(1)} %collective-permute-done.6.refs_2_), channel_id=1, source_target_pairs={{0,1},{1,0},{2,3},{3,2},{4,5},{5,4},{6,7},{7,6},{8,9},{9,8},{10,11... | collective-permute-start | bytes 460808 | tf_op jit(solution)/shard_map/ppermute | solution.py:516
  22.8 13.8 %collective-permute-start.9 = (bf16[24,3200]{1,0:T(8,128)(2,1)S(1)}, bf16[24,3200]{1,0:T(8,128)(2,1)S(1)}, u32[]{:S(2)}, u32[]{:S(2)}) collective-permute-start(bf16[24,3200]{1,0:T(8,128)(2,1)S(1)} %collective-permute-done.8.refs_4_), channel_id=1, source_target_pairs={{0,1},{1,0},{2,3},{3,2},{4,5},{5,4},{6,7},{7,6},{8,9},{9,8},{10,11... | collective-permute-start | bytes 460808 | tf_op jit(solution)/shard_map/ppermute | solution.py:516
  22.9 12.4 %collective-permute-start.3 = (s16[512,128]{1,0:T(8,128)(2,1)S(1)}, s16[512,128]{1,0:T(8,128)(2,1)S(1)}, u32[]{:S(2)}, u32[]{:S(2)}) collective-permute-start(s16[512,128]{1,0:T(8,128)(2,1)S(1)} %pad_add_fusion.refs_0_), channel_id=1, source_target_pairs={{0,1},{1,0},{2,3},{3,2},{4,5},{5,4},{6,7},{7,6},{8,9},{9,8},{10,11... | collective-permute-start | bytes 393224 | tf_op jit(solution)/shard_map/ppermute | solution.py:516
  27.3 2.9 %collective-permute-start.5 = (bf16[96,128]{1,0:T(8,128)(2,1)}, bf16[96,128]{1,0:T(8,128)(2,1)S(1)}, u32[]{:S(2)}, u32[]{:S(2)}) collective-permute-start(bf16[96,128]{1,0:T(8,128)(2,1)} %bitcast.10), channel_id=1, source_target_pairs={{0,8},{1,17},{2,10},{3,19},{4,12},{5,21},{6,14},{7,23},{8,0},{9,25... | collective-permute-start | bytes 73736 | tf_op jit(solution)/shard_map/ppermute | solution.py:523
  30.1 7.4 %collective-permute-start.11 = (bf16[96,128]{1,0:T(8,128)(2,1)S(1)}, bf16[96,128]{1,0:T(8,128)(2,1)S(1)}, u32[]{:S(2)}, u32[]{:S(2)}) collective-permute-start(bf16[96,128]{1,0:T(8,128)(2,1)S(1)} %collective-permute-done.5.refs_1_), channel_id=1, source_target_pairs={{0,1},{1,0},{2,3},{3,2},{4,5},{5,4},{6,7},{7,6},{8,9},{9,8},{10,11... | collective-permute-start | bytes 73736 | tf_op jit(solution)/shard_map/ppermute | solution.py:516
  31.4 1.1 %copy-start = (bf16[24,12288]{1,0:T(8,128)(2,1)S(1)}, bf16[24,12288]{1,0:T(8,128)(2,1)}, u32[]{:S(2)}) copy-start(bf16[24,12288]{1,0:T(8,128)(2,1)} %vectors.1) | copy-start | bytes 1769476
  32.4 1.0 %copy-start.1 = (bf16[144,1152]{1,0:T(8,128)(2,1)S(1)}, bf16[144,1152]{1,0:T(8,128)(2,1)}, u32[]{:S(2)}) copy-start(bf16[144,1152]{1,0:T(8,128)(2,1)} %phi_in.1) | copy-start | bytes 995332
  33.4 0.7 %copy-start.2 = (bf16[12288]{0:T(1024)(128)(2,1)S(1)}, bf16[12288]{0:T(1024)(128)(2,1)}, u32[]{:S(2)}) copy-start(bf16[12288]{0:T(1024)(128)(2,1)} %param.9) | copy-start | bytes 73732
  34.1 0.7 %copy-start.3 = (s32[8,9]{1,0:T(8,128)S(1)}, s32[8,9]{1,0:T(8,128)}, u32[]{:S(2)}) copy-start(s32[8,9]{1,0:T(8,128)} %cells_in.1) | copy-start | bytes 868

commit v3 on v2

--- a/solution.py
+++ b/solution.py
@@ -55,8 +55,6 @@
     depth = local // GROUPS
     group = ((inner.astype(jnp.float32) + 0.5) * (1.0 / depth)).astype(jnp.int32)
     rows_out[...] = (slot - group) * depth + inner
-    if shards == GROUPS:
-        group = jnp.where(near == GROUPS - 1, group ^ (lax.axis_index("wa") & (GROUPS - 1)), group)
     following = pltpu.roll(modes, count - 1, 0)
     first = modes - start
     valid = heading & (following >= 0) & (first >= 0) & (first < kept)
@@ -108,16 +106,6 @@
         return chunk
 
     return [quarter(g) for g in range(GROUPS)], depth
-
-
-def piece_quarters(pieces, depth):
-    def quarter(piece):
-        def chunk(t):
-            return piece[:, t * LANES : (t + 1) * LANES], piece[t : t + 1, depth : depth + LANES]
-
-        return chunk
-
-    return [quarter(piece) for piece in pieces], depth
 
 
 def fill_table(source, table, base):
@@ -157,16 +145,12 @@
     own[...] = jnp.concatenate(parts, axis=0).astype(jnp.bfloat16)
 
 
-def extend(slots, pieces, table_in, *refs):
+def extend(slots, table_in, *refs):
     table = refs[-1]
     whole = len(slots)
     for n, slot in enumerate(slots):
         vectors, lines = refs[n], refs[whole + n]
         fill_table(shard_quarters(vectors, lines), table, slot * vectors.shape[1] // GROUPS)
-    if pieces:
-        parts = refs[2 * whole : -1]
-        depth = parts[0].shape[1] - LANES
-        fill_table(piece_quarters(parts, depth), table, (GROUPS - 1) * depth)
 
 
 def held_rows(e, branches):
@@ -509,7 +493,6 @@
     clusters = cells.shape[0]
     offset = local * shards // 2
     both = ("pb", "wa")
-    worker = lax.axis_index("wa")
     lines = freq.reshape(local // LANES, LANES)
 
     def swap(x):
@@ -523,25 +506,12 @@
         return lax.ppermute(x, both, pairs)
 
     depth = local // GROUPS
-    pieces = []
     if shards == GROUPS:
-        which = worker % GROUPS
-        rows = depth // LANES
-        payload = jnp.concatenate(
-            [
-                lax.dynamic_slice_in_dim(eig, which * depth, depth, 1),
-                lax.dynamic_slice_in_dim(lines, which * rows, rows, 0),
-            ],
-            axis=1,
-        )
-        straight = across(payload, shards - 1, shards - 1)
-        one = across(eig, 1, 2)
-        one_lines = across(lines, 1, 2)
-        along = lax.ppermute(straight, "wa", [(i, i ^ 2) for i in range(workers)])
-        pieces = [straight, swap(straight), along]
-        pieces.append(swap(along))
-        vectors = [eig, one, swap(one)]
-        rows_of = [lines, one_lines, swap(one_lines)]
+        vectors, rows_of = [eig], [lines]
+        for owned, kind in ((eig, vectors), (lines, rows_of)):
+            one = across(owned, 1, 2)
+            far = across(one, 2, 1)
+            kind += [one, swap(one), far]
     else:
         vectors, rows_of = [eig], [lines]
         for k in range(1, shards):
@@ -549,7 +519,7 @@
             rows_of.append(across(lines, k, k))
 
     slots = jnp.arange(held, dtype=jnp.int32)[:, None, None]
-    coded = (jnp.where(slots < counts[0], quartets, -1) - offset).astype(jnp.int16)
+    coded = (jnp.where(slots < counts[:, None, None], quartets, -1) - offset).astype(jnp.int16)
     coded = coded.reshape(held * parts, block)
     line_up = [coded]
     for k in range(2, workers, 2):
@@ -590,13 +560,13 @@
     final = len(vectors) - 1
     whole = tuple(range(1, final))
     table = pl.pallas_call(
-        functools.partial(extend, whole, bool(pieces)),
+        functools.partial(extend, whole),
         out_shape=jax.ShapeDtypeStruct(table.shape, table.dtype),
-        in_specs=[vmem] * (1 + 2 * len(whole) + len(pieces)),
+        in_specs=[vmem] * (1 + 2 * len(whole)),
         out_specs=vmem,
         input_output_aliases={0: 0},
         compiler_params=pltpu.CompilerParams(vmem_limit_bytes=16 * 1024 * 1024),
-    )(table, *vectors[1:final], *rows_of[1:final], *pieces)
+    )(table, *vectors[1:final], *rows_of[1:final])
     rates = rates_call(
         branches,
         final * depth,

time: 51 us -> 48.9 us (0.959)
  starting transfers between devices: 19.5 us -> 13.5 us
  waiting for transfers between devices: 8.57 us -> 14.3 us
  local copies, waits for them, and re-layouts: 5.11 us -> 3.46 us
    ppermute x5 -> x3, starting transfers between devices: 10.5 us -> 4.54 us  [swap(): return lax.ppermute(x, 'wa', [(i, i ^ 1) for i in range(workers)])]
    ppermute x3, waiting for transfers between devices: 0.01 us -> 4.56 us  [body(): lax.ppermute(coded, 'wa', [(i, i ^ k) for i in range(workers)])]
    ppermute x1 -> x0, starting transfers between devices: 1.89 us -> none  [body(): along = lax.ppermute(straight, 'wa', [(i, i ^ 2) for i in range(workers)])]
    ppermute x3 -> x4, starting transfers between devices: 3.5 us -> 5.27 us  [across(): return lax.ppermute(x, both, pairs)]
    dynamic_slice x2 -> x0, local copies, waits for them, and re-layouts: 1.65 us -> none  [the longest x1 0.95 us: body(): lax.dynamic_slice_in_dim(eig, which * depth, depth, 1)]
    ppermute x3 -> x4, waiting for transfers between devices: 8.53 us -> 9.76 us  [across(): return lax.ppermute(x, both, pairs)]
  transfers between devices with their start and end apart: 12 -> 10, of which waited for: 2 -> 4; matrix products, arithmetic and copies ran while one was open for 5% -> 2% of each run, Pallas kernels for 5% -> 5%
where the time goes in v3:
time: 48.9 us; the launch traced here: 48.6 us
  Pallas kernels  15.6 us (32%)
  waiting for transfers between devices  14.3 us (29%)
  starting transfers between devices  13.5 us (28%)
  local copies, waits for them, and re-layouts  3.46 us (7%)
  other arithmetic  0.95 us (2%)
  between operations  0.73 us (1%)
    pallas_call x1, Pallas kernels, rates_call(): pl.pallas_call(functools.partial(kernel, branches, base), out_shape=[jax....  13 us
    ppermute x4, waiting for transfers between devices, across(): return lax.ppermute(x, both, pairs)  9.76 us
    ppermute x4, starting transfers between devices, across(): return lax.ppermute(x, both, pairs)  5.27 us
    ppermute x3, waiting for transfers between devices, body(): lax.ppermute(coded, 'wa', [(i, i ^ k) for i in range(workers)])  4.56 us
    ppermute x3, starting transfers between devices, swap(): return lax.ppermute(x, 'wa', [(i, i ^ 1) for i in range(workers)])  4.54 us
    ppermute x3, starting transfers between devices, body(): lax.ppermute(coded, 'wa', [(i, i ^ k) for i in range(workers)])  3.67 us
    unnamed x8, local copies, waits for them, and re-layouts  3.46 us
    pallas_call x1, Pallas kernels, body(): pl.pallas_call(functools.partial(prepare, branches, local, kept, offset),...  1.21 us
  transfers between devices with their start and end apart: 10, of which 4 were waited for; matrix products, arithmetic and copies ran while one was open for 2% of the time, Pallas kernels for 5%

profile of v3, /device:TPU:1, one launch (start us, length us, event | category | flops | bytes accessed | tf_op | source)
XLA Modules:
  0.0 48.6 jit_solution(10032927441250211168)
XLA Ops:
  0.0 2.1 %collective-permute-start.4 = (bf16[24,12288]{1,0:T(8,128)(2,1)}, bf16[24,12288]{1,0:T(8,128)(2,1)S(1)}, u32[]{:S(2)}, u32[]{:S(2)}) collective-permute-start(bf16[24,12288]{1,0:T(8,128)(2,1)} %vectors.1), channel_id=1, source_target_pairs={{0,8},{1,17},{2,10},{3,19},{4,12},{5,21},{6,14},{7,23},{8,0},{9,25... | collective-permute-start | bytes 1769480 | tf_op jit(solution)/shard_map/ppermute | solution.py:506
  2.7 7.1 %collective-permute-done.4.refs_0_ = bf16[24,12288]{1,0:T(8,128)(2,1)S(1)} collective-permute-done((bf16[24,12288]{1,0:T(8,128)(2,1)}, bf16[24,12288]{1,0:T(8,128)(2,1)S(1)}, u32[]{:S(2)}, u32[]{:S(2)}) %collective-permute-start.4) | collective-permute-done | bytes 589856 | tf_op jit(solution)/shard_map/ppermute | solution.py:506
  9.8 1.2 %collective-permute-start.5 = (bf16[24,12288]{1,0:T(8,128)(2,1)S(1)}, bf16[24,12288]{1,0:T(8,128)(2,1)S(1)}, u32[]{:S(2)}, u32[]{:S(2)}) collective-permute-start(bf16[24,12288]{1,0:T(8,128)(2,1)S(1)} %collective-permute-done.4.refs_0_), channel_id=1, source_target_pairs={{0,1},{1,0},{2,3},{3,2},{4,5},{5,4},{6,7},{7,6},{8,9},{9,8},{10,11... | collective-permute-start | bytes 1769480 | tf_op jit(solution)/shard_map/ppermute | solution.py:499
  11.1 1.7 %collective-permute-start.8 = (bf16[24,12288]{1,0:T(8,128)(2,1)S(1)}, bf16[24,12288]{1,0:T(8,128)(2,1)S(1)}, u32[]{:S(2)}, u32[]{:S(2)}) collective-permute-start(bf16[24,12288]{1,0:T(8,128)(2,1)S(1)} %collective-permute-done.4.refs_0_), channel_id=1, source_target_pairs={{0,16},{1,9},{2,18},{3,11},{4,20},{5,13},{6,22},{7,15},{8,24},{9,1... | collective-permute-start | bytes 1769480 | tf_op jit(solution)/shard_map/ppermute | solution.py:506
  12.8 0.9 %add_convert_fusion = s16[32,4,128]{2,1,0:T(4,128)(2,1)S(1)} fusion(s32[32,4,128]{2,1,0:T(4,128)} %param.6, pred[32]{0:T(512)(128)(4,1)S(1)} %iota_compare_fusion), kind=kLoop, calls=%fused_computation.1 | loop fusion | flops 49152 | bytes 98336 | tf_op jit(solution)/shard_map/convert_element_type | solution.py:522
  13.8 1.4 %collective-permute-start = (s16[128,128]{1,0:T(8,128)(2,1)S(1)}, s16[128,128]{1,0:T(8,128)(2,1)S(1)}, u32[]{:S(2)}, u32[]{:S(2)}) collective-permute-start(s16[128,128]{1,0:T(8,128)(2,1)S(1)} %bitcast.11), channel_id=1, source_target_pairs={{0,2},{1,3},{2,0},{3,1},{4,6},{5,7},{6,4},{7,5},{8,10},{9,11},{10,... | collective-permute-start | bytes 98312 | tf_op jit(solution)/shard_map/ppermute | solution.py:526
  15.1 2.3 %collective-permute-start.1 = (s16[128,128]{1,0:T(8,128)(2,1)S(1)}, s16[128,128]{1,0:T(8,128)(2,1)S(1)}, u32[]{:S(2)}, u32[]{:S(2)}) collective-permute-start(s16[128,128]{1,0:T(8,128)(2,1)S(1)} %bitcast.12), channel_id=1, source_target_pairs={{0,4},{1,5},{2,6},{3,7},{4,0},{5,1},{6,2},{7,3},{8,12},{9,13},{10,... | collective-permute-start | bytes 98312 | tf_op jit(solution)/shard_map/ppermute | solution.py:526
  17.4 0.0 collective-permute-start.2
  17.4 0.0 collective-permute-done
  17.4 1.7 %collective-permute-done.1 = s16[128,128]{1,0:T(8,128)(2,1)S(1)} collective-permute-done((s16[128,128]{1,0:T(8,128)(2,1)S(1)}, s16[128,128]{1,0:T(8,128)(2,1)S(1)}, u32[]{:S(2)}, u32[]{:S(2)}) %collective-permute-start.1) | collective-permute-done | bytes 32800 | tf_op jit(solution)/shard_map/ppermute | solution.py:526
  19.1 2.9 %collective-permute-done.2 = s16[128,128]{1,0:T(8,128)(2,1)S(1)} collective-permute-done((s16[128,128]{1,0:T(8,128)(2,1)S(1)}, s16[128,128]{1,0:T(8,128)(2,1)S(1)}, u32[]{:S(2)}, u32[]{:S(2)}) %collective-permute-start.2) | collective-permute-done | bytes 32800 | tf_op jit(solution)/shard_map/ppermute | solution.py:526
  22.0 2.1 %collective-permute-start.3 = (s16[512,128]{1,0:T(8,128)(2,1)S(1)}, s16[512,128]{1,0:T(8,128)(2,1)S(1)}, u32[]{:S(2)}, u32[]{:S(2)}) collective-permute-start(s16[512,128]{1,0:T(8,128)(2,1)S(1)} %pad_add_fusion.refs_0_), channel_id=1, source_target_pairs={{0,1},{1,0},{2,3},{3,2},{4,5},{5,4},{6,7},{7,6},{8,9},{9,8},{10,11... | collective-permute-start | bytes 393224 | tf_op jit(solution)/shard_map/ppermute | solution.py:499
  24.1 0.3 collective-permute-start.6
  24.3 2.6 %collective-permute-done.6.refs_2_ = bf16[96,128]{1,0:T(8,128)(2,1)S(1)} collective-permute-done((bf16[96,128]{1,0:T(8,128)(2,1)}, bf16[96,128]{1,0:T(8,128)(2,1)S(1)}, u32[]{:S(2)}, u32[]{:S(2)}) %collective-permute-start.6) | collective-permute-done | bytes 24608 | tf_op jit(solution)/shard_map/ppermute | solution.py:506
  27.0 1.2 %collective-permute-start.7 = (bf16[96,128]{1,0:T(8,128)(2,1)S(1)}, bf16[96,128]{1,0:T(8,128)(2,1)S(1)}, u32[]{:S(2)}, u32[]{:S(2)}) collective-permute-start(bf16[96,128]{1,0:T(8,128)(2,1)S(1)} %collective-permute-done.6.refs_2_), channel_id=1, source_target_pairs={{0,1},{1,0},{2,3},{3,2},{4,5},{5,4},{6,7},{7,6},{8,9},{9,8},{10,11... | collective-permute-start | bytes 73736 | tf_op jit(solution)/shard_map/ppermute | solution.py:499
  28.2 1.2 %collective-permute-start.9 = (bf16[96,128]{1,0:T(8,128)(2,1)S(1)}, bf16[96,128]{1,0:T(8,128)(2,1)S(1)}, u32[]{:S(2)}, u32[]{:S(2)}) collective-permute-start(bf16[96,128]{1,0:T(8,128)(2,1)S(1)} %collective-permute-done.6.refs_2_), channel_id=1, source_target_pairs={{0,16},{1,9},{2,18},{3,11},{4,20},{5,13},{6,22},{7,15},{8,24},{9,1... | collective-permute-start | bytes 73736 | tf_op jit(solution)/shard_map/ppermute | solution.py:506
  29.4 0.0 copy-start
  29.4 1.1 %copy-done = bf16[24,12288]{1,0:T(8,128)(2,1)S(1)} copy-done((bf16[24,12288]{1,0:T(8,128)(2,1)S(1)}, bf16[24,12288]{1,0:T(8,128)(2,1)}, u32[]{:S(2)}) %copy-start) | copy-done | bytes 589848
  30.5 0.0 copy-start.1
  30.5 1.0 %copy-done.1 = bf16[144,1152]{1,0:T(8,128)(2,1)S(1)} copy-done((bf16[144,1152]{1,0:T(8,128)(2,1)S(1)}, bf16[144,1152]{1,0:T(8,128)(2,1)}, u32[]{:S(2)}) %copy-start.1) | copy-done | bytes 331800
  31.5 0.0 copy-start.2
  31.5 0.7 %copy-done.2 = bf16[12288]{0:T(1024)(128)(2,1)S(1)} copy-done((bf16[12288]{0:T(1024)(128)(2,1)S(1)}, bf16[12288]{0:T(1024)(128)(2,1)}, u32[]{:S(2)}) %copy-start.2) | copy-done | bytes 24600
  32.2 0.0 copy-start.3
  32.2 0.7 %copy-done.3 = s32[8,9]{1,0:T(8,128)S(1)} copy-done((s32[8,9]{1,0:T(8,128)S(1)}, s32[8,9]{1,0:T(8,128)}, u32[]{:S(2)}) %copy-start.3) | copy-done | bytes 312
  32.9 0.5 %shard_map.65 = (f32[12288,128]{1,0:T(8,128)S(1)}, bf16[304,128]{1,0:T(8,128)(2,1)S(1)}, bf16[144,1152]{1,0:T(8,128)(2,1)S(1)}, s32[9,8,128]{2,1,0:T(8,128)S(1)}) custom-call(bf16[24,12288]{1,0:T(8,128)(2,1)S(1)} %copy-done, bf16[96,128]{1,0:T(8,128)(2,1)S(1)} %bitcast.10, bf16[144,1152]{1,0:T(8,128)(2,1)S(1)} %copy-done.1, s32[8,9]{1,0:T(8,128)S(1)} %copy-done.3), custom_call_target="tpu_custom_call" | custom-call | tf_op jit(solution)/shard_map/pallas_call | solution.py:548
  33.4 0.0 collective-permute-done.3.refs_1_
  33.4 1.2 %shard_map.64 = (s32[1024,128]{1,0:T(8,128)S(1)}, s32[1024,128]{1,0:T(8,128)S(1)}, s32[1,384]{1,0:T(1,128)S(1)}) custom-call(s16[512,128]{1,0:T(8,128)(2,1)S(1)} %pad_add_fusion.refs_0_, s16[512,128]{1,0:T(8,128)(2,1)S(1)} %collective-permute-done.3.refs_1_), custom_call_target="tpu_custom_call" | custom-call | tf_op jit(solution)/shard_map/pallas_call | solution.py:534
  34.6 0.0 collective-permute-done.7.refs_3_
  34.6 0.0 collective-permute-done.5.refs_1_
  34.7 0.9 %shard_map.66.table_in = f32[12288,128]{1,0:T(8,128)S(1)} custom-call(f32[12288,128]{1,0:T(8,128)S(1)} %get-tuple-element.16.table_in, bf16[24,12288]{1,0:T(8,128)(2,1)S(1)} %collective-permute-done.4.refs_0_, bf16[24,12288]{1,0:T(8,128)(2,1)S(1)} %collective-permute-done.5.refs_1_, ...), custom_call_target="tpu_custom_call", output_to_operand_aliasing={{}: (0, {})} | custom-call | tf_op jit(solution)/shard_map/pallas_call | solution.py:562
  35.5 0.0 collective-permute-done.9.lines
  35.5 0.0 collective-permute-done.8.vectors
  35.5 13.0 %shard_map.67 = (f32[12,128]{1,0:T(8,128)}, f32[12288,128]{1,0:T(8,128)S(1)}) custom-call(s32[1,384]{1,0:T(1,128)S(1)} %get-tuple-element.13.order, s32[256,4,128]{2,1,0:T(4,128)S(1)} %bitcast.7, s32[256,4,128]{2,1,0:T(4,128)S(1)} %bitcast.8, f32[12288,128]{1,0:T(8,128)S(1)} %shard_map.66.table_in, ...), custom_call_target="tpu_custom_call", output_to_operand_aliasing={{1}: (3, {})} | custom-call | tf_op jit(solution)/shard_map/pallas_call | solution.py:459
  (2 shorter events, 0.0 us)
Async XLA Ops:
  0.0 9.8 %collective-permute-start.4 = (bf16[24,12288]{1,0:T(8,128)(2,1)}, bf16[24,12288]{1,0:T(8,128)(2,1)S(1)}, u32[]{:S(2)}, u32[]{:S(2)}) collective-permute-start(bf16[24,12288]{1,0:T(8,128)(2,1)} %vectors.1), channel_id=1, source_target_pairs={{0,8},{1,17},{2,10},{3,19},{4,12},{5,21},{6,14},{7,23},{8,0},{9,25... | collective-permute-start | bytes 1769480 | tf_op jit(solution)/shard_map/ppermute | solution.py:506
  9.8 24.8 %collective-permute-start.5 = (bf16[24,12288]{1,0:T(8,128)(2,1)S(1)}, bf16[24,12288]{1,0:T(8,128)(2,1)S(1)}, u32[]{:S(2)}, u32[]{:S(2)}) collective-permute-start(bf16[24,12288]{1,0:T(8,128)(2,1)S(1)} %collective-permute-done.4.refs_0_), channel_id=1, source_target_pairs={{0,1},{1,0},{2,3},{3,2},{4,5},{5,4},{6,7},{7,6},{8,9},{9,8},{10,11... | collective-permute-start | bytes 1769480 | tf_op jit(solution)/shard_map/ppermute | solution.py:499
  11.1 24.5 %collective-permute-start.8 = (bf16[24,12288]{1,0:T(8,128)(2,1)S(1)}, bf16[24,12288]{1,0:T(8,128)(2,1)S(1)}, u32[]{:S(2)}, u32[]{:S(2)}) collective-permute-start(bf16[24,12288]{1,0:T(8,128)(2,1)S(1)} %collective-permute-done.4.refs_0_), channel_id=1, source_target_pairs={{0,16},{1,9},{2,18},{3,11},{4,20},{5,13},{6,22},{7,15},{8,24},{9,1... | collective-permute-start | bytes 1769480 | tf_op jit(solution)/shard_map/ppermute | solution.py:506
  13.8 3.7 %collective-permute-start = (s16[128,128]{1,0:T(8,128)(2,1)S(1)}, s16[128,128]{1,0:T(8,128)(2,1)S(1)}, u32[]{:S(2)}, u32[]{:S(2)}) collective-permute-start(s16[128,128]{1,0:T(8,128)(2,1)S(1)} %bitcast.11), channel_id=1, source_target_pairs={{0,2},{1,3},{2,0},{3,1},{4,6},{5,7},{6,4},{7,5},{8,10},{9,11},{10,... | collective-permute-start | bytes 98312 | tf_op jit(solution)/shard_map/ppermute | solution.py:526
  15.1 4.0 %collective-permute-start.1 = (s16[128,128]{1,0:T(8,128)(2,1)S(1)}, s16[128,128]{1,0:T(8,128)(2,1)S(1)}, u32[]{:S(2)}, u32[]{:S(2)}) collective-permute-start(s16[128,128]{1,0:T(8,128)(2,1)S(1)} %bitcast.12), channel_id=1, source_target_pairs={{0,4},{1,5},{2,6},{3,7},{4,0},{5,1},{6,2},{7,3},{8,12},{9,13},{10,... | collective-permute-start | bytes 98312 | tf_op jit(solution)/shard_map/ppermute | solution.py:526
  17.4 4.6 %collective-permute-start.2 = (s16[128,128]{1,0:T(8,128)(2,1)S(1)}, s16[128,128]{1,0:T(8,128)(2,1)S(1)}, u32[]{:S(2)}, u32[]{:S(2)}) collective-permute-start(s16[128,128]{1,0:T(8,128)(2,1)S(1)} %bitcast.13), channel_id=1, source_target_pairs={{0,6},{1,7},{2,4},{3,5},{4,2},{5,3},{6,0},{7,1},{8,14},{9,15},{10,... | collective-permute-start | bytes 98312 | tf_op jit(solution)/shard_map/ppermute | solution.py:526
  22.0 11.4 %collective-permute-start.3 = (s16[512,128]{1,0:T(8,128)(2,1)S(1)}, s16[512,128]{1,0:T(8,128)(2,1)S(1)}, u32[]{:S(2)}, u32[]{:S(2)}) collective-permute-start(s16[512,128]{1,0:T(8,128)(2,1)S(1)} %pad_add_fusion.refs_0_), channel_id=1, source_target_pairs={{0,1},{1,0},{2,3},{3,2},{4,5},{5,4},{6,7},{7,6},{8,9},{9,8},{10,11... | collective-permute-start | bytes 393224 | tf_op jit(solution)/shard_map/ppermute | solution.py:499
  24.1 2.9 %collective-permute-start.6 = (bf16[96,128]{1,0:T(8,128)(2,1)}, bf16[96,128]{1,0:T(8,128)(2,1)S(1)}, u32[]{:S(2)}, u32[]{:S(2)}) collective-permute-start(bf16[96,128]{1,0:T(8,128)(2,1)} %bitcast.9), channel_id=1, source_target_pairs={{0,8},{1,17},{2,10},{3,19},{4,12},{5,21},{6,14},{7,23},{8,0},{9,25... | collective-permute-start | bytes 73736 | tf_op jit(solution)/shard_map/ppermute | solution.py:506
  27.0 7.7 %collective-permute-start.7 = (bf16[96,128]{1,0:T(8,128)(2,1)S(1)}, bf16[96,128]{1,0:T(8,128)(2,1)S(1)}, u32[]{:S(2)}, u32[]{:S(2)}) collective-permute-start(bf16[96,128]{1,0:T(8,128)(2,1)S(1)} %collective-permute-done.6.refs_2_), channel_id=1, source_target_pairs={{0,1},{1,0},{2,3},{3,2},{4,5},{5,4},{6,7},{7,6},{8,9},{9,8},{10,11... | collective-permute-start | bytes 73736 | tf_op jit(solution)/shard_map/ppermute | solution.py:499
  28.2 7.3 %collective-permute-start.9 = (bf16[96,128]{1,0:T(8,128)(2,1)S(1)}, bf16[96,128]{1,0:T(8,128)(2,1)S(1)}, u32[]{:S(2)}, u32[]{:S(2)}) collective-permute-start(bf16[96,128]{1,0:T(8,128)(2,1)S(1)} %collective-permute-done.6.refs_2_), channel_id=1, source_target_pairs={{0,16},{1,9},{2,18},{3,11},{4,20},{5,13},{6,22},{7,15},{8,24},{9,1... | collective-permute-start | bytes 73736 | tf_op jit(solution)/shard_map/ppermute | solution.py:506
  29.4 1.1 %copy-start = (bf16[24,12288]{1,0:T(8,128)(2,1)S(1)}, bf16[24,12288]{1,0:T(8,128)(2,1)}, u32[]{:S(2)}) copy-start(bf16[24,12288]{1,0:T(8,128)(2,1)} %vectors.1) | copy-start | bytes 1769476
  30.5 1.0 %copy-start.1 = (bf16[144,1152]{1,0:T(8,128)(2,1)S(1)}, bf16[144,1152]{1,0:T(8,128)(2,1)}, u32[]{:S(2)}) copy-start(bf16[144,1152]{1,0:T(8,128)(2,1)} %phi_in.1) | copy-start | bytes 995332
  31.5 0.7 %copy-start.2 = (bf16[12288]{0:T(1024)(128)(2,1)S(1)}, bf16[12288]{0:T(1024)(128)(2,1)}, u32[]{:S(2)}) copy-start(bf16[12288]{0:T(1024)(128)(2,1)} %param.9) | copy-start | bytes 73732
  32.2 0.7 %copy-start.3 = (s32[8,9]{1,0:T(8,128)S(1)}, s32[8,9]{1,0:T(8,128)}, u32[]{:S(2)}) copy-start(s32[8,9]{1,0:T(8,128)} %cells_in.1) | copy-start | bytes 868

commit v4 on v3

--- a/solution.py
+++ b/solution.py
@@ -121,13 +121,16 @@
         table[row : row + LANES, :] = jnp.concatenate(stack, axis=0).T
 
 
-def begin(kept, heads, vectors, lines, phi_in, cells_in, table, own, phi, cells):
-    comps = vectors.shape[0]
+def constants(phi_in, cells_in, phi, cells):
     phi[...] = phi_in[...]
     cell = cells_in[...]
     for j in range(cell.shape[1]):
         column = cell[:, j : j + 1]
         cells[j] = jnp.broadcast_to(column if j < 3 else -column, (cell.shape[0], LANES))
+
+
+def begin(kept, heads, vectors, lines, table, own):
+    comps = vectors.shape[0]
     fill_table(shard_quarters(vectors, lines), table, 0)
     start = lax.axis_index("wa") * kept // LANES
     own_lines = lines[...].astype(jnp.float32)
@@ -507,11 +510,12 @@
 
     depth = local // GROUPS
     if shards == GROUPS:
-        vectors, rows_of = [eig], [lines]
-        for owned, kind in ((eig, vectors), (lines, rows_of)):
-            one = across(owned, 1, 2)
-            far = across(one, 2, 1)
-            kind += [one, swap(one), far]
+        one = across(eig, 1, 2)
+        far = across(one, 2, 1)
+        vectors = [eig, one, swap(one), far]
+        one_lines = across(lines, 1, 2)
+        far_lines = across(lines, shards - 1, shards - 1)
+        rows_of = [lines, one_lines, swap(one_lines), far_lines]
     else:
         vectors, rows_of = [eig], [lines]
         for k in range(1, shards):
@@ -545,18 +549,26 @@
     blocks = total_rows // parts
     padded = -(-heads // 16) * 16
     own_rows = -(-heads * (comps + 1) // 16) * 16
-    table, own, phi, spread_cells = pl.pallas_call(
+    phi, spread_cells = pl.pallas_call(
+        constants,
+        out_shape=[
+            jax.ShapeDtypeStruct(phi.shape, phi.dtype),
+            jax.ShapeDtypeStruct((cells.shape[1], clusters, LANES), jnp.int32),
+        ],
+        in_specs=[vmem] * 2,
+        out_specs=[vmem] * 2,
+        compiler_params=pltpu.CompilerParams(vmem_limit_bytes=16 * 1024 * 1024),
+    )(phi, cells)
+    table, own = pl.pallas_call(
         functools.partial(begin, kept, heads),
         out_shape=[
             jax.ShapeDtypeStruct((shards * depth, LANES), jnp.float32),
             jax.ShapeDtypeStruct((own_rows, LANES), jnp.bfloat16),
-            jax.ShapeDtypeStruct(phi.shape, phi.dtype),
-            jax.ShapeDtypeStruct((cells.shape[1], clusters, LANES), jnp.int32),
         ],
-        in_specs=[vmem] * 4,
-        out_specs=[vmem] * 4,
+        in_specs=[vmem] * 2,
+        out_specs=[vmem] * 2,
         compiler_params=pltpu.CompilerParams(vmem_limit_bytes=16 * 1024 * 1024),
-    )(eig, lines, phi, cells)
+    )(eig, lines)
     final = len(vectors) - 1
     whole = tuple(range(1, final))
     table = pl.pallas_call(

time: 48.9 us -> 48.9 us (level)
  no operation moved by 1% of the time
where the time goes in v4:
time: 48.9 us; the launch traced here: 48.5 us
  Pallas kernels  15.6 us (32%)
  waiting for transfers between devices  14.3 us (29%)
  starting transfers between devices  13.4 us (27%)
  local copies, waits for them, and re-layouts  3.46 us (7%)
  other arithmetic  0.95 us (2%)
  between operations  0.73 us (1%)
    pallas_call x1, Pallas kernels, rates_call(): pl.pallas_call(functools.partial(kernel, branches, base), out_shape=[jax....  13 us
    ppermute x4, waiting for transfers between devices, across(): return lax.ppermute(x, both, pairs)  9.76 us
    ppermute x4, starting transfers between devices, across(): return lax.ppermute(x, both, pairs)  5.21 us
    ppermute x3, waiting for transfers between devices, body(): lax.ppermute(coded, 'wa', [(i, i ^ k) for i in range(workers)])  4.56 us
    ppermute x3, starting transfers between devices, swap(): return lax.ppermute(x, 'wa', [(i, i ^ 1) for i in range(workers)])  4.54 us
    ppermute x3, starting transfers between devices, body(): lax.ppermute(coded, 'wa', [(i, i ^ k) for i in range(workers)])  3.67 us
    unnamed x8, local copies, waits for them, and re-layouts  3.46 us
    pallas_call x1, Pallas kernels, body(): pl.pallas_call(functools.partial(prepare, branches, local, kept, offset),...  1.21 us
  transfers between devices with their start and end apart: 10, of which 4 were waited for; matrix products, arithmetic and copies ran while one was open for 2% of the time, Pallas kernels for 5%

profile of v4, /device:TPU:1, one launch (start us, length us, event | category | flops | bytes accessed | tf_op | source)
XLA Modules:
  0.0 48.5 jit_solution(7067457032520409290)
XLA Ops:
  0.0 2.1 %collective-permute-start.4 = (bf16[24,12288]{1,0:T(8,128)(2,1)}, bf16[24,12288]{1,0:T(8,128)(2,1)S(1)}, u32[]{:S(2)}, u32[]{:S(2)}) collective-permute-start(bf16[24,12288]{1,0:T(8,128)(2,1)} %vectors.1), channel_id=1, source_target_pairs={{0,8},{1,17},{2,10},{3,19},{4,12},{5,21},{6,14},{7,23},{8,0},{9,25... | collective-permute-start | bytes 1769480 | tf_op jit(solution)/shard_map/ppermute | solution.py:509
  2.7 7.1 %collective-permute-done.4.refs_0_ = bf16[24,12288]{1,0:T(8,128)(2,1)S(1)} collective-permute-done((bf16[24,12288]{1,0:T(8,128)(2,1)}, bf16[24,12288]{1,0:T(8,128)(2,1)S(1)}, u32[]{:S(2)}, u32[]{:S(2)}) %collective-permute-start.4) | collective-permute-done | bytes 589856 | tf_op jit(solution)/shard_map/ppermute | solution.py:509
  9.8 1.2 %collective-permute-start.5 = (bf16[24,12288]{1,0:T(8,128)(2,1)S(1)}, bf16[24,12288]{1,0:T(8,128)(2,1)S(1)}, u32[]{:S(2)}, u32[]{:S(2)}) collective-permute-start(bf16[24,12288]{1,0:T(8,128)(2,1)S(1)} %collective-permute-done.4.refs_0_), channel_id=1, source_target_pairs={{0,1},{1,0},{2,3},{3,2},{4,5},{5,4},{6,7},{7,6},{8,9},{9,8},{10,11... | collective-permute-start | bytes 1769480 | tf_op jit(solution)/shard_map/ppermute | solution.py:502
  11.1 1.7 %collective-permute-start.8 = (bf16[24,12288]{1,0:T(8,128)(2,1)S(1)}, bf16[24,12288]{1,0:T(8,128)(2,1)S(1)}, u32[]{:S(2)}, u32[]{:S(2)}) collective-permute-start(bf16[24,12288]{1,0:T(8,128)(2,1)S(1)} %collective-permute-done.4.refs_0_), channel_id=1, source_target_pairs={{0,16},{1,9},{2,18},{3,11},{4,20},{5,13},{6,22},{7,15},{8,24},{9,1... | collective-permute-start | bytes 1769480 | tf_op jit(solution)/shard_map/ppermute | solution.py:509
  12.8 0.9 %add_convert_fusion = s16[32,4,128]{2,1,0:T(4,128)(2,1)S(1)} fusion(s32[32,4,128]{2,1,0:T(4,128)} %param.6, pred[32]{0:T(512)(128)(4,1)S(1)} %iota_compare_fusion), kind=kLoop, calls=%fused_computation.1 | loop fusion | flops 49152 | bytes 98336 | tf_op jit(solution)/shard_map/convert_element_type | solution.py:526
  13.8 1.4 %collective-permute-start = (s16[128,128]{1,0:T(8,128)(2,1)S(1)}, s16[128,128]{1,0:T(8,128)(2,1)S(1)}, u32[]{:S(2)}, u32[]{:S(2)}) collective-permute-start(s16[128,128]{1,0:T(8,128)(2,1)S(1)} %bitcast.12), channel_id=1, source_target_pairs={{0,2},{1,3},{2,0},{3,1},{4,6},{5,7},{6,4},{7,5},{8,10},{9,11},{10,... | collective-permute-start | bytes 98312 | tf_op jit(solution)/shard_map/ppermute | solution.py:530
  15.1 2.3 %collective-permute-start.1 = (s16[128,128]{1,0:T(8,128)(2,1)S(1)}, s16[128,128]{1,0:T(8,128)(2,1)S(1)}, u32[]{:S(2)}, u32[]{:S(2)}) collective-permute-start(s16[128,128]{1,0:T(8,128)(2,1)S(1)} %bitcast.13), channel_id=1, source_target_pairs={{0,4},{1,5},{2,6},{3,7},{4,0},{5,1},{6,2},{7,3},{8,12},{9,13},{10,... | collective-permute-start | bytes 98312 | tf_op jit(solution)/shard_map/ppermute | solution.py:530
  17.4 0.0 collective-permute-start.2
  17.4 0.0 collective-permute-done
  17.4 1.7 %collective-permute-done.1 = s16[128,128]{1,0:T(8,128)(2,1)S(1)} collective-permute-done((s16[128,128]{1,0:T(8,128)(2,1)S(1)}, s16[128,128]{1,0:T(8,128)(2,1)S(1)}, u32[]{:S(2)}, u32[]{:S(2)}) %collective-permute-start.1) | collective-permute-done | bytes 32800 | tf_op jit(solution)/shard_map/ppermute | solution.py:530
  19.1 2.9 %collective-permute-done.2 = s16[128,128]{1,0:T(8,128)(2,1)S(1)} collective-permute-done((s16[128,128]{1,0:T(8,128)(2,1)S(1)}, s16[128,128]{1,0:T(8,128)(2,1)S(1)}, u32[]{:S(2)}, u32[]{:S(2)}) %collective-permute-start.2) | collective-permute-done | bytes 32800 | tf_op jit(solution)/shard_map/ppermute | solution.py:530
  22.0 2.1 %collective-permute-start.3 = (s16[512,128]{1,0:T(8,128)(2,1)S(1)}, s16[512,128]{1,0:T(8,128)(2,1)S(1)}, u32[]{:S(2)}, u32[]{:S(2)}) collective-permute-start(s16[512,128]{1,0:T(8,128)(2,1)S(1)} %pad_add_fusion.refs_0_), channel_id=1, source_target_pairs={{0,1},{1,0},{2,3},{3,2},{4,5},{5,4},{6,7},{7,6},{8,9},{9,8},{10,11... | collective-permute-start | bytes 393224 | tf_op jit(solution)/shard_map/ppermute | solution.py:502
  24.1 0.3 collective-permute-start.6
  24.3 2.6 %collective-permute-done.6.refs_2_ = bf16[96,128]{1,0:T(8,128)(2,1)S(1)} collective-permute-done((bf16[96,128]{1,0:T(8,128)(2,1)}, bf16[96,128]{1,0:T(8,128)(2,1)S(1)}, u32[]{:S(2)}, u32[]{:S(2)}) %collective-permute-start.6) | collective-permute-done | bytes 24608 | tf_op jit(solution)/shard_map/ppermute | solution.py:509
  27.0 1.2 %collective-permute-start.7 = (bf16[96,128]{1,0:T(8,128)(2,1)S(1)}, bf16[96,128]{1,0:T(8,128)(2,1)S(1)}, u32[]{:S(2)}, u32[]{:S(2)}) collective-permute-start(bf16[96,128]{1,0:T(8,128)(2,1)S(1)} %collective-permute-done.6.refs_2_), channel_id=1, source_target_pairs={{0,1},{1,0},{2,3},{3,2},{4,5},{5,4},{6,7},{7,6},{8,9},{9,8},{10,11... | collective-permute-start | bytes 73736 | tf_op jit(solution)/shard_map/ppermute | solution.py:502
  28.2 1.2 %collective-permute-start.9 = (bf16[96,128]{1,0:T(8,128)(2,1)}, bf16[96,128]{1,0:T(8,128)(2,1)S(1)}, u32[]{:S(2)}, u32[]{:S(2)}) collective-permute-start(bf16[96,128]{1,0:T(8,128)(2,1)} %bitcast.10), channel_id=1, source_target_pairs={{0,24},{1,25},{2,26},{3,27},{4,28},{5,29},{6,30},{7,31},{8,16},{9,... | collective-permute-start | bytes 73736 | tf_op jit(solution)/shard_map/ppermute | solution.py:509
  29.4 0.0 copy-start
  29.4 1.1 %copy-done = bf16[24,12288]{1,0:T(8,128)(2,1)S(1)} copy-done((bf16[24,12288]{1,0:T(8,128)(2,1)S(1)}, bf16[24,12288]{1,0:T(8,128)(2,1)}, u32[]{:S(2)}) %copy-start) | copy-done | bytes 589848
  30.4 0.0 copy-start.2
  30.4 0.7 %copy-done.2 = bf16[12288]{0:T(1024)(128)(2,1)S(1)} copy-done((bf16[12288]{0:T(1024)(128)(2,1)S(1)}, bf16[12288]{0:T(1024)(128)(2,1)}, u32[]{:S(2)}) %copy-start.2) | copy-done | bytes 24600
  31.2 0.5 shard_map.65
  31.6 0.0 copy-start.1
  31.6 1.0 %copy-done.1 = bf16[144,1152]{1,0:T(8,128)(2,1)S(1)} copy-done((bf16[144,1152]{1,0:T(8,128)(2,1)S(1)}, bf16[144,1152]{1,0:T(8,128)(2,1)}, u32[]{:S(2)}) %copy-start.1) | copy-done | bytes 331800
  32.6 0.0 copy-start.3
  32.6 0.7 %copy-done.3 = s32[8,9]{1,0:T(8,128)S(1)} copy-done((s32[8,9]{1,0:T(8,128)S(1)}, s32[8,9]{1,0:T(8,128)}, u32[]{:S(2)}) %copy-start.3) | copy-done | bytes 312
  33.3 0.1 shard_map.67
  33.4 0.0 collective-permute-done.3.refs_1_
  33.4 1.2 %shard_map.64 = (s32[1024,128]{1,0:T(8,128)S(1)}, s32[1024,128]{1,0:T(8,128)S(1)}, s32[1,384]{1,0:T(1,128)S(1)}) custom-call(s16[512,128]{1,0:T(8,128)(2,1)S(1)} %pad_add_fusion.refs_0_, s16[512,128]{1,0:T(8,128)(2,1)S(1)} %collective-permute-done.3.refs_1_), custom_call_target="tpu_custom_call" | custom-call | tf_op jit(solution)/shard_map/pallas_call | solution.py:538
  34.6 0.0 collective-permute-done.7.refs_3_
  34.6 0.0 collective-permute-done.5.refs_1_
  34.6 0.9 %shard_map.66.table_in = f32[12288,128]{1,0:T(8,128)S(1)} custom-call(f32[12288,128]{1,0:T(8,128)S(1)} %get-tuple-element.16.table_in, bf16[24,12288]{1,0:T(8,128)(2,1)S(1)} %collective-permute-done.4.refs_0_, bf16[24,12288]{1,0:T(8,128)(2,1)S(1)} %collective-permute-done.5.refs_1_, ...), custom_call_target="tpu_custom_call", output_to_operand_aliasing={{}: (0, {})} | custom-call | tf_op jit(solution)/shard_map/pallas_call | solution.py:574
  35.5 0.0 collective-permute-done.9.lines
  35.5 0.0 collective-permute-done.8.vectors
  35.5 13.0 %shard_map.68 = (f32[12,128]{1,0:T(8,128)}, f32[12288,128]{1,0:T(8,128)S(1)}) custom-call(s32[1,384]{1,0:T(1,128)S(1)} %get-tuple-element.13.order, s32[256,4,128]{2,1,0:T(4,128)S(1)} %bitcast.7, s32[256,4,128]{2,1,0:T(4,128)S(1)} %bitcast.8, f32[12288,128]{1,0:T(8,128)S(1)} %shard_map.66.table_in, ...), custom_call_target="tpu_custom_call", output_to_operand_aliasing={{1}: (3, {})} | custom-call | tf_op jit(solution)/shard_map/pallas_call | solution.py:462
  (2 shorter events, 0.0 us)
Async XLA Ops:
  0.0 9.8 %collective-permute-start.4 = (bf16[24,12288]{1,0:T(8,128)(2,1)}, bf16[24,12288]{1,0:T(8,128)(2,1)S(1)}, u32[]{:S(2)}, u32[]{:S(2)}) collective-permute-start(bf16[24,12288]{1,0:T(8,128)(2,1)} %vectors.1), channel_id=1, source_target_pairs={{0,8},{1,17},{2,10},{3,19},{4,12},{5,21},{6,14},{7,23},{8,0},{9,25... | collective-permute-start | bytes 1769480 | tf_op jit(solution)/shard_map/ppermute | solution.py:509
  9.8 24.8 %collective-permute-start.5 = (bf16[24,12288]{1,0:T(8,128)(2,1)S(1)}, bf16[24,12288]{1,0:T(8,128)(2,1)S(1)}, u32[]{:S(2)}, u32[]{:S(2)}) collective-permute-start(bf16[24,12288]{1,0:T(8,128)(2,1)S(1)} %collective-permute-done.4.refs_0_), channel_id=1, source_target_pairs={{0,1},{1,0},{2,3},{3,2},{4,5},{5,4},{6,7},{7,6},{8,9},{9,8},{10,11... | collective-permute-start | bytes 1769480 | tf_op jit(solution)/shard_map/ppermute | solution.py:502
  11.1 24.5 %collective-permute-start.8 = (bf16[24,12288]{1,0:T(8,128)(2,1)S(1)}, bf16[24,12288]{1,0:T(8,128)(2,1)S(1)}, u32[]{:S(2)}, u32[]{:S(2)}) collective-permute-start(bf16[24,12288]{1,0:T(8,128)(2,1)S(1)} %collective-permute-done.4.refs_0_), channel_id=1, source_target_pairs={{0,16},{1,9},{2,18},{3,11},{4,20},{5,13},{6,22},{7,15},{8,24},{9,1... | collective-permute-start | bytes 1769480 | tf_op jit(solution)/shard_map/ppermute | solution.py:509
  13.8 3.7 %collective-permute-start = (s16[128,128]{1,0:T(8,128)(2,1)S(1)}, s16[128,128]{1,0:T(8,128)(2,1)S(1)}, u32[]{:S(2)}, u32[]{:S(2)}) collective-permute-start(s16[128,128]{1,0:T(8,128)(2,1)S(1)} %bitcast.12), channel_id=1, source_target_pairs={{0,2},{1,3},{2,0},{3,1},{4,6},{5,7},{6,4},{7,5},{8,10},{9,11},{10,... | collective-permute-start | bytes 98312 | tf_op jit(solution)/shard_map/ppermute | solution.py:530
  15.1 4.0 %collective-permute-start.1 = (s16[128,128]{1,0:T(8,128)(2,1)S(1)}, s16[128,128]{1,0:T(8,128)(2,1)S(1)}, u32[]{:S(2)}, u32[]{:S(2)}) collective-permute-start(s16[128,128]{1,0:T(8,128)(2,1)S(1)} %bitcast.13), channel_id=1, source_target_pairs={{0,4},{1,5},{2,6},{3,7},{4,0},{5,1},{6,2},{7,3},{8,12},{9,13},{10,... | collective-permute-start | bytes 98312 | tf_op jit(solution)/shard_map/ppermute | solution.py:530
  17.4 4.6 %collective-permute-start.2 = (s16[128,128]{1,0:T(8,128)(2,1)S(1)}, s16[128,128]{1,0:T(8,128)(2,1)S(1)}, u32[]{:S(2)}, u32[]{:S(2)}) collective-permute-start(s16[128,128]{1,0:T(8,128)(2,1)S(1)} %bitcast.14), channel_id=1, source_target_pairs={{0,6},{1,7},{2,4},{3,5},{4,2},{5,3},{6,0},{7,1},{8,14},{9,15},{10,... | collective-permute-start | bytes 98312 | tf_op jit(solution)/shard_map/ppermute | solution.py:530
  22.0 11.4 %collective-permute-start.3 = (s16[512,128]{1,0:T(8,128)(2,1)S(1)}, s16[512,128]{1,0:T(8,128)(2,1)S(1)}, u32[]{:S(2)}, u32[]{:S(2)}) collective-permute-start(s16[512,128]{1,0:T(8,128)(2,1)S(1)} %pad_add_fusion.refs_0_), channel_id=1, source_target_pairs={{0,1},{1,0},{2,3},{3,2},{4,5},{5,4},{6,7},{7,6},{8,9},{9,8},{10,11... | collective-permute-start | bytes 393224 | tf_op jit(solution)/shard_map/ppermute | solution.py:502
  24.1 2.9 %collective-permute-start.6 = (bf16[96,128]{1,0:T(8,128)(2,1)}, bf16[96,128]{1,0:T(8,128)(2,1)S(1)}, u32[]{:S(2)}, u32[]{:S(2)}) collective-permute-start(bf16[96,128]{1,0:T(8,128)(2,1)} %bitcast.9), channel_id=1, source_target_pairs={{0,8},{1,17},{2,10},{3,19},{4,12},{5,21},{6,14},{7,23},{8,0},{9,25... | collective-permute-start | bytes 73736 | tf_op jit(solution)/shard_map/ppermute | solution.py:509
  27.0 7.6 %collective-permute-start.7 = (bf16[96,128]{1,0:T(8,128)(2,1)S(1)}, bf16[96,128]{1,0:T(8,128)(2,1)S(1)}, u32[]{:S(2)}, u32[]{:S(2)}) collective-permute-start(bf16[96,128]{1,0:T(8,128)(2,1)S(1)} %collective-permute-done.6.refs_2_), channel_id=1, source_target_pairs={{0,1},{1,0},{2,3},{3,2},{4,5},{5,4},{6,7},{7,6},{8,9},{9,8},{10,11... | collective-permute-start | bytes 73736 | tf_op jit(solution)/shard_map/ppermute | solution.py:502
  28.2 7.3 %collective-permute-start.9 = (bf16[96,128]{1,0:T(8,128)(2,1)}, bf16[96,128]{1,0:T(8,128)(2,1)S(1)}, u32[]{:S(2)}, u32[]{:S(2)}) collective-permute-start(bf16[96,128]{1,0:T(8,128)(2,1)} %bitcast.10), channel_id=1, source_target_pairs={{0,24},{1,25},{2,26},{3,27},{4,28},{5,29},{6,30},{7,31},{8,16},{9,... | collective-permute-start | bytes 73736 | tf_op jit(solution)/shard_map/ppermute | solution.py:509
  29.4 1.1 %copy-start = (bf16[24,12288]{1,0:T(8,128)(2,1)S(1)}, bf16[24,12288]{1,0:T(8,128)(2,1)}, u32[]{:S(2)}) copy-start(bf16[24,12288]{1,0:T(8,128)(2,1)} %vectors.1) | copy-start | bytes 1769476
  30.4 0.7 %copy-start.2 = (bf16[12288]{0:T(1024)(128)(2,1)S(1)}, bf16[12288]{0:T(1024)(128)(2,1)}, u32[]{:S(2)}) copy-start(bf16[12288]{0:T(1024)(128)(2,1)} %param.9) | copy-start | bytes 73732
  31.6 1.0 %copy-start.1 = (bf16[144,1152]{1,0:T(8,128)(2,1)S(1)}, bf16[144,1152]{1,0:T(8,128)(2,1)}, u32[]{:S(2)}) copy-start(bf16[144,1152]{1,0:T(8,128)(2,1)} %phi_in.1) | copy-start | bytes 995332
  32.6 0.7 %copy-start.3 = (s32[8,9]{1,0:T(8,128)S(1)}, s32[8,9]{1,0:T(8,128)}, u32[]{:S(2)}) copy-start(s32[8,9]{1,0:T(8,128)} %cells_in.1) | copy-start | bytes 868

commit v5 on v4

--- a/solution.py
+++ b/solution.py
@@ -378,9 +378,6 @@
                 while done[t] * total_steps < step * n:
                     next(track, None)
                     done[t] += 1
-        for track, _ in tracks:
-            for _ in track:
-                pass
 
     gather_steps = 3 * LANES
     choose_steps = 20 + groups + heads
@@ -388,6 +385,11 @@
     turn_steps = clusters * groups // 2
     finish_steps = groups + 3
 
+    def drain(*tracks):
+        for track in tracks:
+            for _ in track:
+                pass
+
     pieces = [(at, min(at + DEPTH, clusters * pairs)) for at in range(0, clusters * pairs, DEPTH)]
 
     def multiply(wide_in, held):
@@ -396,26 +398,43 @@
             held[:] = [part if not held else held[0] + part]
             yield
 
-    def step(i, p):
-        load(i + 3, 1 - p).start()
-        load(i + 2, p).wait()
-        sums = lax.dot_general(
+    def scatter():
+        return lax.dot_general(
             placed[...],
             one_hot(place[0:1, :]),
             (((1,), (1,)), ((), ())),
             preferred_element_type=jnp.float32,
         )
-        weighted = []
-        run(
-            (choose(i + 1, gathered[1 - p], pair[1 - p], single[1 - p]), choose_steps),
-            (multiply(wide[1 - p], weighted), len(pieces)),
-            (turn(pair[p], single[p], wide[p]), turn_steps),
-            (join(single[p], product[p]), join_steps),
-            (gather(p), gather_steps),
-        )
-        run((finish(i - 1, weighted[0], product[1 - p]), finish_steps))
+
+    def add(sums):
         size = acc.shape[0]
         acc[...] += sums[:size] + sums[size : 2 * size] + sums[2 * size :]
+
+    def step(i, p):
+        load(i + 3, 1 - p).start()
+        load(i + 2, p).wait()
+        sums = scatter()
+        weighted = []
+        chosen = choose(i + 1, gathered[1 - p], pair[1 - p], single[1 - p])
+        product_of = multiply(wide[1 - p], weighted)
+        turned = turn(pair[p], single[p], wide[p])
+        joined = join(single[p], product[p])
+        rows = gather(p)
+        run((product_of, len(pieces)), (turned, turn_steps), (rows, 240))
+        drain(product_of)
+        done = finish(i - 1, weighted[0], product[1 - p])
+        run((chosen, choose_steps), (joined, join_steps), (done, finish_steps), (rows, gather_steps - 240))
+        drain(chosen, turned, joined, rows, done)
+        add(sums)
+
+    def last_terms(p):
+        sums = scatter()
+        weighted = []
+        drain(multiply(wide[1 - p], weighted))
+        drain(finish(count - 1, weighted[0], product[1 - p]))
+        add(sums)
+        add(scatter())
+        load(0, p).wait()
 
     load(0, 0).start()
     load(1, 1).start()
@@ -424,30 +443,32 @@
     place[...] = jnp.zeros_like(place)
     fill_table(shard_quarters(vectors, lines), table, base)
     load(0, 0).wait()
-    run((gather(0), gather_steps))
+    drain(gather(0))
     load(2, 0).start()
     load(1, 1).wait()
-    run((choose(0, gathered_a, pair_a, single_a), choose_steps), (gather(1), gather_steps))
+    first, second = choose(0, gathered_a, pair_a, single_a), gather(1)
+    run((first, choose_steps), (second, gather_steps))
+    drain(first, second)
 
     def two_steps(j, carry):
         step(2 * j, 0)
 
-        @pl.when(2 * j + 1 < count + 2)
+        @pl.when(2 * j + 1 < count)
         def _():
             step(2 * j + 1, 1)
 
         return carry
 
-    lax.fori_loop(0, lax.div(count + 3, 2), two_steps, 0)
+    lax.fori_loop(0, lax.div(count + 1, 2), two_steps, 0)
     even = lax.rem(count, 2) == 0
 
     @pl.when(even)
     def _():
-        load(0, 0).wait()
+        last_terms(0)
 
     @pl.when(jnp.logical_not(even))
     def _():
-        load(0, 1).wait()
+        last_terms(1)
 
     out[...] = acc[:heads, :]
 

time: 48.9 us -> 48.1 us (0.984)
  Pallas kernels: 15.6 us -> 14.9 us
    pallas_call x1, Pallas kernels: 13 us -> 12.3 us  [rates_call(): pl.pallas_call(functools.partial(kernel, branches, base), out_shape=[jax....]
where the time goes in v5:
time: 48.1 us; the launch traced here: 47.8 us
  Pallas kernels  14.9 us (31%)
  waiting for transfers between devices  14.3 us (30%)
  starting transfers between devices  13.4 us (28%)
  local copies, waits for them, and re-layouts  3.46 us (7%)
  other arithmetic  0.95 us (2%)
  between operations  0.73 us (2%)
    pallas_call x1, Pallas kernels, rates_call(): pl.pallas_call(functools.partial(kernel, branches, base), out_shape=[jax....  12.3 us
    ppermute x4, waiting for transfers between devices, across(): return lax.ppermute(x, both, pairs)  9.76 us
    ppermute x4, starting transfers between devices, across(): return lax.ppermute(x, both, pairs)  5.21 us
    ppermute x3, waiting for transfers between devices, body(): lax.ppermute(coded, 'wa', [(i, i ^ k) for i in range(workers)])  4.56 us
    ppermute x3, starting transfers between devices, swap(): return lax.ppermute(x, 'wa', [(i, i ^ 1) for i in range(workers)])  4.54 us
    ppermute x3, starting transfers between devices, body(): lax.ppermute(coded, 'wa', [(i, i ^ k) for i in range(workers)])  3.67 us
    unnamed x8, local copies, waits for them, and re-layouts  3.46 us
    pallas_call x1, Pallas kernels, body(): pl.pallas_call(functools.partial(prepare, branches, local, kept, offset),...  1.21 us
  transfers between devices with their start and end apart: 10, of which 4 were waited for; matrix products, arithmetic and copies ran while one was open for 2% of the time, Pallas kernels for 5%

profile of v5, /device:TPU:1, one launch (start us, length us, event | category | flops | bytes accessed | tf_op | source)
XLA Modules:
  0.0 47.8 jit_solution(7863252119119575318)
XLA Ops:
  0.0 2.1 %collective-permute-start.4 = (bf16[24,12288]{1,0:T(8,128)(2,1)}, bf16[24,12288]{1,0:T(8,128)(2,1)S(1)}, u32[]{:S(2)}, u32[]{:S(2)}) collective-permute-start(bf16[24,12288]{1,0:T(8,128)(2,1)} %vectors.1), channel_id=1, source_target_pairs={{0,8},{1,17},{2,10},{3,19},{4,12},{5,21},{6,14},{7,23},{8,0},{9,25... | collective-permute-start | bytes 1769480 | tf_op jit(solution)/shard_map/ppermute | solution.py:530
  2.7 7.1 %collective-permute-done.4.refs_0_ = bf16[24,12288]{1,0:T(8,128)(2,1)S(1)} collective-permute-done((bf16[24,12288]{1,0:T(8,128)(2,1)}, bf16[24,12288]{1,0:T(8,128)(2,1)S(1)}, u32[]{:S(2)}, u32[]{:S(2)}) %collective-permute-start.4) | collective-permute-done | bytes 589856 | tf_op jit(solution)/shard_map/ppermute | solution.py:530
  9.8 1.2 %collective-permute-start.5 = (bf16[24,12288]{1,0:T(8,128)(2,1)S(1)}, bf16[24,12288]{1,0:T(8,128)(2,1)S(1)}, u32[]{:S(2)}, u32[]{:S(2)}) collective-permute-start(bf16[24,12288]{1,0:T(8,128)(2,1)S(1)} %collective-permute-done.4.refs_0_), channel_id=1, source_target_pairs={{0,1},{1,0},{2,3},{3,2},{4,5},{5,4},{6,7},{7,6},{8,9},{9,8},{10,11... | collective-permute-start | bytes 1769480 | tf_op jit(solution)/shard_map/ppermute | solution.py:523
  11.1 1.7 %collective-permute-start.8 = (bf16[24,12288]{1,0:T(8,128)(2,1)S(1)}, bf16[24,12288]{1,0:T(8,128)(2,1)S(1)}, u32[]{:S(2)}, u32[]{:S(2)}) collective-permute-start(bf16[24,12288]{1,0:T(8,128)(2,1)S(1)} %collective-permute-done.4.refs_0_), channel_id=1, source_target_pairs={{0,16},{1,9},{2,18},{3,11},{4,20},{5,13},{6,22},{7,15},{8,24},{9,1... | collective-permute-start | bytes 1769480 | tf_op jit(solution)/shard_map/ppermute | solution.py:530
  12.8 0.9 %add_convert_fusion = s16[32,4,128]{2,1,0:T(4,128)(2,1)S(1)} fusion(s32[32,4,128]{2,1,0:T(4,128)} %param.6, pred[32]{0:T(512)(128)(4,1)S(1)} %iota_compare_fusion), kind=kLoop, calls=%fused_computation.1 | loop fusion | flops 49152 | bytes 98336 | tf_op jit(solution)/shard_map/convert_element_type | solution.py:547
  13.8 1.4 %collective-permute-start = (s16[128,128]{1,0:T(8,128)(2,1)S(1)}, s16[128,128]{1,0:T(8,128)(2,1)S(1)}, u32[]{:S(2)}, u32[]{:S(2)}) collective-permute-start(s16[128,128]{1,0:T(8,128)(2,1)S(1)} %bitcast.12), channel_id=1, source_target_pairs={{0,2},{1,3},{2,0},{3,1},{4,6},{5,7},{6,4},{7,5},{8,10},{9,11},{10,... | collective-permute-start | bytes 98312 | tf_op jit(solution)/shard_map/ppermute | solution.py:551
  15.1 2.3 %collective-permute-start.1 = (s16[128,128]{1,0:T(8,128)(2,1)S(1)}, s16[128,128]{1,0:T(8,128)(2,1)S(1)}, u32[]{:S(2)}, u32[]{:S(2)}) collective-permute-start(s16[128,128]{1,0:T(8,128)(2,1)S(1)} %bitcast.13), channel_id=1, source_target_pairs={{0,4},{1,5},{2,6},{3,7},{4,0},{5,1},{6,2},{7,3},{8,12},{9,13},{10,... | collective-permute-start | bytes 98312 | tf_op jit(solution)/shard_map/ppermute | solution.py:551
  17.4 0.0 collective-permute-start.2
  17.4 0.0 collective-permute-done
  17.4 1.7 %collective-permute-done.1 = s16[128,128]{1,0:T(8,128)(2,1)S(1)} collective-permute-done((s16[128,128]{1,0:T(8,128)(2,1)S(1)}, s16[128,128]{1,0:T(8,128)(2,1)S(1)}, u32[]{:S(2)}, u32[]{:S(2)}) %collective-permute-start.1) | collective-permute-done | bytes 32800 | tf_op jit(solution)/shard_map/ppermute | solution.py:551
  19.1 2.9 %collective-permute-done.2 = s16[128,128]{1,0:T(8,128)(2,1)S(1)} collective-permute-done((s16[128,128]{1,0:T(8,128)(2,1)S(1)}, s16[128,128]{1,0:T(8,128)(2,1)S(1)}, u32[]{:S(2)}, u32[]{:S(2)}) %collective-permute-start.2) | collective-permute-done | bytes 32800 | tf_op jit(solution)/shard_map/ppermute | solution.py:551
  22.0 2.1 %collective-permute-start.3 = (s16[512,128]{1,0:T(8,128)(2,1)S(1)}, s16[512,128]{1,0:T(8,128)(2,1)S(1)}, u32[]{:S(2)}, u32[]{:S(2)}) collective-permute-start(s16[512,128]{1,0:T(8,128)(2,1)S(1)} %pad_add_fusion.refs_0_), channel_id=1, source_target_pairs={{0,1},{1,0},{2,3},{3,2},{4,5},{5,4},{6,7},{7,6},{8,9},{9,8},{10,11... | collective-permute-start | bytes 393224 | tf_op jit(solution)/shard_map/ppermute | solution.py:523
  24.1 0.3 collective-permute-start.6
  24.3 2.6 %collective-permute-done.6.refs_2_ = bf16[96,128]{1,0:T(8,128)(2,1)S(1)} collective-permute-done((bf16[96,128]{1,0:T(8,128)(2,1)}, bf16[96,128]{1,0:T(8,128)(2,1)S(1)}, u32[]{:S(2)}, u32[]{:S(2)}) %collective-permute-start.6) | collective-permute-done | bytes 24608 | tf_op jit(solution)/shard_map/ppermute | solution.py:530
  27.0 1.2 %collective-permute-start.7 = (bf16[96,128]{1,0:T(8,128)(2,1)S(1)}, bf16[96,128]{1,0:T(8,128)(2,1)S(1)}, u32[]{:S(2)}, u32[]{:S(2)}) collective-permute-start(bf16[96,128]{1,0:T(8,128)(2,1)S(1)} %collective-permute-done.6.refs_2_), channel_id=1, source_target_pairs={{0,1},{1,0},{2,3},{3,2},{4,5},{5,4},{6,7},{7,6},{8,9},{9,8},{10,11... | collective-permute-start | bytes 73736 | tf_op jit(solution)/shard_map/ppermute | solution.py:523
  28.2 1.2 %collective-permute-start.9 = (bf16[96,128]{1,0:T(8,128)(2,1)}, bf16[96,128]{1,0:T(8,128)(2,1)S(1)}, u32[]{:S(2)}, u32[]{:S(2)}) collective-permute-start(bf16[96,128]{1,0:T(8,128)(2,1)} %bitcast.10), channel_id=1, source_target_pairs={{0,24},{1,25},{2,26},{3,27},{4,28},{5,29},{6,30},{7,31},{8,16},{9,... | collective-permute-start | bytes 73736 | tf_op jit(solution)/shard_map/ppermute | solution.py:530
  29.4 0.0 copy-start
  29.4 1.1 %copy-done = bf16[24,12288]{1,0:T(8,128)(2,1)S(1)} copy-done((bf16[24,12288]{1,0:T(8,128)(2,1)S(1)}, bf16[24,12288]{1,0:T(8,128)(2,1)}, u32[]{:S(2)}) %copy-start) | copy-done | bytes 589848
  30.4 0.0 copy-start.2
  30.4 0.7 %copy-done.2 = bf16[12288]{0:T(1024)(128)(2,1)S(1)} copy-done((bf16[12288]{0:T(1024)(128)(2,1)S(1)}, bf16[12288]{0:T(1024)(128)(2,1)}, u32[]{:S(2)}) %copy-start.2) | copy-done | bytes 24600
  31.2 0.5 shard_map.65
  31.6 0.0 copy-start.1
  31.6 1.0 %copy-done.1 = bf16[144,1152]{1,0:T(8,128)(2,1)S(1)} copy-done((bf16[144,1152]{1,0:T(8,128)(2,1)S(1)}, bf16[144,1152]{1,0:T(8,128)(2,1)}, u32[]{:S(2)}) %copy-start.1) | copy-done | bytes 331800
  32.6 0.0 copy-start.3
  32.6 0.7 %copy-done.3 = s32[8,9]{1,0:T(8,128)S(1)} copy-done((s32[8,9]{1,0:T(8,128)S(1)}, s32[8,9]{1,0:T(8,128)}, u32[]{:S(2)}) %copy-start.3) | copy-done | bytes 312
  33.3 0.1 shard_map.67
  33.4 0.0 collective-permute-done.3.refs_1_
  33.4 1.2 %shard_map.64 = (s32[1024,128]{1,0:T(8,128)S(1)}, s32[1024,128]{1,0:T(8,128)S(1)}, s32[1,384]{1,0:T(1,128)S(1)}) custom-call(s16[512,128]{1,0:T(8,128)(2,1)S(1)} %pad_add_fusion.refs_0_, s16[512,128]{1,0:T(8,128)(2,1)S(1)} %collective-permute-done.3.refs_1_), custom_call_target="tpu_custom_call" | custom-call | tf_op jit(solution)/shard_map/pallas_call | solution.py:559
  34.6 0.0 collective-permute-done.7.refs_3_
  34.6 0.0 collective-permute-done.5.refs_1_
  34.6 0.9 %shard_map.66.table_in = f32[12288,128]{1,0:T(8,128)S(1)} custom-call(f32[12288,128]{1,0:T(8,128)S(1)} %get-tuple-element.16.table_in, bf16[24,12288]{1,0:T(8,128)(2,1)S(1)} %collective-permute-done.4.refs_0_, bf16[24,12288]{1,0:T(8,128)(2,1)S(1)} %collective-permute-done.5.refs_1_, ...), custom_call_target="tpu_custom_call", output_to_operand_aliasing={{}: (0, {})} | custom-call | tf_op jit(solution)/shard_map/pallas_call | solution.py:595
  35.5 0.0 collective-permute-done.9.lines
  35.5 0.0 collective-permute-done.8.vectors
  35.5 12.3 %shard_map.68 = (f32[12,128]{1,0:T(8,128)}, f32[12288,128]{1,0:T(8,128)S(1)}) custom-call(s32[1,384]{1,0:T(1,128)S(1)} %get-tuple-element.13.order, s32[256,4,128]{2,1,0:T(4,128)S(1)} %bitcast.7, s32[256,4,128]{2,1,0:T(4,128)S(1)} %bitcast.8, f32[12288,128]{1,0:T(8,128)S(1)} %shard_map.66.table_in, ...), custom_call_target="tpu_custom_call", output_to_operand_aliasing={{1}: (3, {})} | custom-call | tf_op jit(solution)/shard_map/pallas_call | solution.py:483
  (2 shorter events, 0.0 us)
Async XLA Ops:
  0.0 9.8 %collective-permute-start.4 = (bf16[24,12288]{1,0:T(8,128)(2,1)}, bf16[24,12288]{1,0:T(8,128)(2,1)S(1)}, u32[]{:S(2)}, u32[]{:S(2)}) collective-permute-start(bf16[24,12288]{1,0:T(8,128)(2,1)} %vectors.1), channel_id=1, source_target_pairs={{0,8},{1,17},{2,10},{3,19},{4,12},{5,21},{6,14},{7,23},{8,0},{9,25... | collective-permute-start | bytes 1769480 | tf_op jit(solution)/shard_map/ppermute | solution.py:530
  9.8 24.8 %collective-permute-start.5 = (bf16[24,12288]{1,0:T(8,128)(2,1)S(1)}, bf16[24,12288]{1,0:T(8,128)(2,1)S(1)}, u32[]{:S(2)}, u32[]{:S(2)}) collective-permute-start(bf16[24,12288]{1,0:T(8,128)(2,1)S(1)} %collective-permute-done.4.refs_0_), channel_id=1, source_target_pairs={{0,1},{1,0},{2,3},{3,2},{4,5},{5,4},{6,7},{7,6},{8,9},{9,8},{10,11... | collective-permute-start | bytes 1769480 | tf_op jit(solution)/shard_map/ppermute | solution.py:523
  11.1 24.5 %collective-permute-start.8 = (bf16[24,12288]{1,0:T(8,128)(2,1)S(1)}, bf16[24,12288]{1,0:T(8,128)(2,1)S(1)}, u32[]{:S(2)}, u32[]{:S(2)}) collective-permute-start(bf16[24,12288]{1,0:T(8,128)(2,1)S(1)} %collective-permute-done.4.refs_0_), channel_id=1, source_target_pairs={{0,16},{1,9},{2,18},{3,11},{4,20},{5,13},{6,22},{7,15},{8,24},{9,1... | collective-permute-start | bytes 1769480 | tf_op jit(solution)/shard_map/ppermute | solution.py:530
  13.8 3.7 %collective-permute-start = (s16[128,128]{1,0:T(8,128)(2,1)S(1)}, s16[128,128]{1,0:T(8,128)(2,1)S(1)}, u32[]{:S(2)}, u32[]{:S(2)}) collective-permute-start(s16[128,128]{1,0:T(8,128)(2,1)S(1)} %bitcast.12), channel_id=1, source_target_pairs={{0,2},{1,3},{2,0},{3,1},{4,6},{5,7},{6,4},{7,5},{8,10},{9,11},{10,... | collective-permute-start | bytes 98312 | tf_op jit(solution)/shard_map/ppermute | solution.py:551
  15.1 4.0 %collective-permute-start.1 = (s16[128,128]{1,0:T(8,128)(2,1)S(1)}, s16[128,128]{1,0:T(8,128)(2,1)S(1)}, u32[]{:S(2)}, u32[]{:S(2)}) collective-permute-start(s16[128,128]{1,0:T(8,128)(2,1)S(1)} %bitcast.13), channel_id=1, source_target_pairs={{0,4},{1,5},{2,6},{3,7},{4,0},{5,1},{6,2},{7,3},{8,12},{9,13},{10,... | collective-permute-start | bytes 98312 | tf_op jit(solution)/shard_map/ppermute | solution.py:551
  17.4 4.6 %collective-permute-start.2 = (s16[128,128]{1,0:T(8,128)(2,1)S(1)}, s16[128,128]{1,0:T(8,128)(2,1)S(1)}, u32[]{:S(2)}, u32[]{:S(2)}) collective-permute-start(s16[128,128]{1,0:T(8,128)(2,1)S(1)} %bitcast.14), channel_id=1, source_target_pairs={{0,6},{1,7},{2,4},{3,5},{4,2},{5,3},{6,0},{7,1},{8,14},{9,15},{10,... | collective-permute-start | bytes 98312 | tf_op jit(solution)/shard_map/ppermute | solution.py:551
  22.0 11.4 %collective-permute-start.3 = (s16[512,128]{1,0:T(8,128)(2,1)S(1)}, s16[512,128]{1,0:T(8,128)(2,1)S(1)}, u32[]{:S(2)}, u32[]{:S(2)}) collective-permute-start(s16[512,128]{1,0:T(8,128)(2,1)S(1)} %pad_add_fusion.refs_0_), channel_id=1, source_target_pairs={{0,1},{1,0},{2,3},{3,2},{4,5},{5,4},{6,7},{7,6},{8,9},{9,8},{10,11... | collective-permute-start | bytes 393224 | tf_op jit(solution)/shard_map/ppermute | solution.py:523
  24.1 2.9 %collective-permute-start.6 = (bf16[96,128]{1,0:T(8,128)(2,1)}, bf16[96,128]{1,0:T(8,128)(2,1)S(1)}, u32[]{:S(2)}, u32[]{:S(2)}) collective-permute-start(bf16[96,128]{1,0:T(8,128)(2,1)} %bitcast.9), channel_id=1, source_target_pairs={{0,8},{1,17},{2,10},{3,19},{4,12},{5,21},{6,14},{7,23},{8,0},{9,25... | collective-permute-start | bytes 73736 | tf_op jit(solution)/shard_map/ppermute | solution.py:530
  27.0 7.6 %collective-permute-start.7 = (bf16[96,128]{1,0:T(8,128)(2,1)S(1)}, bf16[96,128]{1,0:T(8,128)(2,1)S(1)}, u32[]{:S(2)}, u32[]{:S(2)}) collective-permute-start(bf16[96,128]{1,0:T(8,128)(2,1)S(1)} %collective-permute-done.6.refs_2_), channel_id=1, source_target_pairs={{0,1},{1,0},{2,3},{3,2},{4,5},{5,4},{6,7},{7,6},{8,9},{9,8},{10,11... | collective-permute-start | bytes 73736 | tf_op jit(solution)/shard_map/ppermute | solution.py:523
  28.2 7.3 %collective-permute-start.9 = (bf16[96,128]{1,0:T(8,128)(2,1)}, bf16[96,128]{1,0:T(8,128)(2,1)S(1)}, u32[]{:S(2)}, u32[]{:S(2)}) collective-permute-start(bf16[96,128]{1,0:T(8,128)(2,1)} %bitcast.10), channel_id=1, source_target_pairs={{0,24},{1,25},{2,26},{3,27},{4,28},{5,29},{6,30},{7,31},{8,16},{9,... | collective-permute-start | bytes 73736 | tf_op jit(solution)/shard_map/ppermute | solution.py:530
  29.4 1.1 %copy-start = (bf16[24,12288]{1,0:T(8,128)(2,1)S(1)}, bf16[24,12288]{1,0:T(8,128)(2,1)}, u32[]{:S(2)}) copy-start(bf16[24,12288]{1,0:T(8,128)(2,1)} %vectors.1) | copy-start | bytes 1769476
  30.4 0.7 %copy-start.2 = (bf16[12288]{0:T(1024)(128)(2,1)S(1)}, bf16[12288]{0:T(1024)(128)(2,1)}, u32[]{:S(2)}) copy-start(bf16[12288]{0:T(1024)(128)(2,1)} %param.9) | copy-start | bytes 73732
  31.6 1.0 %copy-start.1 = (bf16[144,1152]{1,0:T(8,128)(2,1)S(1)}, bf16[144,1152]{1,0:T(8,128)(2,1)}, u32[]{:S(2)}) copy-start(bf16[144,1152]{1,0:T(8,128)(2,1)} %phi_in.1) | copy-start | bytes 995332
  32.6 0.7 %copy-start.3 = (s32[8,9]{1,0:T(8,128)S(1)}, s32[8,9]{1,0:T(8,128)}, u32[]{:S(2)}) copy-start(s32[8,9]{1,0:T(8,128)} %cells_in.1) | copy-start | bytes 868

commit v6 on v5

--- a/solution.py
+++ b/solution.py
@@ -198,6 +198,8 @@
     wide_b,
     product_a,
     product_b,
+    result_a,
+    result_b,
     placed,
     place,
     acc,
@@ -214,6 +216,7 @@
     count = order[0, last + 1]
     gathered, pair, single = (gathered_a, gathered_b), (pair_a, pair_b), (single_a, single_b)
     wide, product = (wide_a, wide_b), (product_a, product_b)
+    result = (result_a, result_b)
 
     def block_at(i):
         return order[0, jnp.clip(i, 0, last)]
@@ -341,14 +344,14 @@
                     ).astype(jnp.bfloat16)
                 yield
 
-    def finish(i, weighted, product_in):
+    def finish(i, result_in, product_in):
         sum_re = jnp.zeros((SUB, LANES), jnp.float32)
         sum_im = sum_re
         for v in range(groups):
             rows = slice(v * SUB, (v + 1) * SUB)
             nre = product_in[rows, :]
             nim = product_in[pairs + v * SUB : pairs + (v + 1) * SUB, :]
-            wre, wim = weighted[rows, :LANES], weighted[rows, LANES:]
+            wre, wim = result_in[rows, :LANES], result_in[rows, LANES:]
             sum_re = sum_re + (nre * wre - nim * wim)
             sum_im = sum_im + (nre * wim + nim * wre)
             yield
@@ -392,11 +395,14 @@
 
     pieces = [(at, min(at + DEPTH, clusters * pairs)) for at in range(0, clusters * pairs, DEPTH)]
 
-    def multiply(wide_in, held):
+    def multiply(wide_in, result_out):
+        whole = None
         for low, high in pieces:
             part = jnp.dot(phi[:, low:high], wide_in[low:high, :], preferred_element_type=jnp.float32)
-            held[:] = [part if not held else held[0] + part]
+            whole = part if whole is None else whole + part
             yield
+        result_out[...] = whole
+        yield
 
     def scatter():
         return lax.dot_general(
@@ -414,25 +420,31 @@
         load(i + 3, 1 - p).start()
         load(i + 2, p).wait()
         sums = scatter()
-        weighted = []
+        joined = join(single[1 - p], product[1 - p])
+        next(joined)
         chosen = choose(i + 1, gathered[1 - p], pair[1 - p], single[1 - p])
-        product_of = multiply(wide[1 - p], weighted)
+        multiplied = multiply(wide[1 - p], result[1 - p])
         turned = turn(pair[p], single[p], wide[p])
-        joined = join(single[p], product[p])
+        done = finish(i - 2, result[p], product[p])
         rows = gather(p)
-        run((product_of, len(pieces)), (turned, turn_steps), (rows, 240))
-        drain(product_of)
-        done = finish(i - 1, weighted[0], product[1 - p])
-        run((chosen, choose_steps), (joined, join_steps), (done, finish_steps), (rows, gather_steps - 240))
-        drain(chosen, turned, joined, rows, done)
+        run(
+            (multiplied, len(pieces) + 1),
+            (done, finish_steps),
+            (chosen, choose_steps),
+            (turned, turn_steps),
+            (joined, join_steps),
+            (rows, gather_steps),
+        )
+        drain(multiplied, done, chosen, turned, joined, rows)
         add(sums)
 
     def last_terms(p):
         sums = scatter()
-        weighted = []
-        drain(multiply(wide[1 - p], weighted))
-        drain(finish(count - 1, weighted[0], product[1 - p]))
+        drain(join(single[1 - p], product[1 - p]), multiply(wide[1 - p], result[1 - p]))
+        drain(finish(count - 2, result[p], product[p]))
         add(sums)
+        add(scatter())
+        drain(finish(count - 1, result[1 - p], product[1 - p]))
         add(scatter())
         load(0, p).wait()
 
@@ -495,6 +507,7 @@
             *[pltpu.VMEM((singles, LANES), jnp.float32)] * 2,
             *[pltpu.VMEM((phi.shape[1], 2 * LANES), jnp.bfloat16)] * 2,
             *[pltpu.VMEM((2 * pairs + SUB, LANES), jnp.float32)] * 2,
+            *[pltpu.VMEM((pairs, 2 * LANES), jnp.float32)] * 2,
             pltpu.VMEM((3 * padded, LANES), jnp.bfloat16),
             pltpu.VMEM((SUB, LANES), jnp.int32),
             pltpu.VMEM((padded, LANES), jnp.float32),

time: 48.1 us -> 48 us (level)
  transfers between devices with their start and end apart: 10 -> 10, of which waited for: 4 -> 4; matrix products, arithmetic and copies ran while one was open for 2% -> 2% of each run, Pallas kernels for 5% -> 6%
where the time goes in v6:
time: 48 us; the launch traced here: 47.6 us
  Pallas kernels  14.7 us (31%)
  waiting for transfers between devices  14.3 us (30%)
  starting transfers between devices  13.4 us (28%)
  local copies, waits for them, and re-layouts  3.46 us (7%)
  other arithmetic  0.95 us (2%)
  between operations  0.73 us (2%)
    pallas_call x1, Pallas kernels, rates_call(): pl.pallas_call(functools.partial(kernel, branches, base), out_shape=[jax....  12.1 us
    ppermute x4, waiting for transfers between devices, across(): return lax.ppermute(x, both, pairs)  9.76 us
    ppermute x4, starting transfers between devices, across(): return lax.ppermute(x, both, pairs)  5.21 us
    ppermute x3, waiting for transfers between devices, body(): lax.ppermute(coded, 'wa', [(i, i ^ k) for i in range(workers)])  4.56 us
    ppermute x3, starting transfers between devices, swap(): return lax.ppermute(x, 'wa', [(i, i ^ 1) for i in range(workers)])  4.54 us
    ppermute x3, starting transfers between devices, body(): lax.ppermute(coded, 'wa', [(i, i ^ k) for i in range(workers)])  3.67 us
    unnamed x8, local copies, waits for them, and re-layouts  3.46 us
    pallas_call x1, Pallas kernels, body(): pl.pallas_call(functools.partial(prepare, branches, local, kept, offset),...  1.21 us
  transfers between devices with their start and end apart: 10, of which 4 were waited for; matrix products, arithmetic and copies ran while one was open for 2% of the time, Pallas kernels for 6%

profile of v6, /device:TPU:1, one launch (start us, length us, event | category | flops | bytes accessed | tf_op | source)
XLA Modules:
  0.0 47.6 jit_solution(6868834953617139663)
XLA Ops:
  0.0 2.1 %collective-permute-start.4 = (bf16[24,12288]{1,0:T(8,128)(2,1)}, bf16[24,12288]{1,0:T(8,128)(2,1)S(1)}, u32[]{:S(2)}, u32[]{:S(2)}) collective-permute-start(bf16[24,12288]{1,0:T(8,128)(2,1)} %vectors.1), channel_id=1, source_target_pairs={{0,8},{1,17},{2,10},{3,19},{4,12},{5,21},{6,14},{7,23},{8,0},{9,25... | collective-permute-start | bytes 1769480 | tf_op jit(solution)/shard_map/ppermute | solution.py:543
  2.7 7.1 %collective-permute-done.4.refs_0_ = bf16[24,12288]{1,0:T(8,128)(2,1)S(1)} collective-permute-done((bf16[24,12288]{1,0:T(8,128)(2,1)}, bf16[24,12288]{1,0:T(8,128)(2,1)S(1)}, u32[]{:S(2)}, u32[]{:S(2)}) %collective-permute-start.4) | collective-permute-done | bytes 589856 | tf_op jit(solution)/shard_map/ppermute | solution.py:543
  9.8 1.2 %collective-permute-start.5 = (bf16[24,12288]{1,0:T(8,128)(2,1)S(1)}, bf16[24,12288]{1,0:T(8,128)(2,1)S(1)}, u32[]{:S(2)}, u32[]{:S(2)}) collective-permute-start(bf16[24,12288]{1,0:T(8,128)(2,1)S(1)} %collective-permute-done.4.refs_0_), channel_id=1, source_target_pairs={{0,1},{1,0},{2,3},{3,2},{4,5},{5,4},{6,7},{7,6},{8,9},{9,8},{10,11... | collective-permute-start | bytes 1769480 | tf_op jit(solution)/shard_map/ppermute | solution.py:536
  11.1 1.7 %collective-permute-start.8 = (bf16[24,12288]{1,0:T(8,128)(2,1)S(1)}, bf16[24,12288]{1,0:T(8,128)(2,1)S(1)}, u32[]{:S(2)}, u32[]{:S(2)}) collective-permute-start(bf16[24,12288]{1,0:T(8,128)(2,1)S(1)} %collective-permute-done.4.refs_0_), channel_id=1, source_target_pairs={{0,16},{1,9},{2,18},{3,11},{4,20},{5,13},{6,22},{7,15},{8,24},{9,1... | collective-permute-start | bytes 1769480 | tf_op jit(solution)/shard_map/ppermute | solution.py:543
  12.8 0.9 %add_convert_fusion = s16[32,4,128]{2,1,0:T(4,128)(2,1)S(1)} fusion(s32[32,4,128]{2,1,0:T(4,128)} %param.6, pred[32]{0:T(512)(128)(4,1)S(1)} %iota_compare_fusion), kind=kLoop, calls=%fused_computation.1 | loop fusion | flops 49152 | bytes 98336 | tf_op jit(solution)/shard_map/convert_element_type | solution.py:560
  13.8 1.4 %collective-permute-start = (s16[128,128]{1,0:T(8,128)(2,1)S(1)}, s16[128,128]{1,0:T(8,128)(2,1)S(1)}, u32[]{:S(2)}, u32[]{:S(2)}) collective-permute-start(s16[128,128]{1,0:T(8,128)(2,1)S(1)} %bitcast.12), channel_id=1, source_target_pairs={{0,2},{1,3},{2,0},{3,1},{4,6},{5,7},{6,4},{7,5},{8,10},{9,11},{10,... | collective-permute-start | bytes 98312 | tf_op jit(solution)/shard_map/ppermute | solution.py:564
  15.1 2.3 %collective-permute-start.1 = (s16[128,128]{1,0:T(8,128)(2,1)S(1)}, s16[128,128]{1,0:T(8,128)(2,1)S(1)}, u32[]{:S(2)}, u32[]{:S(2)}) collective-permute-start(s16[128,128]{1,0:T(8,128)(2,1)S(1)} %bitcast.13), channel_id=1, source_target_pairs={{0,4},{1,5},{2,6},{3,7},{4,0},{5,1},{6,2},{7,3},{8,12},{9,13},{10,... | collective-permute-start | bytes 98312 | tf_op jit(solution)/shard_map/ppermute | solution.py:564
  17.4 0.0 collective-permute-start.2
  17.4 0.0 collective-permute-done
  17.4 1.7 %collective-permute-done.1 = s16[128,128]{1,0:T(8,128)(2,1)S(1)} collective-permute-done((s16[128,128]{1,0:T(8,128)(2,1)S(1)}, s16[128,128]{1,0:T(8,128)(2,1)S(1)}, u32[]{:S(2)}, u32[]{:S(2)}) %collective-permute-start.1) | collective-permute-done | bytes 32800 | tf_op jit(solution)/shard_map/ppermute | solution.py:564
  19.1 2.9 %collective-permute-done.2 = s16[128,128]{1,0:T(8,128)(2,1)S(1)} collective-permute-done((s16[128,128]{1,0:T(8,128)(2,1)S(1)}, s16[128,128]{1,0:T(8,128)(2,1)S(1)}, u32[]{:S(2)}, u32[]{:S(2)}) %collective-permute-start.2) | collective-permute-done | bytes 32800 | tf_op jit(solution)/shard_map/ppermute | solution.py:564
  22.0 2.1 %collective-permute-start.3 = (s16[512,128]{1,0:T(8,128)(2,1)S(1)}, s16[512,128]{1,0:T(8,128)(2,1)S(1)}, u32[]{:S(2)}, u32[]{:S(2)}) collective-permute-start(s16[512,128]{1,0:T(8,128)(2,1)S(1)} %pad_add_fusion.refs_0_), channel_id=1, source_target_pairs={{0,1},{1,0},{2,3},{3,2},{4,5},{5,4},{6,7},{7,6},{8,9},{9,8},{10,11... | collective-permute-start | bytes 393224 | tf_op jit(solution)/shard_map/ppermute | solution.py:536
  24.1 0.3 collective-permute-start.6
  24.3 2.6 %collective-permute-done.6.refs_2_ = bf16[96,128]{1,0:T(8,128)(2,1)S(1)} collective-permute-done((bf16[96,128]{1,0:T(8,128)(2,1)}, bf16[96,128]{1,0:T(8,128)(2,1)S(1)}, u32[]{:S(2)}, u32[]{:S(2)}) %collective-permute-start.6) | collective-permute-done | bytes 24608 | tf_op jit(solution)/shard_map/ppermute | solution.py:543
  27.0 1.2 %collective-permute-start.7 = (bf16[96,128]{1,0:T(8,128)(2,1)S(1)}, bf16[96,128]{1,0:T(8,128)(2,1)S(1)}, u32[]{:S(2)}, u32[]{:S(2)}) collective-permute-start(bf16[96,128]{1,0:T(8,128)(2,1)S(1)} %collective-permute-done.6.refs_2_), channel_id=1, source_target_pairs={{0,1},{1,0},{2,3},{3,2},{4,5},{5,4},{6,7},{7,6},{8,9},{9,8},{10,11... | collective-permute-start | bytes 73736 | tf_op jit(solution)/shard_map/ppermute | solution.py:536
  28.2 1.2 %collective-permute-start.9 = (bf16[96,128]{1,0:T(8,128)(2,1)}, bf16[96,128]{1,0:T(8,128)(2,1)S(1)}, u32[]{:S(2)}, u32[]{:S(2)}) collective-permute-start(bf16[96,128]{1,0:T(8,128)(2,1)} %bitcast.10), channel_id=1, source_target_pairs={{0,24},{1,25},{2,26},{3,27},{4,28},{5,29},{6,30},{7,31},{8,16},{9,... | collective-permute-start | bytes 73736 | tf_op jit(solution)/shard_map/ppermute | solution.py:543
  29.4 0.0 copy-start
  29.4 1.1 %copy-done = bf16[24,12288]{1,0:T(8,128)(2,1)S(1)} copy-done((bf16[24,12288]{1,0:T(8,128)(2,1)S(1)}, bf16[24,12288]{1,0:T(8,128)(2,1)}, u32[]{:S(2)}) %copy-start) | copy-done | bytes 589848
  30.4 0.0 copy-start.2
  30.4 0.7 %copy-done.2 = bf16[12288]{0:T(1024)(128)(2,1)S(1)} copy-done((bf16[12288]{0:T(1024)(128)(2,1)S(1)}, bf16[12288]{0:T(1024)(128)(2,1)}, u32[]{:S(2)}) %copy-start.2) | copy-done | bytes 24600
  31.2 0.5 shard_map.65
  31.6 0.0 copy-start.1
  31.6 1.0 %copy-done.1 = bf16[144,1152]{1,0:T(8,128)(2,1)S(1)} copy-done((bf16[144,1152]{1,0:T(8,128)(2,1)S(1)}, bf16[144,1152]{1,0:T(8,128)(2,1)}, u32[]{:S(2)}) %copy-start.1) | copy-done | bytes 331800
  32.6 0.0 copy-start.3
  32.6 0.7 %copy-done.3 = s32[8,9]{1,0:T(8,128)S(1)} copy-done((s32[8,9]{1,0:T(8,128)S(1)}, s32[8,9]{1,0:T(8,128)}, u32[]{:S(2)}) %copy-start.3) | copy-done | bytes 312
  33.3 0.1 shard_map.67
  33.4 0.0 collective-permute-done.3.refs_1_
  33.4 1.2 %shard_map.64 = (s32[1024,128]{1,0:T(8,128)S(1)}, s32[1024,128]{1,0:T(8,128)S(1)}, s32[1,384]{1,0:T(1,128)S(1)}) custom-call(s16[512,128]{1,0:T(8,128)(2,1)S(1)} %pad_add_fusion.refs_0_, s16[512,128]{1,0:T(8,128)(2,1)S(1)} %collective-permute-done.3.refs_1_), custom_call_target="tpu_custom_call" | custom-call | tf_op jit(solution)/shard_map/pallas_call | solution.py:572
  34.6 0.0 collective-permute-done.7.refs_3_
  34.6 0.0 collective-permute-done.5.refs_1_
  34.6 0.9 %shard_map.66.table_in = f32[12288,128]{1,0:T(8,128)S(1)} custom-call(f32[12288,128]{1,0:T(8,128)S(1)} %get-tuple-element.16.table_in, bf16[24,12288]{1,0:T(8,128)(2,1)S(1)} %collective-permute-done.4.refs_0_, bf16[24,12288]{1,0:T(8,128)(2,1)S(1)} %collective-permute-done.5.refs_1_, ...), custom_call_target="tpu_custom_call", output_to_operand_aliasing={{}: (0, {})} | custom-call | tf_op jit(solution)/shard_map/pallas_call | solution.py:608
  35.5 0.0 collective-permute-done.9.lines
  35.5 0.0 collective-permute-done.8.vectors
  35.5 12.1 %shard_map.68 = (f32[12,128]{1,0:T(8,128)}, f32[12288,128]{1,0:T(8,128)S(1)}) custom-call(s32[1,384]{1,0:T(1,128)S(1)} %get-tuple-element.13.order, s32[256,4,128]{2,1,0:T(4,128)S(1)} %bitcast.7, s32[256,4,128]{2,1,0:T(4,128)S(1)} %bitcast.8, f32[12288,128]{1,0:T(8,128)S(1)} %shard_map.66.table_in, ...), custom_call_target="tpu_custom_call", output_to_operand_aliasing={{1}: (3, {})} | custom-call | tf_op jit(solution)/shard_map/pallas_call | solution.py:495
  (2 shorter events, 0.0 us)
Async XLA Ops:
  0.0 9.8 %collective-permute-start.4 = (bf16[24,12288]{1,0:T(8,128)(2,1)}, bf16[24,12288]{1,0:T(8,128)(2,1)S(1)}, u32[]{:S(2)}, u32[]{:S(2)}) collective-permute-start(bf16[24,12288]{1,0:T(8,128)(2,1)} %vectors.1), channel_id=1, source_target_pairs={{0,8},{1,17},{2,10},{3,19},{4,12},{5,21},{6,14},{7,23},{8,0},{9,25... | collective-permute-start | bytes 1769480 | tf_op jit(solution)/shard_map/ppermute | solution.py:543
  9.8 24.8 %collective-permute-start.5 = (bf16[24,12288]{1,0:T(8,128)(2,1)S(1)}, bf16[24,12288]{1,0:T(8,128)(2,1)S(1)}, u32[]{:S(2)}, u32[]{:S(2)}) collective-permute-start(bf16[24,12288]{1,0:T(8,128)(2,1)S(1)} %collective-permute-done.4.refs_0_), channel_id=1, source_target_pairs={{0,1},{1,0},{2,3},{3,2},{4,5},{5,4},{6,7},{7,6},{8,9},{9,8},{10,11... | collective-permute-start | bytes 1769480 | tf_op jit(solution)/shard_map/ppermute | solution.py:536
  11.1 24.5 %collective-permute-start.8 = (bf16[24,12288]{1,0:T(8,128)(2,1)S(1)}, bf16[24,12288]{1,0:T(8,128)(2,1)S(1)}, u32[]{:S(2)}, u32[]{:S(2)}) collective-permute-start(bf16[24,12288]{1,0:T(8,128)(2,1)S(1)} %collective-permute-done.4.refs_0_), channel_id=1, source_target_pairs={{0,16},{1,9},{2,18},{3,11},{4,20},{5,13},{6,22},{7,15},{8,24},{9,1... | collective-permute-start | bytes 1769480 | tf_op jit(solution)/shard_map/ppermute | solution.py:543
  13.8 3.7 %collective-permute-start = (s16[128,128]{1,0:T(8,128)(2,1)S(1)}, s16[128,128]{1,0:T(8,128)(2,1)S(1)}, u32[]{:S(2)}, u32[]{:S(2)}) collective-permute-start(s16[128,128]{1,0:T(8,128)(2,1)S(1)} %bitcast.12), channel_id=1, source_target_pairs={{0,2},{1,3},{2,0},{3,1},{4,6},{5,7},{6,4},{7,5},{8,10},{9,11},{10,... | collective-permute-start | bytes 98312 | tf_op jit(solution)/shard_map/ppermute | solution.py:564
  15.1 4.0 %collective-permute-start.1 = (s16[128,128]{1,0:T(8,128)(2,1)S(1)}, s16[128,128]{1,0:T(8,128)(2,1)S(1)}, u32[]{:S(2)}, u32[]{:S(2)}) collective-permute-start(s16[128,128]{1,0:T(8,128)(2,1)S(1)} %bitcast.13), channel_id=1, source_target_pairs={{0,4},{1,5},{2,6},{3,7},{4,0},{5,1},{6,2},{7,3},{8,12},{9,13},{10,... | collective-permute-start | bytes 98312 | tf_op jit(solution)/shard_map/ppermute | solution.py:564
  17.4 4.6 %collective-permute-start.2 = (s16[128,128]{1,0:T(8,128)(2,1)S(1)}, s16[128,128]{1,0:T(8,128)(2,1)S(1)}, u32[]{:S(2)}, u32[]{:S(2)}) collective-permute-start(s16[128,128]{1,0:T(8,128)(2,1)S(1)} %bitcast.14), channel_id=1, source_target_pairs={{0,6},{1,7},{2,4},{3,5},{4,2},{5,3},{6,0},{7,1},{8,14},{9,15},{10,... | collective-permute-start | bytes 98312 | tf_op jit(solution)/shard_map/ppermute | solution.py:564
  22.0 11.4 %collective-permute-start.3 = (s16[512,128]{1,0:T(8,128)(2,1)S(1)}, s16[512,128]{1,0:T(8,128)(2,1)S(1)}, u32[]{:S(2)}, u32[]{:S(2)}) collective-permute-start(s16[512,128]{1,0:T(8,128)(2,1)S(1)} %pad_add_fusion.refs_0_), channel_id=1, source_target_pairs={{0,1},{1,0},{2,3},{3,2},{4,5},{5,4},{6,7},{7,6},{8,9},{9,8},{10,11... | collective-permute-start | bytes 393224 | tf_op jit(solution)/shard_map/ppermute | solution.py:536
  24.1 2.9 %collective-permute-start.6 = (bf16[96,128]{1,0:T(8,128)(2,1)}, bf16[96,128]{1,0:T(8,128)(2,1)S(1)}, u32[]{:S(2)}, u32[]{:S(2)}) collective-permute-start(bf16[96,128]{1,0:T(8,128)(2,1)} %bitcast.9), channel_id=1, source_target_pairs={{0,8},{1,17},{2,10},{3,19},{4,12},{5,21},{6,14},{7,23},{8,0},{9,25... | collective-permute-start | bytes 73736 | tf_op jit(solution)/shard_map/ppermute | solution.py:543
  27.0 7.6 %collective-permute-start.7 = (bf16[96,128]{1,0:T(8,128)(2,1)S(1)}, bf16[96,128]{1,0:T(8,128)(2,1)S(1)}, u32[]{:S(2)}, u32[]{:S(2)}) collective-permute-start(bf16[96,128]{1,0:T(8,128)(2,1)S(1)} %collective-permute-done.6.refs_2_), channel_id=1, source_target_pairs={{0,1},{1,0},{2,3},{3,2},{4,5},{5,4},{6,7},{7,6},{8,9},{9,8},{10,11... | collective-permute-start | bytes 73736 | tf_op jit(solution)/shard_map/ppermute | solution.py:536
  28.2 7.3 %collective-permute-start.9 = (bf16[96,128]{1,0:T(8,128)(2,1)}, bf16[96,128]{1,0:T(8,128)(2,1)S(1)}, u32[]{:S(2)}, u32[]{:S(2)}) collective-permute-start(bf16[96,128]{1,0:T(8,128)(2,1)} %bitcast.10), channel_id=1, source_target_pairs={{0,24},{1,25},{2,26},{3,27},{4,28},{5,29},{6,30},{7,31},{8,16},{9,... | collective-permute-start | bytes 73736 | tf_op jit(solution)/shard_map/ppermute | solution.py:543
  29.4 1.1 %copy-start = (bf16[24,12288]{1,0:T(8,128)(2,1)S(1)}, bf16[24,12288]{1,0:T(8,128)(2,1)}, u32[]{:S(2)}) copy-start(bf16[24,12288]{1,0:T(8,128)(2,1)} %vectors.1) | copy-start | bytes 1769476
  30.4 0.7 %copy-start.2 = (bf16[12288]{0:T(1024)(128)(2,1)S(1)}, bf16[12288]{0:T(1024)(128)(2,1)}, u32[]{:S(2)}) copy-start(bf16[12288]{0:T(1024)(128)(2,1)} %param.9) | copy-start | bytes 73732
  31.6 1.0 %copy-start.1 = (bf16[144,1152]{1,0:T(8,128)(2,1)S(1)}, bf16[144,1152]{1,0:T(8,128)(2,1)}, u32[]{:S(2)}) copy-start(bf16[144,1152]{1,0:T(8,128)(2,1)} %phi_in.1) | copy-start | bytes 995332
  32.6 0.7 %copy-start.3 = (s32[8,9]{1,0:T(8,128)S(1)}, s32[8,9]{1,0:T(8,128)}, u32[]{:S(2)}) copy-start(s32[8,9]{1,0:T(8,128)} %cells_in.1) | copy-start | bytes 868

commit v7 on v6

--- a/solution.py
+++ b/solution.py
@@ -15,7 +15,7 @@
 GROUPS = 4
 SLOT = LANES // GROUPS
 PARTS = 4
-AHEAD = 2
+AHEAD = 4
 DEPTH = 256
 
 smearing = 0.5
@@ -221,15 +221,15 @@
     def block_at(i):
         return order[0, jnp.clip(i, 0, last)]
 
-    def load(i, p):
-        return pltpu.make_async_copy(rows_any.at[block_at(i)], spots.at[p], sems.at[p])
-
-    def gather(p):
-        into = gathered[p]
+    def load(i, slot):
+        return pltpu.make_async_copy(rows_any.at[block_at(i)], spots.at[slot], sems.at[slot])
+
+    def gather(slot):
+        into = gathered[slot % 2]
         for which in range(3):
             for n in range(LANES):
                 at = which * LANES + n
-                into[at : at + 1, :] = table[pl.ds(spots[p, which + 1, n], 1), :]
+                into[at : at + 1, :] = table[pl.ds(spots[slot, which + 1, n], 1), :]
                 yield
 
     def one_hot(local):
@@ -416,9 +416,10 @@
         size = acc.shape[0]
         acc[...] += sums[:size] + sums[size : 2 * size] + sums[2 * size :]
 
-    def step(i, p):
-        load(i + 3, 1 - p).start()
-        load(i + 2, p).wait()
+    def step(i, turn_of):
+        p = turn_of % 2
+        load(i + AHEAD + 1, (turn_of + 1) % AHEAD).start()
+        load(i + 2, (turn_of + 2) % AHEAD).wait()
         sums = scatter()
         joined = join(single[1 - p], product[1 - p])
         next(joined)
@@ -426,7 +427,7 @@
         multiplied = multiply(wide[1 - p], result[1 - p])
         turned = turn(pair[p], single[p], wide[p])
         done = finish(i - 2, result[p], product[p])
-        rows = gather(p)
+        rows = gather((turn_of + 2) % AHEAD)
         run(
             (multiplied, len(pieces) + 1),
             (done, finish_steps),
@@ -446,32 +447,34 @@
         add(scatter())
         drain(finish(count - 1, result[1 - p], product[1 - p]))
         add(scatter())
-        load(0, p).wait()
-
-    load(0, 0).start()
-    load(1, 1).start()
+
+    for i in range(AHEAD):
+        load(i, i).start()
     acc[...] = jnp.zeros_like(acc)
     placed[...] = jnp.zeros_like(placed)
     place[...] = jnp.zeros_like(place)
     fill_table(shard_quarters(vectors, lines), table, base)
     load(0, 0).wait()
     drain(gather(0))
-    load(2, 0).start()
+    load(AHEAD, 0).start()
     load(1, 1).wait()
     first, second = choose(0, gathered_a, pair_a, single_a), gather(1)
     run((first, choose_steps), (second, gather_steps))
     drain(first, second)
 
-    def two_steps(j, carry):
-        step(2 * j, 0)
-
-        @pl.when(2 * j + 1 < count)
-        def _():
-            step(2 * j + 1, 1)
+    def one_round(j, carry):
+        step(AHEAD * j, 0)
+        for turn_of in range(1, AHEAD):
+
+            @pl.when(AHEAD * j + turn_of < count)
+            def _():
+                step(AHEAD * j + turn_of, turn_of)
 
         return carry
 
-    lax.fori_loop(0, lax.div(count + 1, 2), two_steps, 0)
+    lax.fori_loop(0, lax.div(count + AHEAD - 1, AHEAD), one_round, 0)
+    for i in range(2, AHEAD + 1):
+        load(0, lax.rem(count + i, AHEAD)).wait()
     even = lax.rem(count, 2) == 0
 
     @pl.when(even)

time: 48 us -> 47.3 us (0.985)
  Pallas kernels: 14.7 us -> 14.1 us
    pallas_call x1, Pallas kernels: 12.1 us -> 11.5 us  [rates_call(): pl.pallas_call(functools.partial(kernel, branches, base), out_shape=[jax....]
where the time goes in v7:
time: 47.3 us; the launch traced here: 47 us
  waiting for transfers between devices  14.3 us (30%)
  Pallas kernels  14.1 us (30%)
  starting transfers between devices  13.4 us (28%)
  local copies, waits for them, and re-layouts  3.46 us (7%)
  other arithmetic  0.95 us (2%)
  between operations  0.73 us (2%)
    pallas_call x1, Pallas kernels, rates_call(): pl.pallas_call(functools.partial(kernel, branches, base), out_shape=[jax....  11.5 us
    ppermute x4, waiting for transfers between devices, across(): return lax.ppermute(x, both, pairs)  9.76 us
    ppermute x4, starting transfers between devices, across(): return lax.ppermute(x, both, pairs)  5.21 us
    ppermute x3, waiting for transfers between devices, body(): lax.ppermute(coded, 'wa', [(i, i ^ k) for i in range(workers)])  4.56 us
    ppermute x3, starting transfers between devices, swap(): return lax.ppermute(x, 'wa', [(i, i ^ 1) for i in range(workers)])  4.54 us
    ppermute x3, starting transfers between devices, body(): lax.ppermute(coded, 'wa', [(i, i ^ k) for i in range(workers)])  3.67 us
    unnamed x8, local copies, waits for them, and re-layouts  3.46 us
    pallas_call x1, Pallas kernels, body(): pl.pallas_call(functools.partial(prepare, branches, local, kept, offset),...  1.21 us
  transfers between devices with their start and end apart: 10, of which 4 were waited for; matrix products, arithmetic and copies ran while one was open for 2% of the time, Pallas kernels for 6%

profile of v7, /device:TPU:1, one launch (start us, length us, event | category | flops | bytes accessed | tf_op | source)
XLA Modules:
  0.0 47.0 jit_solution(5053090631545404464)
XLA Ops:
  0.0 2.1 %collective-permute-start.4 = (bf16[24,12288]{1,0:T(8,128)(2,1)}, bf16[24,12288]{1,0:T(8,128)(2,1)S(1)}, u32[]{:S(2)}, u32[]{:S(2)}) collective-permute-start(bf16[24,12288]{1,0:T(8,128)(2,1)} %vectors.1), channel_id=1, source_target_pairs={{0,8},{1,17},{2,10},{3,19},{4,12},{5,21},{6,14},{7,23},{8,0},{9,25... | collective-permute-start | bytes 1769480 | tf_op jit(solution)/shard_map/ppermute | solution.py:546
  2.7 7.1 %collective-permute-done.4.refs_0_ = bf16[24,12288]{1,0:T(8,128)(2,1)S(1)} collective-permute-done((bf16[24,12288]{1,0:T(8,128)(2,1)}, bf16[24,12288]{1,0:T(8,128)(2,1)S(1)}, u32[]{:S(2)}, u32[]{:S(2)}) %collective-permute-start.4) | collective-permute-done | bytes 589856 | tf_op jit(solution)/shard_map/ppermute | solution.py:546
  9.8 1.2 %collective-permute-start.5 = (bf16[24,12288]{1,0:T(8,128)(2,1)S(1)}, bf16[24,12288]{1,0:T(8,128)(2,1)S(1)}, u32[]{:S(2)}, u32[]{:S(2)}) collective-permute-start(bf16[24,12288]{1,0:T(8,128)(2,1)S(1)} %collective-permute-done.4.refs_0_), channel_id=1, source_target_pairs={{0,1},{1,0},{2,3},{3,2},{4,5},{5,4},{6,7},{7,6},{8,9},{9,8},{10,11... | collective-permute-start | bytes 1769480 | tf_op jit(solution)/shard_map/ppermute | solution.py:539
  11.1 1.7 %collective-permute-start.8 = (bf16[24,12288]{1,0:T(8,128)(2,1)S(1)}, bf16[24,12288]{1,0:T(8,128)(2,1)S(1)}, u32[]{:S(2)}, u32[]{:S(2)}) collective-permute-start(bf16[24,12288]{1,0:T(8,128)(2,1)S(1)} %collective-permute-done.4.refs_0_), channel_id=1, source_target_pairs={{0,16},{1,9},{2,18},{3,11},{4,20},{5,13},{6,22},{7,15},{8,24},{9,1... | collective-permute-start | bytes 1769480 | tf_op jit(solution)/shard_map/ppermute | solution.py:546
  12.8 0.9 %add_convert_fusion = s16[32,4,128]{2,1,0:T(4,128)(2,1)S(1)} fusion(s32[32,4,128]{2,1,0:T(4,128)} %param.6, pred[32]{0:T(512)(128)(4,1)S(1)} %iota_compare_fusion), kind=kLoop, calls=%fused_computation.1 | loop fusion | flops 49152 | bytes 98336 | tf_op jit(solution)/shard_map/convert_element_type | solution.py:563
  13.8 1.4 %collective-permute-start = (s16[128,128]{1,0:T(8,128)(2,1)S(1)}, s16[128,128]{1,0:T(8,128)(2,1)S(1)}, u32[]{:S(2)}, u32[]{:S(2)}) collective-permute-start(s16[128,128]{1,0:T(8,128)(2,1)S(1)} %bitcast.12), channel_id=1, source_target_pairs={{0,2},{1,3},{2,0},{3,1},{4,6},{5,7},{6,4},{7,5},{8,10},{9,11},{10,... | collective-permute-start | bytes 98312 | tf_op jit(solution)/shard_map/ppermute | solution.py:567
  15.1 2.3 %collective-permute-start.1 = (s16[128,128]{1,0:T(8,128)(2,1)S(1)}, s16[128,128]{1,0:T(8,128)(2,1)S(1)}, u32[]{:S(2)}, u32[]{:S(2)}) collective-permute-start(s16[128,128]{1,0:T(8,128)(2,1)S(1)} %bitcast.13), channel_id=1, source_target_pairs={{0,4},{1,5},{2,6},{3,7},{4,0},{5,1},{6,2},{7,3},{8,12},{9,13},{10,... | collective-permute-start | bytes 98312 | tf_op jit(solution)/shard_map/ppermute | solution.py:567
  17.4 0.0 collective-permute-start.2
  17.4 0.0 collective-permute-done
  17.4 1.7 %collective-permute-done.1 = s16[128,128]{1,0:T(8,128)(2,1)S(1)} collective-permute-done((s16[128,128]{1,0:T(8,128)(2,1)S(1)}, s16[128,128]{1,0:T(8,128)(2,1)S(1)}, u32[]{:S(2)}, u32[]{:S(2)}) %collective-permute-start.1) | collective-permute-done | bytes 32800 | tf_op jit(solution)/shard_map/ppermute | solution.py:567
  19.1 2.9 %collective-permute-done.2 = s16[128,128]{1,0:T(8,128)(2,1)S(1)} collective-permute-done((s16[128,128]{1,0:T(8,128)(2,1)S(1)}, s16[128,128]{1,0:T(8,128)(2,1)S(1)}, u32[]{:S(2)}, u32[]{:S(2)}) %collective-permute-start.2) | collective-permute-done | bytes 32800 | tf_op jit(solution)/shard_map/ppermute | solution.py:567
  22.0 2.1 %collective-permute-start.3 = (s16[512,128]{1,0:T(8,128)(2,1)S(1)}, s16[512,128]{1,0:T(8,128)(2,1)S(1)}, u32[]{:S(2)}, u32[]{:S(2)}) collective-permute-start(s16[512,128]{1,0:T(8,128)(2,1)S(1)} %pad_add_fusion.refs_0_), channel_id=1, source_target_pairs={{0,1},{1,0},{2,3},{3,2},{4,5},{5,4},{6,7},{7,6},{8,9},{9,8},{10,11... | collective-permute-start | bytes 393224 | tf_op jit(solution)/shard_map/ppermute | solution.py:539
  24.1 0.3 collective-permute-start.6
  24.3 2.6 %collective-permute-done.6.refs_2_ = bf16[96,128]{1,0:T(8,128)(2,1)S(1)} collective-permute-done((bf16[96,128]{1,0:T(8,128)(2,1)}, bf16[96,128]{1,0:T(8,128)(2,1)S(1)}, u32[]{:S(2)}, u32[]{:S(2)}) %collective-permute-start.6) | collective-permute-done | bytes 24608 | tf_op jit(solution)/shard_map/ppermute | solution.py:546
  27.0 1.2 %collective-permute-start.7 = (bf16[96,128]{1,0:T(8,128)(2,1)S(1)}, bf16[96,128]{1,0:T(8,128)(2,1)S(1)}, u32[]{:S(2)}, u32[]{:S(2)}) collective-permute-start(bf16[96,128]{1,0:T(8,128)(2,1)S(1)} %collective-permute-done.6.refs_2_), channel_id=1, source_target_pairs={{0,1},{1,0},{2,3},{3,2},{4,5},{5,4},{6,7},{7,6},{8,9},{9,8},{10,11... | collective-permute-start | bytes 73736 | tf_op jit(solution)/shard_map/ppermute | solution.py:539
  28.2 1.2 %collective-permute-start.9 = (bf16[96,128]{1,0:T(8,128)(2,1)}, bf16[96,128]{1,0:T(8,128)(2,1)S(1)}, u32[]{:S(2)}, u32[]{:S(2)}) collective-permute-start(bf16[96,128]{1,0:T(8,128)(2,1)} %bitcast.10), channel_id=1, source_target_pairs={{0,24},{1,25},{2,26},{3,27},{4,28},{5,29},{6,30},{7,31},{8,16},{9,... | collective-permute-start | bytes 73736 | tf_op jit(solution)/shard_map/ppermute | solution.py:546
  29.4 0.0 copy-start
  29.4 1.1 %copy-done = bf16[24,12288]{1,0:T(8,128)(2,1)S(1)} copy-done((bf16[24,12288]{1,0:T(8,128)(2,1)S(1)}, bf16[24,12288]{1,0:T(8,128)(2,1)}, u32[]{:S(2)}) %copy-start) | copy-done | bytes 589848
  30.4 0.0 copy-start.2
  30.4 0.7 %copy-done.2 = bf16[12288]{0:T(1024)(128)(2,1)S(1)} copy-done((bf16[12288]{0:T(1024)(128)(2,1)S(1)}, bf16[12288]{0:T(1024)(128)(2,1)}, u32[]{:S(2)}) %copy-start.2) | copy-done | bytes 24600
  31.2 0.5 shard_map.65
  31.6 0.0 copy-start.1
  31.6 1.0 %copy-done.1 = bf16[144,1152]{1,0:T(8,128)(2,1)S(1)} copy-done((bf16[144,1152]{1,0:T(8,128)(2,1)S(1)}, bf16[144,1152]{1,0:T(8,128)(2,1)}, u32[]{:S(2)}) %copy-start.1) | copy-done | bytes 331800
  32.6 0.0 copy-start.3
  32.6 0.7 %copy-done.3 = s32[8,9]{1,0:T(8,128)S(1)} copy-done((s32[8,9]{1,0:T(8,128)S(1)}, s32[8,9]{1,0:T(8,128)}, u32[]{:S(2)}) %copy-start.3) | copy-done | bytes 312
  33.3 0.1 shard_map.67
  33.4 0.0 collective-permute-done.3.refs_1_
  33.4 1.2 %shard_map.64 = (s32[1024,128]{1,0:T(8,128)S(1)}, s32[1024,128]{1,0:T(8,128)S(1)}, s32[1,384]{1,0:T(1,128)S(1)}) custom-call(s16[512,128]{1,0:T(8,128)(2,1)S(1)} %pad_add_fusion.refs_0_, s16[512,128]{1,0:T(8,128)(2,1)S(1)} %collective-permute-done.3.refs_1_), custom_call_target="tpu_custom_call" | custom-call | tf_op jit(solution)/shard_map/pallas_call | solution.py:575
  34.6 0.0 collective-permute-done.7.refs_3_
  34.6 0.0 collective-permute-done.5.refs_1_
  34.6 0.9 %shard_map.66.table_in = f32[12288,128]{1,0:T(8,128)S(1)} custom-call(f32[12288,128]{1,0:T(8,128)S(1)} %get-tuple-element.16.table_in, bf16[24,12288]{1,0:T(8,128)(2,1)S(1)} %collective-permute-done.4.refs_0_, bf16[24,12288]{1,0:T(8,128)(2,1)S(1)} %collective-permute-done.5.refs_1_, ...), custom_call_target="tpu_custom_call", output_to_operand_aliasing={{}: (0, {})} | custom-call | tf_op jit(solution)/shard_map/pallas_call | solution.py:611
  35.5 0.0 collective-permute-done.9.lines
  35.5 0.0 collective-permute-done.8.vectors
  35.5 11.5 %shard_map.68 = (f32[12,128]{1,0:T(8,128)}, f32[12288,128]{1,0:T(8,128)S(1)}) custom-call(s32[1,384]{1,0:T(1,128)S(1)} %get-tuple-element.13.order, s32[256,4,128]{2,1,0:T(4,128)S(1)} %bitcast.7, s32[256,4,128]{2,1,0:T(4,128)S(1)} %bitcast.8, f32[12288,128]{1,0:T(8,128)S(1)} %shard_map.66.table_in, ...), custom_call_target="tpu_custom_call", output_to_operand_aliasing={{1}: (3, {})} | custom-call | tf_op jit(solution)/shard_map/pallas_call | solution.py:498
  (2 shorter events, 0.0 us)
Async XLA Ops:
  0.0 9.8 %collective-permute-start.4 = (bf16[24,12288]{1,0:T(8,128)(2,1)}, bf16[24,12288]{1,0:T(8,128)(2,1)S(1)}, u32[]{:S(2)}, u32[]{:S(2)}) collective-permute-start(bf16[24,12288]{1,0:T(8,128)(2,1)} %vectors.1), channel_id=1, source_target_pairs={{0,8},{1,17},{2,10},{3,19},{4,12},{5,21},{6,14},{7,23},{8,0},{9,25... | collective-permute-start | bytes 1769480 | tf_op jit(solution)/shard_map/ppermute | solution.py:546
  9.8 24.8 %collective-permute-start.5 = (bf16[24,12288]{1,0:T(8,128)(2,1)S(1)}, bf16[24,12288]{1,0:T(8,128)(2,1)S(1)}, u32[]{:S(2)}, u32[]{:S(2)}) collective-permute-start(bf16[24,12288]{1,0:T(8,128)(2,1)S(1)} %collective-permute-done.4.refs_0_), channel_id=1, source_target_pairs={{0,1},{1,0},{2,3},{3,2},{4,5},{5,4},{6,7},{7,6},{8,9},{9,8},{10,11... | collective-permute-start | bytes 1769480 | tf_op jit(solution)/shard_map/ppermute | solution.py:539
  11.1 24.5 %collective-permute-start.8 = (bf16[24,12288]{1,0:T(8,128)(2,1)S(1)}, bf16[24,12288]{1,0:T(8,128)(2,1)S(1)}, u32[]{:S(2)}, u32[]{:S(2)}) collective-permute-start(bf16[24,12288]{1,0:T(8,128)(2,1)S(1)} %collective-permute-done.4.refs_0_), channel_id=1, source_target_pairs={{0,16},{1,9},{2,18},{3,11},{4,20},{5,13},{6,22},{7,15},{8,24},{9,1... | collective-permute-start | bytes 1769480 | tf_op jit(solution)/shard_map/ppermute | solution.py:546
  13.8 3.7 %collective-permute-start = (s16[128,128]{1,0:T(8,128)(2,1)S(1)}, s16[128,128]{1,0:T(8,128)(2,1)S(1)}, u32[]{:S(2)}, u32[]{:S(2)}) collective-permute-start(s16[128,128]{1,0:T(8,128)(2,1)S(1)} %bitcast.12), channel_id=1, source_target_pairs={{0,2},{1,3},{2,0},{3,1},{4,6},{5,7},{6,4},{7,5},{8,10},{9,11},{10,... | collective-permute-start | bytes 98312 | tf_op jit(solution)/shard_map/ppermute | solution.py:567
  15.1 4.0 %collective-permute-start.1 = (s16[128,128]{1,0:T(8,128)(2,1)S(1)}, s16[128,128]{1,0:T(8,128)(2,1)S(1)}, u32[]{:S(2)}, u32[]{:S(2)}) collective-permute-start(s16[128,128]{1,0:T(8,128)(2,1)S(1)} %bitcast.13), channel_id=1, source_target_pairs={{0,4},{1,5},{2,6},{3,7},{4,0},{5,1},{6,2},{7,3},{8,12},{9,13},{10,... | collective-permute-start | bytes 98312 | tf_op jit(solution)/shard_map/ppermute | solution.py:567
  17.4 4.6 %collective-permute-start.2 = (s16[128,128]{1,0:T(8,128)(2,1)S(1)}, s16[128,128]{1,0:T(8,128)(2,1)S(1)}, u32[]{:S(2)}, u32[]{:S(2)}) collective-permute-start(s16[128,128]{1,0:T(8,128)(2,1)S(1)} %bitcast.14), channel_id=1, source_target_pairs={{0,6},{1,7},{2,4},{3,5},{4,2},{5,3},{6,0},{7,1},{8,14},{9,15},{10,... | collective-permute-start | bytes 98312 | tf_op jit(solution)/shard_map/ppermute | solution.py:567
  22.0 11.4 %collective-permute-start.3 = (s16[512,128]{1,0:T(8,128)(2,1)S(1)}, s16[512,128]{1,0:T(8,128)(2,1)S(1)}, u32[]{:S(2)}, u32[]{:S(2)}) collective-permute-start(s16[512,128]{1,0:T(8,128)(2,1)S(1)} %pad_add_fusion.refs_0_), channel_id=1, source_target_pairs={{0,1},{1,0},{2,3},{3,2},{4,5},{5,4},{6,7},{7,6},{8,9},{9,8},{10,11... | collective-permute-start | bytes 393224 | tf_op jit(solution)/shard_map/ppermute | solution.py:539
  24.1 2.9 %collective-permute-start.6 = (bf16[96,128]{1,0:T(8,128)(2,1)}, bf16[96,128]{1,0:T(8,128)(2,1)S(1)}, u32[]{:S(2)}, u32[]{:S(2)}) collective-permute-start(bf16[96,128]{1,0:T(8,128)(2,1)} %bitcast.9), channel_id=1, source_target_pairs={{0,8},{1,17},{2,10},{3,19},{4,12},{5,21},{6,14},{7,23},{8,0},{9,25... | collective-permute-start | bytes 73736 | tf_op jit(solution)/shard_map/ppermute | solution.py:546
  27.0 7.6 %collective-permute-start.7 = (bf16[96,128]{1,0:T(8,128)(2,1)S(1)}, bf16[96,128]{1,0:T(8,128)(2,1)S(1)}, u32[]{:S(2)}, u32[]{:S(2)}) collective-permute-start(bf16[96,128]{1,0:T(8,128)(2,1)S(1)} %collective-permute-done.6.refs_2_), channel_id=1, source_target_pairs={{0,1},{1,0},{2,3},{3,2},{4,5},{5,4},{6,7},{7,6},{8,9},{9,8},{10,11... | collective-permute-start | bytes 73736 | tf_op jit(solution)/shard_map/ppermute | solution.py:539
  28.2 7.3 %collective-permute-start.9 = (bf16[96,128]{1,0:T(8,128)(2,1)}, bf16[96,128]{1,0:T(8,128)(2,1)S(1)}, u32[]{:S(2)}, u32[]{:S(2)}) collective-permute-start(bf16[96,128]{1,0:T(8,128)(2,1)} %bitcast.10), channel_id=1, source_target_pairs={{0,24},{1,25},{2,26},{3,27},{4,28},{5,29},{6,30},{7,31},{8,16},{9,... | collective-permute-start | bytes 73736 | tf_op jit(solution)/shard_map/ppermute | solution.py:546
  29.4 1.1 %copy-start = (bf16[24,12288]{1,0:T(8,128)(2,1)S(1)}, bf16[24,12288]{1,0:T(8,128)(2,1)}, u32[]{:S(2)}) copy-start(bf16[24,12288]{1,0:T(8,128)(2,1)} %vectors.1) | copy-start | bytes 1769476
  30.4 0.7 %copy-start.2 = (bf16[12288]{0:T(1024)(128)(2,1)S(1)}, bf16[12288]{0:T(1024)(128)(2,1)}, u32[]{:S(2)}) copy-start(bf16[12288]{0:T(1024)(128)(2,1)} %param.9) | copy-start | bytes 73732
  31.6 1.0 %copy-start.1 = (bf16[144,1152]{1,0:T(8,128)(2,1)S(1)}, bf16[144,1152]{1,0:T(8,128)(2,1)}, u32[]{:S(2)}) copy-start(bf16[144,1152]{1,0:T(8,128)(2,1)} %phi_in.1) | copy-start | bytes 995332
  32.6 0.7 %copy-start.3 = (s32[8,9]{1,0:T(8,128)S(1)}, s32[8,9]{1,0:T(8,128)}, u32[]{:S(2)}) copy-start(s32[8,9]{1,0:T(8,128)} %cells_in.1) | copy-start | bytes 868
